TPU v7x, 128 devices: a whole 4x4x4 slice. The times are simulated.
128 devices in a mesh: lat: 8 (over x, core), lon: 16 (over y, z).
Axes of the slice: x: 4, y: 4, z: 4, core: 2. Of those that a mesh axis runs over, the one named last changes fastest.
Arguments:
- spectra: bfloat16 [393216, 616], P(('lat', 'lon')), may hold values from -6 to 6
- block_target: int32 [3072], P(('lat', 'lon')), may hold values from 0 to 15, as said below
- block_patch: int32 [3072], P(('lat', 'lon')), may hold values from 0 to 11
- block_kernel: int32 [3072], P(('lat', 'lon')), may hold values from 0 to 15
- encoder_weight: bfloat16 [616, 512], replicated, may hold values from -0.25 to 0.25
- kernels: bfloat16 [16, 128, 128], replicated, may hold values from 0.049804688 to 1
- gain: float32 [512], replicated, may hold values from 0.1 to 1.9
- conv_weight: bfloat16 [3, 3, 512, 512], replicated, may hold values from -0.09375 to 0.09375
- cotangent: bfloat16 [192, 1024, 512], P('lat', 'lon'), may hold values from -6 to 6
Outputs:
- conv_out: bfloat16 [192, 1024, 512], P('lat', 'lon')
- conv_grad: float32 [3, 3, 512, 512], replicated
- encoder_grad: float32 [616, 512], replicated
- gain_grad: float32 [512], replicated
Inputs may be any that keep to these rules, and one draw needn't show every extreme that they name: `block_target`: within one device's 24 blocks no tile is named more than 3 times; in every latitude band one tile is named exactly 3 times by every device of the band.
All inputs are finite; a program needn't handle non-finite values.
Results may differ from a plain program's by a relative error of at most 0.0059.
Values may be sent and summed in bfloat16 or wider, within the bound.
A program may use at most 192 MiB of HBM per device.

v0:
```python
import math

import jax
import jax.numpy as jnp
from jax import lax
from jax.sharding import PartitionSpec as P

PH = 8
PW = 16
MOST = 3


def padded_2(shard, sides, width, wrap):
    for axis, dim in sides:
        size, length = (lax.axis_size(axis), shard.shape[dim])
        up = [(i, (i + 1) % size) for i in range(size if wrap else size - 1)]
        down = [(j, i) for i, j in up]
        last = lax.slice_in_dim(shard, length - width, length, axis=dim)
        leading = lax.slice_in_dim(shard, 0, width, axis=dim)
        before = lax.ppermute(last, axis, up)
        after = lax.ppermute(leading, axis, down)
        shard = jnp.concatenate([before, shard, after], axis=dim)
    return shard


def gather_turned(arrays, axis, dims):
    turned = [jnp.moveaxis(a, dim, 0) for a, dim in zip(arrays, dims)]
    both = jnp.concatenate([t.reshape(len(t), -1) for t in turned], axis=1)
    result, at, finished = (lax.all_gather(both, axis, axis=0, tiled=True), 0, [])
    for t, dim in zip(turned, dims):
        piece = result[:, at : at + t[0].size].reshape(-1, *t.shape[1:])
        finished.append(jnp.moveaxis(piece, 0, dim))
        at += t[0].size
    return tuple(finished)


def normalise(field, gain):
    meansq = jnp.mean(field * field, axis=-1, keepdims=True)
    return field * lax.rsqrt(meansq + 1e-06) * gain


def silu_slope(preact):
    logistic = jax.nn.sigmoid(preact)
    return logistic * (1.0 + preact * (1.0 - logistic))


def widen(field):
    beside_all = padded_2(field, (("lon", 1),), 1, True)
    return padded_2(beside_all, (("lat", 0),), 1, False)


def slot_layout(targets, lon_count):
    lanes = jnp.arange(lon_count, dtype=jnp.int32)
    onehot = (targets[..., None] == lanes).astype(jnp.int32)
    before = jnp.cumsum(onehot, axis=-2) - onehot
    ranks = jnp.sum(before * onehot, axis=-1)
    return targets * MOST + ranks


def to_tile(patches_in, tile_rows, tile_cols, width):
    shaped = patches_in.reshape(tile_rows // PH, tile_cols // PW, PH, PW, width)
    return shaped.transpose(0, 2, 1, 3, 4).reshape(tile_rows, tile_cols, width)


def to_patches(tile, tile_rows, tile_cols, width):
    shaped = tile.reshape(tile_rows // PH, PH, tile_cols // PW, PW, width)
    return shaped.transpose(0, 2, 1, 3, 4).reshape(-1, PH * PW, width)


def shards(
    spectra,
    block_target,
    block_patch,
    block_kernel,
    encoder_weight,
    kernels,
    gain,
    conv_weight,
    cotangent,
):
    lon_count = lax.axis_size("lon")
    lat_count = lax.axis_size("lat")
    own_lon = lax.axis_index("lon")
    blocks = block_target.shape[0]
    kernel_count, block_rows, patch_cells = kernels.shape
    channels = spectra.shape[1]
    width = encoder_weight.shape[1]
    tile_rows, tile_cols = (cotangent.shape[0], cotangent.shape[1])
    slots = lon_count * MOST
    patch_count = tile_rows // PH * (tile_cols // PW)
    loss_scale = 1.0 / math.sqrt(tile_rows * lat_count * tile_cols * lon_count)
    all_target, all_patch, all_kernel = gather_turned(
        (block_target, block_patch, block_kernel), "lon", (0, 0, 0)
    )
    all_target = all_target.reshape(lon_count, blocks)
    all_patch = all_patch.reshape(lon_count, blocks)
    all_kernel = all_kernel.reshape(lon_count, blocks)
    own_slot = slot_layout(block_target, lon_count)
    slot_ids = jnp.arange(slots, dtype=jnp.int32)
    chosen_slots = own_slot[None, :] == slot_ids[:, None]
    filled = jnp.any(chosen_slots, axis=1)
    source_block = jnp.sum(chosen_slots * jnp.arange(blocks, dtype=jnp.int32)[None, :], axis=1)
    all_slot = slot_layout(all_target, lon_count)
    wanted = own_lon * MOST + jnp.arange(MOST, dtype=jnp.int32)
    arrive = (all_slot[:, None, :] == wanted[None, :, None]).astype(jnp.int32)
    present = jnp.sum(arrive, axis=2).reshape(-1) > 0
    slot_kernel = jnp.sum(arrive * all_kernel[:, None, :], axis=2).reshape(-1)
    slot_kernel = jnp.where(present, slot_kernel, -1)
    slot_patch = jnp.sum(arrive * all_patch[:, None, :], axis=2).reshape(-1)
    taken = jnp.take(spectra.reshape(blocks, block_rows, channels), source_block, axis=0)
    taken = jnp.where(filled[:, None, None], taken, jnp.zeros_like(taken))
    arrived = lax.all_to_all(
        taken.reshape(lon_count, MOST, -1), "lon", split_axis=0, concat_axis=0, tiled=True
    )
    slot_spectra = arrived.reshape(slots * block_rows, channels)
    slot_preact = jnp.dot(slot_spectra, encoder_weight, preferred_element_type=jnp.float32)
    slot_rows = jax.nn.silu(slot_preact).astype(jnp.bfloat16).reshape(slots, block_rows, width)
    kernel_pick = (
        slot_kernel[:, None] == jnp.arange(kernel_count, dtype=jnp.int32)[None, :]
    ).astype(jnp.bfloat16)
    slot_kernels = jnp.dot(
        kernel_pick, kernels.reshape(kernel_count, -1), preferred_element_type=jnp.float32
    )
    slot_kernels = slot_kernels.astype(jnp.bfloat16).reshape(slots, block_rows, patch_cells)
    contribution = jnp.einsum(
        "sbp,sbd->spd", slot_kernels, slot_rows, preferred_element_type=jnp.float32
    )
    patch_pick = (slot_patch[:, None] == jnp.arange(patch_count, dtype=jnp.int32)[None, :]).astype(
        jnp.float32
    )
    tile_patches = jnp.einsum(
        "sq,spd->qpd", patch_pick, contribution, precision=lax.Precision.HIGHEST
    )
    spread = to_tile(tile_patches, tile_rows, tile_cols, width)
    normed = normalise(spread, gain).astype(jnp.bfloat16)
    padded = widen(normed)
    windows = []
    result_sum = jnp.zeros((tile_rows * tile_cols, width), jnp.float32)
    for row_shift in range(3):
        for col_shift in range(3):
            window = padded[
                row_shift : row_shift + tile_rows, col_shift : col_shift + tile_cols
            ].reshape(-1, width)
            windows.append(window)
            result_sum = result_sum + jnp.dot(
                window, conv_weight[row_shift, col_shift], preferred_element_type=jnp.float32
            )
    conv_out = result_sum.reshape(tile_rows, tile_cols, width).astype(jnp.bfloat16)
    cot_padded = widen(cotangent)
    cot_flat = cotangent.reshape(-1, width)
    d_normed = jnp.zeros((tile_rows * tile_cols, width), jnp.float32)
    kernel_grads = []
    for row_shift in range(3):
        for col_shift in range(3):
            back_window = cot_padded[
                2 - row_shift : 2 - row_shift + tile_rows, 2 - col_shift : 2 - col_shift + tile_cols
            ].reshape(-1, width)
            d_normed = d_normed + lax.dot_general(
                back_window,
                conv_weight[row_shift, col_shift],
                (((1,), (1,)), ((), ())),
                preferred_element_type=jnp.float32,
            )
            kernel_grads.append(
                lax.dot_general(
                    windows[row_shift * 3 + col_shift],
                    cot_flat,
                    (((0,), (0,)), ((), ())),
                    preferred_element_type=jnp.float32,
                )
            )
    conv_part = jnp.stack(kernel_grads).reshape(3, 3, width, width)
    _, pullback = jax.vjp(normalise, spread, gain)
    d_spread, gain_part = pullback(d_normed.reshape(tile_rows, tile_cols, width))
    d_patches = to_patches(d_spread.astype(jnp.bfloat16), tile_rows, tile_cols, width)
    slot_dpatch = jnp.take(d_patches, slot_patch, axis=0)
    slot_drows = jnp.einsum(
        "sbp,spd->sbd", slot_kernels, slot_dpatch, preferred_element_type=jnp.float32
    ).astype(jnp.bfloat16)
    d_preact = (slot_drows.reshape(-1, width).astype(jnp.float32) * silu_slope(slot_preact)).astype(
        jnp.bfloat16
    )
    encoder_part = lax.dot_general(
        slot_spectra, d_preact, (((0,), (0,)), ((), ())), preferred_element_type=jnp.float32
    )
    conv_total, encoder_total, gain_total = lax.psum(
        (conv_part, encoder_part, gain_part), ("lat", "lon")
    )
    return (conv_out, conv_total * loss_scale, encoder_total * loss_scale, gain_total * loss_scale)


def solution(mesh):
    placed = (
        P(("lat", "lon"), None),
        P(("lat", "lon")),
        P(("lat", "lon")),
        P(("lat", "lon")),
        P(),
        P(),
        P(),
        P(),
        P("lat", "lon", None),
    )
    return jax.shard_map(
        shards,
        mesh=mesh,
        in_specs=placed,
        out_specs=(P("lat", "lon", None), P(), P(), P()),
        check_vma=False,
    )
```

profile of v0, /device:TPU:1, one launch (start us, length us, event | category | flops | bytes accessed | tf_op | source)
XLA Modules:
  0.0 534.3 jit_solution(6251264387614628848)
XLA Ops:
  10.5 20.2 %all-gather = s32[16,24,3]{1,2,0:T(4,128)S(1)} all-gather(s32[1,24,3]{1,2,0:T(4,128)S(1)} %add_bitcast_fusion), channel_id=1, replica_groups=mesh['lat'=8,'lon'=16] {'lon'}, dimensions={0}, use_global_device_ids=true | all-gather | bytes 4896 | tf_op jit(solution)/shard_map/all_gather | solution.py:29
  32.4 4.6 copy_bitcast_fusion
  37.0 7.6 %gather_fusion = bf16[48,128,616]{1,2,0:T(8,128)(2,1)} fusion(bf16[24,128,616]{1,2,0:T(8,128)(2,1)} %copy_bitcast_fusion, s32[1024]{0:T(1024)S(1)} %get-tuple-element.49), kind=kCustom, calls=%fused_computation | custom fusion | bytes 15139008 | tf_op jit(solution)/shard_map/jit(_take)/gather | solution.py:110
  44.7 10.3 %copy.102 = bf16[48,128,616]{2,1,0:T(8,128)(2,1)} copy(bf16[48,128,616]{1,2,0:T(8,128)(2,1)} %gather_fusion) | data formatting | bytes 15138816 | tf_op jit(solution)/shard_map/jit(_take)/gather | solution.py:110
  55.0 20.1 %gather.11 = bf16[16,3,78848]{2,1,0:T(4,128)(2,1)} reshape(bf16[48,128,616]{2,1,0:T(8,128)(2,1)} %copy.102) | data formatting | bytes 15138816 | tf_op jit(solution)/shard_map/jit(_take)/gather | solution.py:110
  75.3 9.7 %select_select_fusion = bf16[16,3,78848]{2,1,0:T(4,128)(2,1)} fusion(bf16[16,3,78848]{2,1,0:T(4,128)(2,1)} %gather.11, pred[16,3]{1,0:T(8,128)(4,1)S(1)} %copy.100, pred[16,3]{1,0:T(8,128)(4,1)S(1)} %broadcast_in_dim.57), kind=kLoop, calls=%fused_computation.9 | loop fusion | flops 7569408 | bytes 15138912 | tf_op jit(solution)/shard_map/jit(_where)/select_n | solution.py:111
  85.1 5.0 all-to-all-start
  90.2 1.4 collective-permute-start.4
  91.6 3.5 collective-permute-start.5
  95.3 2.1 fusion.41
  98.1 1.6 copy.116
  99.7 105.0 %collective-permute-done.4 = bf16[24,1,512]{2,1,0:T(2,128)(2,1)S(1)} collective-permute-done((bf16[24,1,512]{2,1,0:T(2,128)(2,1)S(1)}, bf16[24,1,512]{2,1,0:T(2,128)(2,1)S(1)}, u32[]{:S(2)}, u32[]{:S(2)}) %collective-permute-start.4) | collective-permute-done | bytes 24608 | tf_op jit(solution)/shard_map/ppermute | solution.py:20
  204.6 5.4 %collective-permute-done.5 = bf16[24,1,512]{2,1,0:T(2,128)(2,1)S(1)} collective-permute-done((bf16[24,1,512]{2,1,0:T(2,128)(2,1)S(1)}, bf16[24,1,512]{2,1,0:T(2,128)(2,1)S(1)}, u32[]{:S(2)}, u32[]{:S(2)}) %collective-permute-start.5) | collective-permute-done | bytes 24608 | tf_op jit(solution)/shard_map/ppermute | solution.py:21
  210.1 8.3 %collective-permute-start.6 = (bf16[1,66,512]{2,1,0:T(8,128)(2,1)S(1)}, bf16[1,66,512]{2,1,0:T(8,128)(2,1)S(1)}, u32[]{:S(2)}, u32[]{:S(2)}) collective-permute-start(bf16[1,66,512]{2,1,0:T(8,128)(2,1)S(1)} %get-tuple-element.34), channel_id=1, source_target_pairs={{16,0},{32,16},{48,32},{64,48},{80,64},{96,80},{112,96},{17,1},{33... | collective-permute-start | bytes 202760 | tf_op jit(solution)/shard_map/ppermute | solution.py:21
  218.4 3.2 collective-permute-start.7
  222.8 2.0 pad_maximum_fusion.1
  224.8 2.3 fusion.96
  234.6 2.7 convolution_add_fusion
  237.4 20.1 %reshape.267 = bf16[6144,616]{1,0:T(8,128)(2,1)} reshape(bf16[16,3,78848]{2,1,0:T(4,128)(2,1)} %all-to-all-done) | data formatting | bytes 15138816 | tf_op jit(solution)/shard_map/reshape | solution.py:115
  257.5 11.7 %multiply_convert_fusion = (bf16[6144,512]{1,0:T(8,128)(2,1)S(1)}, f32[6144,512]{1,0:T(8,128)}) fusion(bf16[6144,616]{1,0:T(8,128)(2,1)} %reshape.267, bf16[616,512]{1,0:T(8,128)(2,1)S(1)} %copy-done), kind=kOutput, calls=%fused_computation.7 | convolution fusion | flops 3891265536 | bytes 27074560 | tf_op jit(solution)/shard_map/dot_general | solution.py:116
  269.2 1.8 fusion.101
  271.0 12.0 %fusion.1 = f32[12,128,512]{2,0,1:T(8,128)S(1)} fusion(f32[48,128,512]{2,1,0:T(8,128)S(1)} %fusion.101, s32[48]{0:T(128)S(1)} %eq.86), kind=kOutput, calls=%fused_computation.5 | convolution fusion | flops 452985408 | bytes 15728832 | tf_op jit(solution)/shard_map/sq,spd->qpd/dot_general | solution.py:131
  283.0 1.8 copy.105
  284.9 2.0 copy.106
  288.5 2.2 fusion.13
  290.8 2.2 multiply_convert_fusion.2
  293.1 1.2 copy-done.5
  294.4 4.8 collective-permute-start.1
  299.2 6.6 %gather_fusion.1 = bf16[48,128,512]{2,1,0:T(8,128)(2,1)} fusion(bf16[12,128,512]{2,1,0:T(8,128)(2,1)} %bitcast.199, s32[1024]{0:T(1024)S(1)} %get-tuple-element.48), kind=kCustom, calls=%fused_computation.1 | custom fusion | bytes 12583104 | tf_op jit(solution)/shard_map/jit(_take)/gather | solution.py:176
  305.7 5.3 fusion.6
  311.0 7.8 %fusion = bf16[6144,512]{1,0:T(8,128)(2,1)S(1)} fusion(f32[6144,512]{1,0:T(8,128)} %get-tuple-element.47, bf16[48,128,512]{2,1,0:T(8,128)(2,1)S(1)} %fusion.6), kind=kLoop, calls=%fused_computation.4 | loop fusion | flops 31457280 | bytes 25165824 | tf_op jit(solution)/shard_map/convert_element_type | solution.py:180
  318.8 5.1 fusion.102
  324.0 4.8 collective-permute-start.2
  328.9 1.9 collective-permute-start.3
  330.8 1.1 pad_maximum_fusion.4
  332.0 2.6 collective-permute-done.3
  334.5 2.3 maximum_maximum_fusion
  346.1 3.7 copy-done.16
  350.0 2.9 copy.108
  352.8 2.3 fusion.15
  355.1 66.2 %psum.23 = f32[512]{0:T(512)S(1)} all-reduce(f32[512]{0:T(512)S(1)} %fusion.15), channel_id=1, replica_groups=mesh['lat'=8,'lon'=16] {'lat','lon'}, use_global_device_ids=true, to_apply=%region_14.15 | all-reduce | flops 512 | bytes 4096 | tf_op jit(solution)/shard_map/psum | solution.py:186
  421.9 2.6 fusion.43
  424.6 1.1 fusion.95
  427.3 1.1 fusion.94
  435.3 2.2 fusion.17
  437.4 79.1 %all-reduce.3.cloned.1.call-done = (f32[3,3,512,512]{3,2,1,0:T(8,128)}, f32[616,512]{1,0:T(8,128)}) async-done(((f32[3,3,512,512]{3,2,1,0:T(8,128)}, f32[616,512]{1,0:T(8,128)}), (f32[3,3,512,512]{3,2,1,0:T(8,128)}, f32[616,512]{1,0:T(8,128)})) %all-reduce.3.cloned.1.call-update) | async-done | bytes 10698768 | tf_op jit(solution)/shard_map/psum | solution.py:186
  516.5 9.2 %broadcast_multiply_fusion = f32[3,3,512,512]{3,2,1,0:T(8,128)} fusion(f32[3,3,512,512]{3,2,1,0:T(8,128)} %get-tuple-element.12), kind=kLoop, calls=%fused_computation.14 | loop fusion | flops 2359296 | bytes 18874368 | tf_op jit(solution)/shard_map/mul | solution.py:189
  525.7 1.2 broadcast_multiply_fusion.1
  (131 shorter events, 35.2 us)
Async XLA Ops:
  7.2 250.3 %copy-start = (bf16[616,512]{1,0:T(8,128)(2,1)S(1)}, bf16[616,512]{1,0:T(8,128)(2,1)}, u32[]{:S(2)}) copy-start(bf16[616,512]{1,0:T(8,128)(2,1)} %param.13) | copy-start | bytes 1892356
  85.1 5.0 copy-start.2
  85.1 152.3 %all-to-all-start = ((bf16[16,3,78848]{2,1,0:T(4,128)(2,1)}), bf16[16,3,78848]{2,1,0:T(4,128)(2,1)}, u32[]{:S(2)}, u32[]{:S(2)}) async-start(bf16[16,3,78848]{2,1,0:T(4,128)(2,1)} %select_select_fusion), calls=%async_computation | async-start | bytes 20185088 | tf_op jit(solution)/shard_map/all_to_all | solution.py:112
  90.0 426.5 %all-reduce.3.cloned.1.call-start = ((), (), s32[]{:S(2)}) async-start(), calls=%async_computation.1 | async-start | bytes 21397504 | tf_op jit(solution)/shard_map/psum | solution.py:186
  90.2 114.4 %collective-permute-start.4 = (bf16[24,1,512]{2,1,0:T(2,128)(2,1)S(1)}, bf16[24,1,512]{2,1,0:T(2,128)(2,1)S(1)}, u32[]{:S(2)}, u32[]{:S(2)}) collective-permute-start(bf16[24,1,512]{2,1,0:T(2,128)(2,1)S(1)} %get-tuple-element.42), channel_id=1, source_target_pairs={{0,1},{1,2},{2,3},{3,4},{4,5},{5,6},{6,7},{7,8},{8,9},{9,10},{10,1... | collective-permute-start | bytes 73736 | tf_op jit(solution)/shard_map/ppermute | solution.py:20
  91.6 118.5 %collective-permute-start.5 = (bf16[24,1,512]{2,1,0:T(2,128)(2,1)S(1)}, bf16[24,1,512]{2,1,0:T(2,128)(2,1)S(1)}, u32[]{:S(2)}, u32[]{:S(2)}) collective-permute-start(bf16[24,1,512]{2,1,0:T(2,128)(2,1)S(1)} %get-tuple-element.43), channel_id=1, source_target_pairs={{1,0},{2,1},{3,2},{4,3},{5,4},{6,5},{7,6},{8,7},{9,8},{10,9},{11,1... | collective-permute-start | bytes 73736 | tf_op jit(solution)/shard_map/ppermute | solution.py:21
  95.3 2.2 copy-start.18
  210.1 12.6 %collective-permute-start.6 = (bf16[1,66,512]{2,1,0:T(8,128)(2,1)S(1)}, bf16[1,66,512]{2,1,0:T(8,128)(2,1)S(1)}, u32[]{:S(2)}, u32[]{:S(2)}) collective-permute-start(bf16[1,66,512]{2,1,0:T(8,128)(2,1)S(1)} %get-tuple-element.34), channel_id=1, source_target_pairs={{16,0},{32,16},{48,32},{64,48},{80,64},{96,80},{112,96},{17,1},{33... | collective-permute-start | bytes 202760 | tf_op jit(solution)/shard_map/ppermute | solution.py:21
  218.4 4.4 collective-permute-start.7
  222.8 4.4 slice-start
  224.8 2.4 slice-start.1
  257.5 11.7 %copy-start.9 = (bf16[6,8,128,128]{3,2,1,0:T(8,128)(2,1)S(1)}, bf16[6,8,128,128]{3,2,1,0:T(8,128)(2,1)}, u32[]{:S(2)}) copy-start(bf16[6,8,128,128]{3,2,1,0:T(8,128)(2,1)} %copy.116) | copy-start | bytes 4718596
  284.9 3.0 copy-start.3
  284.9 3.0 copy-start.19
  293.1 1.2 copy-start.5
  294.3 29.7 %collective-permute-start = (bf16[24,1,512]{2,1,0:T(2,128)(2,1)S(1)}, bf16[24,1,512]{2,1,0:T(2,128)(2,1)S(1)}, u32[]{:S(2)}, u32[]{:S(2)}) collective-permute-start(bf16[24,1,512]{2,1,0:T(2,128)(2,1)S(1)} %get-tuple-element.38), channel_id=1, source_target_pairs={{0,1},{1,2},{2,3},{3,4},{4,5},{5,6},{6,7},{7,8},{8,9},{9,10},{10,1... | collective-permute-start | bytes 73736 | tf_op jit(solution)/shard_map/ppermute | solution.py:20
  294.4 29.6 %collective-permute-start.1 = (bf16[24,1,512]{2,1,0:T(2,128)(2,1)S(1)}, bf16[24,1,512]{2,1,0:T(2,128)(2,1)S(1)}, u32[]{:S(2)}, u32[]{:S(2)}) collective-permute-start(bf16[24,1,512]{2,1,0:T(2,128)(2,1)S(1)} %get-tuple-element.39), channel_id=1, source_target_pairs={{1,0},{2,1},{3,2},{4,3},{5,4},{6,5},{7,6},{8,7},{9,8},{10,9},{11,1... | collective-permute-start | bytes 73736 | tf_op jit(solution)/shard_map/ppermute | solution.py:21
  305.7 13.0 %slice-start.4 = ((s8[7864320]{0:T(1024)(128)(4,1)}), s8[4194304]{0:T(1024)(128)(4,1)S(1)}, s32[]{:S(2)}) async-start(s8[7864320]{0:T(1024)(128)(4,1)} %bitcast.216), calls=%async_computation.6 | async-start | bytes 8388608
  311.0 7.8 %slice-start.5 = ((s8[7864320]{0:T(1024)(128)(4,1)}), s8[3670016]{0:T(1024)(128)(4,1)S(1)}, s32[]{:S(2)}) async-start(s8[7864320]{0:T(1024)(128)(4,1)} %bitcast.216), calls=%async_computation.7 | async-start | bytes 7340032
  318.8 5.2 copy-start.6
  324.0 7.9 %collective-permute-start.2 = (bf16[1,66,512]{2,1,0:T(8,128)(2,1)S(1)}, bf16[1,66,512]{2,1,0:T(8,128)(2,1)S(1)}, u32[]{:S(2)}, u32[]{:S(2)}) collective-permute-start(bf16[1,66,512]{2,1,0:T(8,128)(2,1)S(1)} %get-tuple-element.30), channel_id=1, source_target_pairs={{0,16},{16,32},{32,48},{48,64},{64,80},{80,96},{96,112},{1,17},{17... | collective-permute-start | bytes 202760 | tf_op jit(solution)/shard_map/ppermute | solution.py:20
  328.9 5.7 %collective-permute-start.3 = (bf16[1,66,512]{2,1,0:T(8,128)(2,1)S(1)}, bf16[1,66,512]{2,1,0:T(8,128)(2,1)S(1)}, u32[]{:S(2)}, u32[]{:S(2)}) collective-permute-start(bf16[1,66,512]{2,1,0:T(8,128)(2,1)S(1)} %get-tuple-element.31), channel_id=1, source_target_pairs={{16,0},{32,16},{48,32},{64,48},{80,64},{96,80},{112,96},{17,1},{33... | collective-permute-start | bytes 202760 | tf_op jit(solution)/shard_map/ppermute | solution.py:21
  331.9 8.0 %copy-start.14 = (bf16[24,64,512]{2,1,0:T(8,128)(2,1)}, bf16[24,64,512]{2,1,0:T(8,128)(2,1)S(1)}, u32[]{:S(2)}) copy-start(bf16[24,64,512]{2,1,0:T(8,128)(2,1)S(1)} %get-tuple-element.37) | copy-start | bytes 4718596
  331.9 10.0 %copy-start.12 = (bf16[24,64,512]{2,1,0:T(8,128)(2,1)}, bf16[24,64,512]{2,1,0:T(8,128)(2,1)S(1)}, u32[]{:S(2)}) copy-start(bf16[24,64,512]{2,1,0:T(8,128)(2,1)S(1)} %get-tuple-element.36) | copy-start | bytes 4718596
  336.8 2.1 copy-start.10
  336.8 8.2 %copy-start.7 = (bf16[25,66,512]{2,1,0:T(8,128)(2,1)}, bf16[25,66,512]{2,1,0:T(8,128)(2,1)S(1)}, u32[]{:S(2)}) copy-start(bf16[25,66,512]{2,1,0:T(8,128)(2,1)S(1)} %get-tuple-element.29) | copy-start | bytes 5068804
  346.1 3.7 copy-start.16
  349.9 3.0 copy-start.4
  421.9 2.6 copy-start.11
  421.9 3.8 slice-start.2
  424.6 1.2 slice-start.3
  425.8 1.5 copy-start.8
  430.5 1.4 copy-start.15
  431.9 1.4 copy-start.13
  516.5 9.2 %copy-start.17 = (f32[616,512]{1,0:T(8,128)S(1)}, f32[616,512]{1,0:T(8,128)}, u32[]{:S(2)}) copy-start(f32[616,512]{1,0:T(8,128)} %get-tuple-element.13) | copy-start | bytes 3784708
  516.5 10.4 %copy-start.1 = (bf16[616,512]{1,0:T(8,128)(2,1)S(1)}, bf16[616,512]{1,0:T(8,128)(2,1)}, u32[]{:S(2)}) copy-start(bf16[616,512]{1,0:T(8,128)(2,1)} %param.13) | copy-start | bytes 1892356
Sparse Core Ops, SparseCore 0:
  350.0 166.4 all-reduce.2
where the time goes:
time: 542 us; the launch traced here: 534 us
  waiting for transfers between devices  192 us (35%)
  local copies, waits for them, and re-layouts  91 us (17%)
  blocking collectives  86.4 us (16%)
  matrix products  69.9 us (13%)
  other arithmetic  46.6 us (9%)
  starting transfers between devices  33 us (6%)
  between operations  15.2 us (3%)
    ppermute x4, waiting for transfers between devices, padded_2(): before = lax.ppermute(last, axis, up)  105 us
    psum x1, waiting for transfers between devices, shards(): lax.psum((conv_part, encoder_part, gain_part), ('lat', 'lon'))  79.1 us
    psum x1, blocking collectives, shards(): lax.psum((conv_part, encoder_part, gain_part), ('lat', 'lon'))  66.2 us
    gather x3, local copies, waits for them, and re-layouts, shards(): jnp.take(spectra.reshape(blocks, block_rows, channels), source_block, axi...  38 us
    all_gather x1, blocking collectives, gather_turned(): lax.all_gather(both, axis, axis=0, tiled=True)  20.2 us
    reshape x1, local copies, waits for them, and re-layouts, shards(): slot_spectra = arrived.reshape(slots * block_rows, channels)  20.1 us
    ppermute x4, starting transfers between devices, padded_2(): after = lax.ppermute(leading, axis, down)  18.5 us
    dot_general x9, matrix products, shards(): lax.dot_general(back_window, conv_weight[row_shift, col_shift], (((1,), (...  12.3 us
  transfers between devices with their start and end apart: 10, of which 5 were waited for; matrix products, arithmetic and copies ran while one was open for 12% of the time, Pallas kernels for 0%

commit v1 on v0

v1 whole, which is shorter than its diff:
```python
import math

import jax
import jax.numpy as jnp
from jax import lax
from jax.experimental import pallas as pl
from jax.experimental.pallas import tpu as pltpu
from jax.sharding import PartitionSpec as P

PH = 8
PW = 16
MOST = 3
SIDE = 4
MESH = pl.DeviceIdType.MESH
VMEM_LIMIT = 60 * 1024 * 1024


def dot(a, b, ca, cb):
    return lax.dot_general(a, b, (((ca,), (cb,)), ((), ())), preferred_element_type=jnp.float32)


def pack_kernel(source_ref, spectra, to_a, to_b, held, blank, in_sem, out_sems):
    slots = source_ref.shape[0]
    rows = held.shape[1] // 2
    fetch = pltpu.make_async_copy(spectra, held, in_sem)
    fetch.start()
    blank[...] = jnp.zeros_like(blank)
    fetch.wait()

    def pieces(slot, source):
        tile = slot // MOST
        rank = slot - tile * MOST
        y, z = tile // SIDE, tile % SIDE
        return (
            pltpu.make_async_copy(source(0), to_a.at[z, y, rank], out_sems.at[slot, 0]),
            pltpu.make_async_copy(source(1), to_b.at[y, z, rank], out_sems.at[slot, 1]),
        )

    @pl.loop(0, slots)
    def _(slot):
        block = source_ref[slot]

        @pl.when(block >= 0)
        def _():
            for piece in pieces(slot, lambda half: held.at[block, pl.ds(half * rows, rows)]):
                piece.start()

        @pl.when(block < 0)
        def _():
            for piece in pieces(slot, lambda half: blank):
                piece.start()

    @pl.loop(0, slots)
    def _(slot):
        for piece in pieces(slot, lambda half: blank):
            piece.wait()


def pack(source_block, spectra, block_rows):
    blocks = spectra.shape[0] // block_rows
    channels = spectra.shape[1]
    half = block_rows // 2
    slots = source_block.shape[0]
    out = jax.ShapeDtypeStruct((SIDE, SIDE, MOST, half, channels), jnp.bfloat16)
    return pl.pallas_call(
        pack_kernel,
        name="pack",
        out_shape=(out, out),
        in_specs=[pl.BlockSpec(memory_space=pltpu.SMEM), pl.BlockSpec(memory_space=pl.ANY)],
        out_specs=(pl.BlockSpec(memory_space=pl.ANY),) * 2,
        scratch_shapes=[
            pltpu.VMEM((blocks, block_rows, channels), jnp.bfloat16),
            pltpu.VMEM((half, channels), jnp.bfloat16),
            pltpu.SemaphoreType.DMA,
            pltpu.SemaphoreType.DMA((slots, 2)),
        ],
        compiler_params=pltpu.CompilerParams(vmem_limit_bytes=VMEM_LIMIT),
    )(source_block, spectra.reshape(blocks, block_rows, channels))


def position():
    lat, lon = lax.axis_index("lat"), lax.axis_index("lon")
    return lat, lon, lon // SIDE, lon % SIDE


def halo_peers():
    lat, lon = lax.axis_index("lat"), lax.axis_index("lon")
    lats, lons = lax.axis_size("lat"), lax.axis_size("lon")
    up, down = (lat + lats - 1) % lats, (lat + 1) % lats
    left, right = (lon + lons - 1) % lons, (lon + 1) % lons
    return lat, lon, up, down, left, right


def halo_copies(top, bottom, first, last, from_above, from_below, from_left, from_right, sends, recvs):
    lat, lon, up, down, left, right = halo_peers()
    rows = first.shape[0]
    body = pl.ds(1, rows)
    plan = [
        (top, from_below, (up, lon)),
        (bottom, from_above, (down, lon)),
        (last, from_left.at[body], (lat, right)),
        (first, from_right.at[body], (lat, left)),
        (last.at[0], from_left.at[rows + 1], (up, right)),
        (last.at[rows - 1], from_left.at[0], (down, right)),
        (first.at[0], from_right.at[rows + 1], (up, left)),
        (first.at[rows - 1], from_right.at[0], (down, left)),
    ]
    return [
        pltpu.make_async_remote_copy(
            src_ref=src, dst_ref=dst, send_sem=sends.at[n], recv_sem=recvs.at[n], device_id=to, device_id_type=MESH
        )
        for n, (src, dst, to) in enumerate(plan)
    ]


def lay_windows(tile, from_above, from_below, from_left, from_right, wide, reverse):
    lat, lats = lax.axis_index("lat"), lax.axis_size("lat")
    rows, cols, width = tile.shape
    index = lax.broadcasted_iota(jnp.int32, (cols, width), 0)

    def lay(at, center, keep):
        value = center.astype(jnp.float32)
        before = jnp.where(index == 0, from_left[at], pltpu.roll(value, 1, 0))
        after = jnp.where(index == cols - 1, from_right[at], pltpu.roll(value, cols - 1, 0))
        if keep is not None:
            before, value, after = (jnp.where(keep, v, 0.0) for v in (before, value, after))
        order = (after, value, before) if reverse else (before, value, after)
        for n, v in enumerate(order):
            wide[at, :, n * width : (n + 1) * width] = v.astype(jnp.bfloat16)

    @pl.loop(0, rows)
    def _(row):
        lay(row + 1, tile[row], None)

    lay(0, from_above[...], lat > 0)
    lay(rows + 1, from_below[...], lat < lats - 1)


def exchange_kernel(
    send_a, send_b, meta, cot, first, last, weight,
    got_a, got_b, got_meta, wide_out, back_out, mid_a, mid_b, relay_a, relay_b,
    tile, wide, held_weight, back, above, below, lefts, rights,
    halo_send, halo_recv, meta_send, meta_recv, sends, recvs, local,
):
    lat, lon, y, z = position()
    lats = lax.axis_size("lat")
    count = lax.axis_size("lon")
    _, _, up, down, left, right = halo_peers()
    rows, cols, width = tile.shape

    barrier = pltpu.get_barrier_semaphore()
    for step in range(1, SIDE * SIDE):
        peer = (lon + step) % count
        pl.semaphore_signal(barrier, inc=1, device_id=(lat, peer), device_id_type=MESH)
    for other in (up, down):
        for peer in (left, lon, right):
            pl.semaphore_signal(barrier, inc=1, device_id=(other, peer), device_id_type=MESH)
    load_tile = pltpu.make_async_copy(cot, tile, local.at[0])
    load_weight = pltpu.make_async_copy(weight, held_weight, local.at[1])
    load_tile.start()
    load_weight.start()
    own_meta = pltpu.make_async_copy(meta.at[lon], got_meta.at[0], local.at[2])
    own_meta.start()
    pl.semaphore_wait(barrier, SIDE * SIDE - 1 + 6)

    halo = halo_copies(
        cot.at[0], cot.at[rows - 1], first, last, above, below, lefts, rights, halo_send, halo_recv
    )
    for copy in halo:
        copy.start()
    notes = []
    for dy in range(SIDE):
        for dz in range(SIDE):
            if dy or dz:
                n = dy * SIDE + dz
                to = (y + dy) % SIDE * SIDE + (z + dz) % SIDE
                notes.append(
                    pltpu.make_async_remote_copy(
                        src_ref=meta.at[to], dst_ref=got_meta.at[n], send_sem=meta_send.at[n],
                        recv_sem=meta_recv.at[n], device_id=(lat, to), device_id_type=MESH,
                    )
                )
    for copy in notes:
        copy.start()

    flows = []
    for flow, (src, mid, relay, got, u, v) in enumerate(
        ((send_a, mid_a, relay_a, got_a, z, y), (send_b, mid_b, relay_b, got_b, y, z))
    ):
        made = []

        def make(src_ref, dst_ref, du, dv, flow=flow, made=made, u=u, v=v):
            n = len(made)
            uu, vv = (u + du) % SIDE, (v + dv) % SIDE
            to = vv * SIDE + uu if flow == 0 else uu * SIDE + vv
            copy = pltpu.make_async_remote_copy(
                src_ref=src_ref, dst_ref=dst_ref, send_sem=sends.at[flow, n], recv_sem=recvs.at[flow, n],
                device_id=(lat, to), device_id_type=MESH,
            )
            made.append(copy)
            return copy

        def land(g, e, mid=mid, got=got):
            return got.at[0, e] if g == 0 else mid.at[g, e]

        def part(g, e, src=src, mid=mid, u=u, v=v):
            return src.at[u, (v + g) % SIDE] if e == 0 else mid.at[g, e]

        f = {"made": made}
        for d, sign in ((0, 1), (1, -1)):
            for j in range(2):
                g = 2 * d + j
                f["q1", d, j] = make(src.at[(u + 2) % SIDE, (v + g) % SIDE], relay.at[0, d, j], sign, 0)
                f["r1", d, j] = make(relay.at[0, d, j], land(g, 2), sign, 0)
            for g in range(SIDE):
                f["d1", d, g] = make(src.at[(u + sign) % SIDE, (v + g) % SIDE], land(g, 1 if d == 0 else 3), sign, 0)
            for e in range(SIDE):
                g = 1 if d == 0 else 3
                f["d2", d, e] = make(part(g, e), got.at[g, e], 0, sign)
            for j in range(2):
                e = ((0, 1), (3, 2))[d][j]
                f["q2", d, j] = make(part(2, e), relay.at[1, d, j], 0, sign)
                f["r2", d, j] = make(relay.at[1, d, j], got.at[2, e], 0, sign)
        flows.append(f)

    def start(*keys):
        for key in keys:
            for f in flows:
                f[key].start()

    def arrived(*keys):
        for key in keys:
            for f in flows:
                f[key].wait_recv()

    start(("q1", 0, 1), ("q1", 1, 0), ("q1", 0, 0), ("q1", 1, 1))
    for g in (2, 1, 3, 0):
        start(("d1", 0, g), ("d1", 1, g))

    load_tile.wait()
    for copy in halo:
        copy.wait()
    lay_windows(tile, above, below, lefts, rights, wide, True)
    save_wide = pltpu.make_async_copy(wide, wide_out, local.at[3])
    save_wide.start()
    load_weight.wait()
    step_rows = 4

    @pl.loop(0, rows // step_rows)
    def _(chunk):
        total = jnp.zeros((step_rows * cols, width), jnp.float32)
        for a in range(3):
            for b in range(3):
                window = wide[pl.ds(chunk * step_rows + 2 - a, step_rows), :, b * width : (b + 1) * width]
                total += dot(window.reshape(step_rows * cols, width), held_weight[a * 3 + b], 1, 1)
        back[pl.ds(chunk * step_rows, step_rows)] = total.reshape(step_rows, cols, width)

    save_back = pltpu.make_async_copy(back, back_out, local.at[4])
    save_back.start()

    for d, j in ((0, 1), (1, 0), (0, 0), (1, 1)):
        arrived(("q1", d, j))
        start(("r1", d, j))
    start(("q2", 0, 0), ("d2", 0, 0), ("d2", 1, 0))
    for g in (2, 1, 3, 0):
        arrived(("d1", 0, g), ("d1", 1, g))
        if g == 2:
            start(("q2", 0, 1), ("q2", 1, 0))
        if g == 1:
            start(("d2", 0, 1), ("d2", 0, 3))
        if g == 3:
            start(("d2", 1, 1), ("d2", 1, 3))
    arrived(("r1", 1, 0))
    start(("q2", 1, 1))
    arrived(("r1", 0, 1), ("r1", 1, 1))
    arrived(("q2", 0, 0))
    start(("r2", 0, 0))
    arrived(("q2", 0, 1), ("q2", 1, 0))
    start(("r2", 0, 1), ("r2", 1, 0))
    start(("d2", 0, 2), ("d2", 1, 2))
    arrived(("q2", 1, 1))
    start(("r2", 1, 1))
    arrived(("r1", 0, 0))
    for d in range(2):
        arrived(*(("d2", d, e) for e in range(SIDE)))
        arrived(("r2", d, 0), ("r2", d, 1))
    for f in flows:
        for copy in f["made"]:
            copy.wait_send()
    for copy in notes:
        copy.wait()
    own_meta.wait()
    save_wide.wait()
    save_back.wait()


def exchange(send_a, send_b, meta, cotangent, first, last, weight):
    rows, cols, width = cotangent.shape
    slot = send_a.shape[2:]
    lon = SIDE * SIDE
    bf, f32 = jnp.bfloat16, jnp.float32
    anywhere = pl.BlockSpec(memory_space=pl.ANY)
    whole = jax.ShapeDtypeStruct((SIDE, SIDE) + slot, bf)
    relay = jax.ShapeDtypeStruct((2, 2, 2) + slot, bf)
    out = pl.pallas_call(
        exchange_kernel,
        name="exchange",
        out_shape=(
            whole, whole, jax.ShapeDtypeStruct(meta.shape, meta.dtype),
            jax.ShapeDtypeStruct((rows + 2, cols, 3 * width), bf), jax.ShapeDtypeStruct((rows, cols, width), f32),
            whole, whole, relay, relay,
        ),
        in_specs=[anywhere] * 7,
        out_specs=(anywhere,) * 9,
        scratch_shapes=[
            pltpu.VMEM((rows, cols, width), bf),
            pltpu.VMEM((rows + 2, cols, 3 * width), bf),
            pltpu.VMEM(weight.shape, bf),
            pltpu.VMEM((rows, cols, width), f32),
            pltpu.VMEM((cols, width), bf),
            pltpu.VMEM((cols, width), bf),
            pltpu.VMEM((rows + 2, 1, width), f32),
            pltpu.VMEM((rows + 2, 1, width), f32),
            pltpu.SemaphoreType.DMA((8,)),
            pltpu.SemaphoreType.DMA((8,)),
            pltpu.SemaphoreType.DMA((lon,)),
            pltpu.SemaphoreType.DMA((lon,)),
            pltpu.SemaphoreType.DMA((2, 32)),
            pltpu.SemaphoreType.DMA((2, 32)),
            pltpu.SemaphoreType.DMA((5,)),
        ],
        compiler_params=pltpu.CompilerParams(
            collective_id=0, has_side_effects=True, vmem_limit_bytes=VMEM_LIMIT
        ),
    )(send_a, send_b, meta, cotangent, first, last, weight)
    return out[:5]


def middle_kernel(
    meta, own_a, own_b, got_a, got_b, encoder, kernels, turned, gain, wide_in, back_in,
    normed, parts,
    x, slope, encoded, spread, d_spread, wide, back, flipped, d_rows, encoder_sum, gain_sum,
    x_sems, local,
):
    lat, lon, y, z = position()
    rows, cols, width = normed.shape
    channels = encoder.shape[0]
    sources = SIDE * SIDE
    block = kernels.shape[1]
    copies = []
    for n in range(sources):
        dy, dz = n // SIDE, n % SIDE
        from_a = own_a.at[z, y] if n == 0 else got_a.at[dy, dz]
        from_b = own_b.at[y, z] if n == 0 else got_b.at[dz, dy]
        copies.append(pltpu.make_async_copy(from_a, x.at[n, :, 0], x_sems.at[n, 0]))
        copies.append(pltpu.make_async_copy(from_b, x.at[n, :, 1], x_sems.at[n, 1]))
    for copy in copies:
        copy.start()
    load_back = pltpu.make_async_copy(back_in, back, local.at[0])
    load_wide = pltpu.make_async_copy(wide_in, wide, local.at[1])
    load_back.start()
    load_wide.start()
    spread[...] = jnp.zeros_like(spread)

    @pl.loop(0, sources)
    def _(n):
        for half in range(2):
            pltpu.make_async_copy(got_a.at[0, 0], x.at[n, :, half], x_sems.at[n, half]).wait()
        pre = dot(x[n].reshape(MOST * block, channels), encoder[...], 1, 0)
        logistic = 0.5 * jnp.tanh(0.5 * pre) + 0.5
        encoded[...] = (pre * logistic).astype(jnp.bfloat16)
        slope[n] = (logistic * (1.0 + pre * (1.0 - logistic))).astype(jnp.bfloat16)
        for rank in range(MOST):
            which, patch = meta[n, rank], meta[n, MOST + rank]

            @pl.when(which >= 0)
            def _():
                spread[patch] += dot(turned[which], encoded[rank * block : (rank + 1) * block], 1, 0)

    load_back.wait()
    gain_sum[...] = jnp.zeros_like(gain_sum)
    across = cols // PW

    @pl.loop(0, spread.shape[0])
    def _(q):
        at = (pl.ds(q // across * PH, PH), pl.ds(pl.multiple_of(q % across * PW, PW), PW))
        value = spread[q]
        scale = lax.rsqrt(jnp.mean(value * value, axis=1, keepdims=True) + 1e-06)
        unit = value * scale
        weight = gain[...]
        normed[at] = (unit * weight).astype(jnp.bfloat16).reshape(PH, PW, width)
        given = back[at].reshape(PH * PW, width)
        product = given * unit
        gain_sum[...] += jnp.sum(product.reshape(PH * PW // 8, 8, width), axis=0)
        inner = jnp.mean(product * weight, axis=1, keepdims=True)
        d_spread[q] = (scale * (given * weight - unit * inner)).astype(jnp.bfloat16)

    step_rows = 4

    @pl.loop(0, rows // step_rows)
    def _(n):
        some = normed[pl.ds(n * step_rows, step_rows)].reshape(step_rows * cols, width)
        flipped[:, pl.ds(pl.multiple_of(n * step_rows * cols, 128), step_rows * cols)] = some.T

    load_wide.wait()
    for a in range(3):

        @pl.loop(0, 3 * width // 256)
        def _(j):
            window = wide[2 - a : 2 - a + rows, :, pl.ds(pl.multiple_of(j * 256, 256), 256)]
            got = dot(flipped[...], window.reshape(rows * cols, 256), 1, 0).astype(jnp.bfloat16)
            base = pl.multiple_of((a * (3 * width // 128) + 2 * j) * width, width)
            parts[pl.ds(base, width)] = got[:, :128]
            parts[pl.ds(pl.multiple_of(base + width, width), width)] = got[:, 128:]

    encoder_sum[...] = jnp.zeros_like(encoder_sum)

    @pl.loop(0, sources)
    def _(n):
        for rank in range(MOST):
            which, patch = jnp.maximum(meta[n, rank], 0), meta[n, MOST + rank]
            at = slice(rank * block, (rank + 1) * block)
            here = dot(kernels[which], d_spread[patch], 1, 0).astype(jnp.bfloat16).astype(jnp.float32)
            d_rows[at] = (here * slope[n, at].astype(jnp.float32)).astype(jnp.bfloat16)
        encoder_sum[...] += dot(x[n].reshape(MOST * block, channels), d_rows[...], 0, 0)

    base = 9 * width * width // 128
    for n in range(width // 128):
        lanes = slice(n * 128, (n + 1) * 128)
        parts[base + n * channels : base + (n + 1) * channels] = encoder_sum[:, lanes].astype(jnp.bfloat16)
    base += channels * width // 128
    for n in range(width // 128):
        parts[base + n * 8 : base + (n + 1) * 8] = gain_sum[:, n * 128 : (n + 1) * 128].astype(jnp.bfloat16)
    base += 8 * width // 128
    parts[base:] = jnp.zeros((parts.shape[0] - base, 128), jnp.bfloat16)


def middle(meta, own_a, own_b, got_a, got_b, encoder, kernels, gain, wide, back, part_rows):
    rows, cols, width = back.shape
    channels = encoder.shape[0]
    block, cells = kernels.shape[1:]
    patches = rows * cols // cells
    sources = SIDE * SIDE
    bf, f32 = jnp.bfloat16, jnp.float32
    anywhere = pl.BlockSpec(memory_space=pl.ANY)
    local = pl.BlockSpec(memory_space=pltpu.VMEM)
    return pl.pallas_call(
        middle_kernel,
        name="middle",
        out_shape=(jax.ShapeDtypeStruct((rows, cols, width), bf), jax.ShapeDtypeStruct((part_rows, 128), bf)),
        in_specs=[pl.BlockSpec(memory_space=pltpu.SMEM)] + [anywhere] * 4 + [local] * 4 + [anywhere] * 2,
        out_specs=(local, local),
        scratch_shapes=[
            pltpu.VMEM((sources, MOST, 2, block // 2, channels), bf),
            pltpu.VMEM((sources, MOST * block, width), bf),
            pltpu.VMEM((MOST * block, width), bf),
            pltpu.VMEM((patches, cells, width), f32),
            pltpu.VMEM((patches, cells, width), bf),
            pltpu.VMEM(wide.shape, bf),
            pltpu.VMEM(back.shape, f32),
            pltpu.VMEM((width, rows * cols), bf),
            pltpu.VMEM((MOST * block, width), bf),
            pltpu.VMEM((channels, width), f32),
            pltpu.VMEM((8, width), f32),
            pltpu.SemaphoreType.DMA((sources, 2)),
            pltpu.SemaphoreType.DMA((2,)),
        ],
        compiler_params=pltpu.CompilerParams(vmem_limit_bytes=VMEM_LIMIT),
    )(meta, own_a, own_b, got_a, got_b, encoder, kernels, kernels.swapaxes(1, 2), gain, wide, back)


def padded_2(shard, sides, width, wrap):
    for axis, dim in sides:
        size, length = (lax.axis_size(axis), shard.shape[dim])
        up = [(i, (i + 1) % size) for i in range(size if wrap else size - 1)]
        down = [(j, i) for i, j in up]
        last = lax.slice_in_dim(shard, length - width, length, axis=dim)
        leading = lax.slice_in_dim(shard, 0, width, axis=dim)
        before = lax.ppermute(last, axis, up)
        after = lax.ppermute(leading, axis, down)
        shard = jnp.concatenate([before, shard, after], axis=dim)
    return shard


def widen(field):
    beside_all = padded_2(field, (("lon", 1),), 1, True)
    return padded_2(beside_all, (("lat", 0),), 1, False)


def slot_tables(target, patch, kernel, tiles):
    blocks = target.shape[0]
    index = jnp.arange(blocks, dtype=jnp.int32)
    same = (target[:, None] == target[None, :]) & (index[None, :] < index[:, None])
    slot = target * MOST + jnp.sum(same, axis=1, dtype=jnp.int32)
    chosen = slot[None, :] == jnp.arange(tiles * MOST, dtype=jnp.int32)[:, None]

    def pick(values):
        return jnp.sum(jnp.where(chosen, values[None, :] + 1, 0), axis=1, dtype=jnp.int32) - 1

    source, kernels, patches = pick(index), pick(kernel), jnp.maximum(pick(patch), 0)
    meta = jnp.concatenate([kernels.reshape(tiles, MOST), patches.reshape(tiles, MOST)], axis=1)
    return source, jnp.pad(meta, ((0, 0), (0, 128 - 2 * MOST))).reshape(tiles, 1, 128)


def shards(spectra, target, patch, kernel, encoder_weight, kernels, gain, conv_weight, cotangent):
    tiles, bands = lax.axis_size("lon"), lax.axis_size("lat")
    rows, cols, width = cotangent.shape
    channels = spectra.shape[1]
    loss_scale = 1.0 / math.sqrt(rows * bands * cols * tiles)
    source, meta = slot_tables(target, patch, kernel, tiles)
    send_a, send_b = pack(source, spectra, kernels.shape[1])
    first = cotangent[:, :1].astype(jnp.float32)
    last = cotangent[:, -1:].astype(jnp.float32)
    weight = conv_weight.reshape(9, width, width)
    got_a, got_b, got_meta, wide, back = exchange(send_a, send_b, meta, cotangent, first, last, weight)
    part_rows = 192 * 112
    normed, parts = middle(
        got_meta.reshape(tiles, 128), send_a, send_b, got_a, got_b, encoder_weight, kernels,
        gain.reshape(1, width), wide, back, part_rows,
    )
    padded = widen(normed)
    total = jnp.zeros((rows * cols, width), jnp.float32)
    for a in range(3):
        for b in range(3):
            window = padded[a : a + rows, b : b + cols].reshape(-1, width)
            total = total + jnp.dot(window, conv_weight[a, b], preferred_element_type=jnp.float32)
    conv_out = total.reshape(rows, cols, width).astype(jnp.bfloat16)
    summed = lax.psum(parts.astype(jnp.float32), ("lat", "lon")) * loss_scale
    base = 9 * width * width // 128
    lanes = width // 128
    conv_grad = summed[:base].reshape(9, lanes, width, 128).swapaxes(1, 2).reshape(3, 3, width, width)
    size = channels * lanes
    encoder_grad = summed[base : base + size].reshape(lanes, channels, 128).swapaxes(0, 1).reshape(channels, width)
    gain_grad = summed[base + size : base + size + 8 * lanes].reshape(lanes, 8, 128).sum(axis=1).reshape(width)
    return conv_out, conv_grad, encoder_grad, gain_grad


def solution(mesh):
    placed = (
        P(("lat", "lon"), None),
        P(("lat", "lon")),
        P(("lat", "lon")),
        P(("lat", "lon")),
        P(),
        P(),
        P(),
        P(),
        P("lat", "lon", None),
    )
    return jax.shard_map(
        shards,
        mesh=mesh,
        in_specs=placed,
        out_specs=(P("lat", "lon", None), P(), P(), P()),
        check_vma=False,
    )
```

time: 542 us -> 353 us (0.65); the launches traced: 534 us -> 352 us
  waiting for transfers between devices: 192 us -> 2.4 us
  Pallas kernels: 0 us -> 148 us
  matrix products: 69.9 us -> 14.1 us
  local copies, waits for them, and re-layouts: 91 us -> 42.8 us
  blocking collectives: 86.4 us -> 119 us
  other arithmetic: 46.6 us -> 14.2 us
  starting transfers between devices: 33 us -> 11.2 us
  between operations: 15.2 us -> 0.85 us
    pallas_call x0 -> x3, Pallas kernels: none -> 148 us  [the longest x1 95.7 us: exchange(): pl.pallas_call(exchange_kernel, name='exchange', out_shape=(whole, whole,...]
    ppermute x4 -> x2, waiting for transfers between devices: 105 us -> 0.01 us  [padded_2(): before = lax.ppermute(last, axis, up)]
    psum x1 -> x0, waiting for transfers between devices: 79.1 us -> none  [shards(): lax.psum((conv_part, encoder_part, gain_part), ('lat', 'lon'))]
    dot_general x33 -> x9, matrix products: 69.9 us -> 14.1 us  [shards(): jnp.dot(window, conv_weight[a, b], preferred_element_type=jnp.float32)]
    psum x1, blocking collectives: 66.2 us -> 119 us  [shards(): summed = lax.psum(parts.astype(jnp.float32), ('lat', 'lon')) * loss_scale]
    gather x4 -> x0, local copies, waits for them, and re-layouts: 44.6 us -> none  [the longest x3 38 us: shards(): jnp.take(spectra.reshape(blocks, block_rows, channels), source_block, axi...]
    all_gather x1 -> x0, blocking collectives: 20.2 us -> none  [gather_turned(): lax.all_gather(both, axis, axis=0, tiled=True)]
    ppermute x4 -> x2, starting transfers between devices: 18.5 us -> 5.64 us  [padded_2(): after = lax.ppermute(leading, axis, down)]
  transfers between devices with their start and end apart: 10 -> 4, of which waited for: 5 -> 1; matrix products, arithmetic and copies ran while one was open for 12% -> 12% of each run, Pallas kernels for 0% -> 0%
where the time goes in v1:
time: 353 us; the launch traced here: 352 us
  Pallas kernels  148 us (42%)
  blocking collectives  119 us (34%)
  local copies, waits for them, and re-layouts  42.8 us (12%)
  other arithmetic  14.2 us (4%)
  matrix products  14.1 us (4%)
  starting transfers between devices  11.2 us (3%)
    psum x1, blocking collectives, shards(): summed = lax.psum(parts.astype(jnp.float32), ('lat', 'lon')) * loss_scale  119 us
    pallas_call x1, Pallas kernels, exchange(): pl.pallas_call(exchange_kernel, name='exchange', out_shape=(whole, whole,...  95.7 us
    pallas_call x1, Pallas kernels, middle(): pl.pallas_call(middle_kernel, name='middle', out_shape=(jax.ShapeDtypeStr...  45.5 us
    dot_general x9, matrix products, shards(): jnp.dot(window, conv_weight[a, b], preferred_element_type=jnp.float32)  14.1 us
    transpose x1, local copies, waits for them, and re-layouts, shards(): summed[:base].reshape(9, lanes, width, 128).swapaxes(1, 2)  13.3 us
    reshape x1, local copies, waits for them, and re-layouts, shards(): summed[:base].reshape(9, lanes, width, 128).swapaxes(1, 2)  12.3 us
    unnamed x14, local copies, waits for them, and re-layouts  8.01 us
  transfers between devices with their start and end apart: 4, of which 1 were waited for; matrix products, arithmetic and copies ran while one was open for 12% of the time, Pallas kernels for 0%

profile of v1, /device:TPU:1, one launch (start us, length us, event | category | flops | bytes accessed | tf_op | source)
XLA Modules:
  0.0 352.5 jit_solution(3877386010119065365)
XLA Ops:
  0.6 0.9 convert_reduce_fusion
  1.6 0.7 multiply_add_fusion
  2.2 0.7 broadcast_add_fusion.2
  2.9 0.7 broadcast_add_fusion.3
  3.5 0.1 select_reduce_fusion.1
  3.6 0.1 max.12
  3.7 0.1 sub.13
  3.8 0.5 broadcast_add_fusion.1.source_ref
  4.3 6.2 %copy.21 = bf16[3072,616]{1,0:T(8,128)(2,1)} copy(bf16[3072,616]{0,1:T(8,128)(2,1)} %param.9) | data formatting | bytes 7569408 | tf_op args[0]
  10.5 1.7 slice_convert_fusion
  12.2 1.0 copy.22
  13.2 0.1 pad_add_fusion
  13.3 0.6 pad.4
  13.9 6.8 %pack.1 = (bf16[4,4,3,64,616]{4,3,2,1,0:T(8,128)(2,1)}, bf16[4,4,3,64,616]{4,3,2,1,0:T(8,128)(2,1)}) custom-call(s32[48]{0:T(128)} %broadcast_add_fusion.1.source_ref, bf16[24,128,616]{2,1,0:T(8,128)(2,1)} %bitcast.73), custom_call_target="tpu_custom_call" | custom-call | tf_op jit(solution)/shard_map/pack/pallas_call | solution.py:65
  20.7 95.7 %exchange.1 = (bf16[4,4,3,64,616]{4,3,2,1,0:T(8,128)(2,1)}, bf16[4,4,3,64,616]{4,3,2,1,0:T(8,128)(2,1)}, s32[16,1,128]{2,1,0:T(1,128)}, bf16[26,64,1536]{2,1,0:T...) custom-call(bf16[4,4,3,64,616]{4,3,2,1,0:T(8,128)(2,1)} %get-tuple-e, ...), custom_call_target="tpu_custom_call" | custom-call | tf_op jit(solution)/shard_map/exchange/pallas_call | solution.py:305
  116.5 45.5 %middle.1 = (bf16[24,64,512]{2,1,0:T(8,128)(2,1)}, bf16[21504,128]{1,0:T(8,128)(2,1)}) custom-call(s32[16,128]{1,0:T(8,128)} %bitcast.86, bf16[4,4,3,64,616]{4,3,2,1,0:T(8,128)(2,1)} %get-tuple-element.13.send_a.own_a, bf16[4,4,3,64,616]{4,3,2,1,0:T(8,128)(2,1)} %get-tuple-element.14.send_b.own_b, bf16[4,4,3,64,616]{4,3,2,1,0:T(8,128)(2,1)} %get-tuple-element.16.got_a, ...), custom_call_target="tpu_custom_call" | custom-call | tf_op jit(solution)/shard_map/middle/pallas_call | solution.py:447
  162.0 1.1 fusion.28
  163.1 1.4 collective-permute-start
  164.5 3.5 collective-permute-start.1
  168.0 118.9 %all-reduce.2 = f32[21504,128]{1,0:T(8,128)} all-reduce(bf16[21504,128]{1,0:T(8,128)(2,1)} %get-tuple-element.21), channel_id=1, replica_groups=mesh['lat'=8,'lon'=16] {'lat','lon'}, use_global_device_ids=true, to_apply=%region_4.5 | all-reduce | flops 2752512 | bytes 16515072 | tf_op jit(solution)/shard_map/psum | solution.py:528
  286.8 5.0 %broadcast_multiply_fusion = f32[21504,128]{1,0:T(8,128)S(1)} fusion(f32[21504,128]{1,0:T(8,128)} %all-reduce.2), kind=kLoop, calls=%fused_computation | loop fusion | flops 2752512 | bytes 22020096 | tf_op jit(solution)/shard_map/mul | solution.py:528
  291.9 4.9 %fusion.8 = f32[1536,512]{1,0:T(8,128)} fusion(bf16[1536,512]{1,0:T(8,128)(2,1)S(1)} %bitcast.69, bf16[3,3,512,512]{3,2,1,0:T(8,128)(2,1)} %param.16), kind=kOutput, calls=%fused_computation.20 | convolution fusion | flops 805306368 | bytes 5242880 | tf_op jit(solution)/shard_map/dot_general | solution.py:526
  296.8 0.6 fusion.24
  297.4 3.9 %slice.118 = f32[18432,128]{1,0:T(8,128)} slice(f32[21504,128]{1,0:T(8,128)S(1)} %broadcast_multiply_fusion), slice={[0:18432], [0:128]} | slice | bytes 18874368 | tf_op jit(solution)/shard_map/slice | solution.py:531
  301.3 0.0 copy-done
  301.3 13.3 %copy.23 = f32[9,512,4,128]{3,2,1,0:T(4,128)} copy(f32[9,512,4,128]{3,1,2,0:T(8,128)} %bitcast.68) | data formatting | bytes 18874368 | tf_op jit(solution)/shard_map/transpose | solution.py:531
  314.6 12.3 %reshape.107 = f32[3,3,512,512]{3,2,1,0:T(8,128)} reshape(f32[9,512,4,128]{3,2,1,0:T(4,128)} %copy.23) | data formatting | bytes 18874368 | tf_op jit(solution)/shard_map/reshape | solution.py:531
  327.0 1.2 copy.27
  328.2 0.0 collective-permute-done
  328.2 0.0 collective-permute-done.1
  328.2 4.2 %collective-permute-start.2 = (bf16[1,66,512]{2,1,0:T(8,128)(2,1)S(1)}, bf16[1,66,512]{2,1,0:T(8,128)(2,1)S(1)}, u32[]{:S(2)}, u32[]{:S(2)}) collective-permute-start(bf16[1,66,512]{2,1,0:T(8,128)(2,1)S(1)} %get-tuple-element.33), channel_id=1, source_target_pairs={{0,16},{16,32},{32,48},{48,64},{64,80},{80,96},{96,112},{1,17},{17... | collective-permute-start | bytes 202760 | tf_op jit(solution)/shard_map/ppermute | solution.py:479
  332.5 2.1 collective-permute-start.3
  334.6 1.1 pad_maximum_fusion.1
  335.7 0.0 collective-permute-done.2
  335.7 2.4 collective-permute-done.3
  338.1 2.0 maximum_maximum_fusion
  340.2 0.0 slice-start.2
  340.2 1.1 fusion.27
  341.3 1.0 fusion.12
  342.3 1.1 fusion.26
  343.4 1.0 fusion.5
  344.4 1.1 convolution_add_fusion.5
  345.4 1.1 convolution_add_fusion.4
  346.5 0.8 copy-done.2
  347.3 1.0 fusion.1
  348.3 1.0 fusion
  349.3 1.0 convolution_add_fusion.1
  350.3 2.2 fusion.2
  (15 shorter events, 0.1 us)
Async XLA Ops:
  4.3 7.9 %copy-start.3 = (bf16[16,128,128]{2,1,0:T(8,128)(2,1)S(1)}, bf16[16,128,128]{2,1,0:T(8,128)(2,1)}, u32[]{:S(2)}) copy-start(bf16[16,128,128]{2,1,0:T(8,128)(2,1)} %kernels.1) | copy-start | bytes 1572868
  163.1 165.1 %collective-permute-start = (bf16[24,1,512]{2,1,0:T(2,128)(2,1)S(1)}, bf16[24,1,512]{2,1,0:T(2,128)(2,1)S(1)}, u32[]{:S(2)}, u32[]{:S(2)}) collective-permute-start(bf16[24,1,512]{2,1,0:T(2,128)(2,1)S(1)} %get-tuple-element.37), channel_id=1, source_target_pairs={{0,1},{1,2},{2,3},{3,4},{4,5},{5,6},{6,7},{7,8},{8,9},{9,10},{10,1... | collective-permute-start | bytes 73736 | tf_op jit(solution)/shard_map/ppermute | solution.py:479
  164.5 163.7 %collective-permute-start.1 = (bf16[24,1,512]{2,1,0:T(2,128)(2,1)S(1)}, bf16[24,1,512]{2,1,0:T(2,128)(2,1)S(1)}, u32[]{:S(2)}, u32[]{:S(2)}) collective-permute-start(bf16[24,1,512]{2,1,0:T(2,128)(2,1)S(1)} %get-tuple-element.38), channel_id=1, source_target_pairs={{1,0},{2,1},{3,2},{4,3},{5,4},{6,5},{7,6},{8,7},{9,8},{10,9},{11,1... | collective-permute-start | bytes 73736 | tf_op jit(solution)/shard_map/ppermute | solution.py:480
  286.8 5.1 %copy-start.1 = (bf16[24,64,512]{2,1,0:T(8,128)(2,1)S(1)}, bf16[24,64,512]{2,1,0:T(8,128)(2,1)}, u32[]{:S(2)}) copy-start(bf16[24,64,512]{2,1,0:T(8,128)(2,1)} %get-tuple-element.20) | copy-start | bytes 4718596
  291.9 9.4 %copy-start = (f32[21504,128]{1,0:T(8,128)}, f32[21504,128]{1,0:T(8,128)S(1)}, u32[]{:S(2)}) copy-start(f32[21504,128]{1,0:T(8,128)S(1)} %broadcast_multiply_fusion) | copy-start | bytes 33030148
  314.6 12.3 %slice-start = ((f32[21504,128]{1,0:T(8,128)}), f32[2464,128]{1,0:T(8,128)S(1)}, s32[]{:S(2)}) async-start(f32[21504,128]{1,0:T(8,128)} %copy-done), calls=%async_computation | async-start | bytes 2523136 | tf_op jit(solution)/shard_map/slice | solution.py:533
  328.2 7.5 %collective-permute-start.2 = (bf16[1,66,512]{2,1,0:T(8,128)(2,1)S(1)}, bf16[1,66,512]{2,1,0:T(8,128)(2,1)S(1)}, u32[]{:S(2)}, u32[]{:S(2)}) collective-permute-start(bf16[1,66,512]{2,1,0:T(8,128)(2,1)S(1)} %get-tuple-element.33), channel_id=1, source_target_pairs={{0,16},{16,32},{32,48},{48,64},{64,80},{80,96},{96,112},{1,17},{17... | collective-permute-start | bytes 202760 | tf_op jit(solution)/shard_map/ppermute | solution.py:479
  332.5 5.7 %collective-permute-start.3 = (bf16[1,66,512]{2,1,0:T(8,128)(2,1)S(1)}, bf16[1,66,512]{2,1,0:T(8,128)(2,1)S(1)}, u32[]{:S(2)}, u32[]{:S(2)}) collective-permute-start(bf16[1,66,512]{2,1,0:T(8,128)(2,1)S(1)} %get-tuple-element.34), channel_id=1, source_target_pairs={{16,0},{32,16},{48,32},{64,48},{80,64},{96,80},{112,96},{17,1},{33... | collective-permute-start | bytes 202760 | tf_op jit(solution)/shard_map/ppermute | solution.py:480
  338.1 3.2 slice-start.1
  340.2 1.1 slice-start.2
  345.4 1.9 copy-start.2

commit v2 on v1

--- a/solution.py
+++ b/solution.py
@@ -469,22 +469,269 @@
     )(meta, own_a, own_b, got_a, got_b, encoder, kernels, kernels.swapaxes(1, 2), gain, wide, back)
 
 
-def padded_2(shard, sides, width, wrap):
-    for axis, dim in sides:
-        size, length = (lax.axis_size(axis), shard.shape[dim])
-        up = [(i, (i + 1) % size) for i in range(size if wrap else size - 1)]
-        down = [(j, i) for i, j in up]
-        last = lax.slice_in_dim(shard, length - width, length, axis=dim)
-        leading = lax.slice_in_dim(shard, 0, width, axis=dim)
-        before = lax.ppermute(last, axis, up)
-        after = lax.ppermute(leading, axis, down)
-        shard = jnp.concatenate([before, shard, after], axis=dim)
-    return shard
-
-
-def widen(field):
-    beside_all = padded_2(field, (("lon", 1),), 1, True)
-    return padded_2(beside_all, (("lat", 0),), 1, False)
+PIECES = 16
+PIECE_ROWS = 112
+FLOWS = 6
+STEP_AT = (0, 0, 8, 12, 14, 15, 16)
+STEP_PIECES = 17
+
+
+def pairing(place, parity):
+    near, far = place + 1 - 2 * (place % 2), (place + 3 - 2 * (place % 2)) % SIDE
+    turn, high, low = (place + 1) // 2 % 2, place // 2, place % 2
+    return ((near, turn), (far, high)) if parity == 0 else ((far, high), (near, low))
+
+
+def sum_kernel(
+    parts, normed, first, last, weight,
+    conv_out, summed,
+    own, other, total, outgoing, incoming, result,
+    tile, wide, held_weight, made, above, below, lefts, rights,
+    halo_send, halo_recv, sends, recvs, local,
+):
+    lat, lon, y, z = position()
+    x, core = lat // 2, lat % 2
+    twin = (lat + 1 - 2 * core, lon)
+    rows, cols, width = tile.shape
+    _, _, up, down, left, right = halo_peers()
+
+    def at_place(axis, place):
+        if axis == 0:
+            return (place * 2 + core, lon)
+        return (lat, place * SIDE + z) if axis == 1 else (lat, y * SIDE + place)
+
+    barrier = pltpu.get_barrier_semaphore()
+    peers = [twin]
+    for axis, place in enumerate((x, y, z)):
+        peers += [at_place(axis, (place + 1) % SIDE), at_place(axis, (place + 3) % SIDE)]
+    peers += [(lat, left), (lat, right)]
+    peers += [(a, b) for a in (up, down) for b in (left, lon, right)]
+    for peer in peers:
+        pl.semaphore_signal(barrier, inc=1, device_id=peer, device_id_type=MESH)
+    load_own = [pltpu.make_async_copy(parts.at[core, f], own.at[f], local.at[f]) for f in range(FLOWS)]
+    load_tile = pltpu.make_async_copy(normed, tile, local.at[FLOWS])
+    load_weight = pltpu.make_async_copy(weight, held_weight, local.at[FLOWS + 1])
+    for copy in (load_tile, *load_own, load_weight):
+        copy.start()
+    pl.semaphore_wait(barrier, len(peers))
+
+    halo = halo_copies(
+        normed.at[0], normed.at[rows - 1], first, last, above, below, lefts, rights, halo_send, halo_recv
+    )
+    for copy in halo:
+        copy.start()
+
+    begun = []
+
+    def remote(src, dst, flow, n, to):
+        copy = pltpu.make_async_remote_copy(
+            src_ref=src, dst_ref=dst, send_sem=sends.at[flow, n], recv_sem=recvs.at[flow, n],
+            device_id=to, device_id_type=MESH,
+        )
+        copy.start()
+        begun.append(copy)
+        return copy
+
+    plans = []
+    for f in range(FLOWS):
+        turn, parity = f // 2, f % 2
+        places = (x, y, z)
+        steps, base = [], 0
+        for k in range(3):
+            axis = (turn + k) % 3
+            for partner, keep in pairing(places[axis], parity):
+                size = PIECES >> (len(steps) + 1)
+                if k < 2:
+                    kept, sent = base + keep * size, base + (1 - keep) * size
+                    base = kept
+                else:
+                    size, kept, sent = 1, base, base
+                steps.append((at_place(axis, partner), size, kept, sent))
+        plans.append(steps)
+
+    crossing = [remote(parts.at[1 - core, f], other.at[f], f, 0, twin) for f in range(FLOWS)]
+
+    load_tile.wait()
+    for copy in halo:
+        copy.wait()
+    lay_windows(tile, above, below, lefts, rights, wide, False)
+    load_weight.wait()
+    step_rows = 4
+    save = [pltpu.make_async_copy(made, conv_out, local.at[FLOWS + 2])]
+
+    def convolve(chunk):
+        value = jnp.zeros((step_rows * cols, width), jnp.float32)
+        for a in range(3):
+            window = wide[chunk * step_rows + a : chunk * step_rows + a + step_rows]
+            value += dot(window.reshape(step_rows * cols, 3 * width), held_weight[a], 1, 0)
+        made[chunk * step_rows : (chunk + 1) * step_rows] = value.astype(jnp.bfloat16).reshape(step_rows, cols, width)
+
+    def send_step(f, k):
+        to, size, _, _ = plans[f][k - 1]
+        at = pl.ds(STEP_AT[k], size)
+        return remote(outgoing.at[f, at], incoming.at[f, at], f, k, to)
+
+    def absorb(f, k):
+        _, size, kept, _ = plans[f][k - 1]
+        _, _, kept_next, sent_next = plans[f][k]
+        half = size // 2
+
+        @pl.loop(0, half)
+        def _(i):
+            total[f, kept_next + i] += incoming[f, STEP_AT[k] + kept_next - kept + i].astype(jnp.float32)
+            value = total[f, sent_next + i] + incoming[f, STEP_AT[k] + sent_next - kept + i].astype(jnp.float32)
+            outgoing[f, STEP_AT[k + 1] + i] = value.astype(jnp.bfloat16)
+
+    convolve(0)
+    flying = []
+    for f in range(FLOWS):
+        _, size, kept, sent = plans[f][0]
+        load_own[f].wait()
+        crossing[f].wait_recv()
+
+        @pl.loop(0, size)
+        def _(i):
+            total[f, kept + i] = own[f, kept + i].astype(jnp.float32) + other[f, kept + i].astype(jnp.float32)
+            value = own[f, sent + i].astype(jnp.float32) + other[f, sent + i].astype(jnp.float32)
+            outgoing[f, i] = value.astype(jnp.bfloat16)
+
+        flying.append(send_step(f, 1))
+    for k in range(1, 4):
+        for chunk in ((), (1, 2, 3), (4,), (5,))[k]:
+            convolve(chunk)
+        if k == 3:
+            save[0].start()
+        for f in range(FLOWS):
+            flying[f].wait_recv()
+            absorb(f, k)
+            flying[f] = send_step(f, k + 1)
+    for f in range(FLOWS):
+        flying[f].wait_recv()
+        value = total[f, plans[f][3][2]] + incoming[f, STEP_AT[4]].astype(jnp.float32)
+        outgoing[f, STEP_AT[5]] = value.astype(jnp.bfloat16)
+        flying[f] = send_step(f, 5)
+    for f in range(FLOWS):
+        flying[f].wait_recv()
+        value = outgoing[f, STEP_AT[5]].astype(jnp.float32) + incoming[f, STEP_AT[5]].astype(jnp.float32)
+        outgoing[f, STEP_AT[6]] = value.astype(jnp.bfloat16)
+        flying[f] = send_step(f, 6)
+
+    n = 7
+    passed = []
+
+    def pass_on(f, start, size, n):
+        at = result.at[core, f, pl.ds(start, size)]
+        passed.append(remote(at, at, f, n, twin))
+
+    for f in range(FLOWS):
+        flying[f].wait_recv()
+        value = outgoing[f, STEP_AT[6]].astype(jnp.float32) + incoming[f, STEP_AT[6]].astype(jnp.float32)
+        base = plans[f][3][2]
+        result[core, f, base] = value.astype(jnp.bfloat16)
+        at = result.at[core, f, pl.ds(base, 1)]
+        flying[f] = remote(at, at, f, n, plans[f][3][0])
+        pass_on(f, base, 1, n + 1)
+    for k in range(4, 0, -1):
+        n += 2
+        for f in range(FLOWS):
+            _, size, kept, sent = plans[f][k - 1]
+            flying[f].wait_recv()
+            if k > 1:
+                to, size_up, kept_up, _ = plans[f][k - 2]
+                at = result.at[core, f, pl.ds(kept_up, size_up)]
+                flying[f] = remote(at, at, f, n, to)
+            pass_on(f, sent, size, n + 1)
+    for copy in passed:
+        copy.wait_recv()
+    stored = pltpu.make_async_copy(result, summed, local.at[FLOWS + 3])
+    stored.start()
+    for copy in begun:
+        copy.wait_send()
+    save[0].wait()
+    stored.wait()
+
+
+def sum_all(parts, normed, first, last, weight):
+    rows, cols, width = normed.shape
+    bf, f32 = jnp.bfloat16, jnp.float32
+    anywhere = pl.BlockSpec(memory_space=pl.ANY)
+    inside = pl.BlockSpec(memory_space=pltpu.VMEM)
+    piece = (PIECE_ROWS, 128)
+    parts = parts.reshape((2, FLOWS, PIECES) + piece)
+    return pl.pallas_call(
+        sum_kernel,
+        name="sum_all",
+        out_shape=(jax.ShapeDtypeStruct(normed.shape, bf), jax.ShapeDtypeStruct(parts.shape, bf)),
+        in_specs=[anywhere, anywhere, inside, inside, anywhere],
+        out_specs=(anywhere, anywhere),
+        scratch_shapes=[
+            pltpu.VMEM((FLOWS, PIECES) + piece, bf),
+            pltpu.VMEM((FLOWS, PIECES) + piece, bf),
+            pltpu.VMEM((FLOWS, PIECES) + piece, f32),
+            pltpu.VMEM((FLOWS, STEP_PIECES) + piece, bf),
+            pltpu.VMEM((FLOWS, STEP_PIECES) + piece, bf),
+            pltpu.VMEM((2, FLOWS, PIECES) + piece, bf),
+            pltpu.VMEM((rows, cols, width), bf),
+            pltpu.VMEM((rows + 2, cols, 3 * width), bf),
+            pltpu.VMEM(weight.shape, bf),
+            pltpu.VMEM((rows, cols, width), bf),
+            pltpu.VMEM((cols, width), bf),
+            pltpu.VMEM((cols, width), bf),
+            pltpu.VMEM((rows + 2, 1, width), f32),
+            pltpu.VMEM((rows + 2, 1, width), f32),
+            pltpu.SemaphoreType.DMA((8,)),
+            pltpu.SemaphoreType.DMA((8,)),
+            pltpu.SemaphoreType.DMA((FLOWS, 17)),
+            pltpu.SemaphoreType.DMA((FLOWS, 17)),
+            pltpu.SemaphoreType.DMA((FLOWS + 4,)),
+        ],
+        compiler_params=pltpu.CompilerParams(
+            collective_id=1, has_side_effects=True, vmem_limit_bytes=VMEM_LIMIT
+        ),
+    )(parts, normed, first, last, weight)
+
+
+def finish_kernel(scale, some, everything, conv_grad, encoder_grad, gain_grad, rest, sem):
+    width = conv_grad.shape[2]
+    lanes = width // 128
+    channels = encoder_grad.shape[0]
+    for n in range(lanes):
+        conv_grad[0, :, n * 128 : (n + 1) * 128] = some[n * width : (n + 1) * width].astype(jnp.float32) * scale
+
+    @pl.when(pl.program_id(0) == 0)
+    def _():
+        copy = pltpu.make_async_copy(everything.at[pl.ds(9 * lanes * width, rest.shape[0])], rest, sem)
+        copy.start()
+        copy.wait()
+        base = channels * lanes
+        for n in range(lanes):
+            at = slice(n * 128, (n + 1) * 128)
+            encoder_grad[:, at] = rest[n * channels : (n + 1) * channels].astype(jnp.float32) * scale
+            eight = rest[base + n * 8 : base + (n + 1) * 8].astype(jnp.float32)
+            gain_grad[:, at] = jnp.sum(eight, axis=0, keepdims=True) * scale
+
+
+def finish(summed, scale, channels, width):
+    f32 = jnp.float32
+    lanes = width // 128
+    return pl.pallas_call(
+        lambda *refs: finish_kernel(scale, *refs),
+        name="finish",
+        grid=(9,),
+        out_shape=(
+            jax.ShapeDtypeStruct((9, width, width), f32),
+            jax.ShapeDtypeStruct((channels, width), f32),
+            jax.ShapeDtypeStruct((1, width), f32),
+        ),
+        in_specs=[pl.BlockSpec((lanes * width, 128), lambda t: (t, 0)), pl.BlockSpec(memory_space=pl.ANY)],
+        out_specs=(
+            pl.BlockSpec((1, width, width), lambda t: (t, 0, 0)),
+            pl.BlockSpec((channels, width), lambda t: (0, 0)),
+            pl.BlockSpec((1, width), lambda t: (0, 0)),
+        ),
+        scratch_shapes=[pltpu.VMEM((channels * lanes + 8 * lanes, 128), jnp.bfloat16), pltpu.SemaphoreType.DMA],
+        compiler_params=pltpu.CompilerParams(vmem_limit_bytes=VMEM_LIMIT),
+    )(summed, summed)
 
 
 def slot_tables(target, patch, kernel, tiles):
@@ -518,21 +765,11 @@
         got_meta.reshape(tiles, 128), send_a, send_b, got_a, got_b, encoder_weight, kernels,
         gain.reshape(1, width), wide, back, part_rows,
     )
-    padded = widen(normed)
-    total = jnp.zeros((rows * cols, width), jnp.float32)
-    for a in range(3):
-        for b in range(3):
-            window = padded[a : a + rows, b : b + cols].reshape(-1, width)
-            total = total + jnp.dot(window, conv_weight[a, b], preferred_element_type=jnp.float32)
-    conv_out = total.reshape(rows, cols, width).astype(jnp.bfloat16)
-    summed = lax.psum(parts.astype(jnp.float32), ("lat", "lon")) * loss_scale
-    base = 9 * width * width // 128
-    lanes = width // 128
-    conv_grad = summed[:base].reshape(9, lanes, width, 128).swapaxes(1, 2).reshape(3, 3, width, width)
-    size = channels * lanes
-    encoder_grad = summed[base : base + size].reshape(lanes, channels, 128).swapaxes(0, 1).reshape(channels, width)
-    gain_grad = summed[base + size : base + size + 8 * lanes].reshape(lanes, 8, 128).sum(axis=1).reshape(width)
-    return conv_out, conv_grad, encoder_grad, gain_grad
+    first = normed[:, :1].astype(jnp.float32)
+    last = normed[:, -1:].astype(jnp.float32)
+    conv_out, summed = sum_all(parts, normed, first, last, conv_weight.reshape(3, 3 * width, width))
+    conv_grad, encoder_grad, gain_grad = finish(summed.reshape(part_rows, 128), loss_scale, channels, width)
+    return conv_out, conv_grad.reshape(3, 3, width, width), encoder_grad, gain_grad.reshape(width)
 
 
 def solution(mesh):

time: 353 us -> 243 us (0.69)
  blocking collectives: 119 us -> 0 us
  Pallas kernels: 148 us -> 225 us
  local copies, waits for them, and re-layouts: 42.8 us -> 9.03 us
  matrix products: 14.1 us -> 0 us
  starting transfers between devices: 11.2 us -> 0 us
  other arithmetic: 14.2 us -> 7.04 us
    psum x1 -> x0, blocking collectives: 119 us -> none  [shards(): summed = lax.psum(parts.astype(jnp.float32), ('lat', 'lon')) * loss_scale]
    pallas_call x0 -> x2, Pallas kernels: none -> 77.3 us  [the longest x1 66.9 us: sum_all(): pl.pallas_call(sum_kernel, name='sum_all', out_shape=(jax.ShapeDtypeStruc...]
    dot_general x9 -> x0, matrix products: 14.1 us -> none  [shards(): jnp.dot(window, conv_weight[a, b], preferred_element_type=jnp.float32)]
    reshape x2 -> x0, local copies, waits for them, and re-layouts: 13.5 us -> none  [the longest x1 12.3 us: shards(): summed[:base].reshape(9, lanes, width, 128).swapaxes(1, 2)]
    transpose x1 -> x0, local copies, waits for them, and re-layouts: 13.3 us -> none  [shards(): summed[:base].reshape(9, lanes, width, 128).swapaxes(1, 2)]
    ppermute x4 -> x0, starting transfers between devices: 11.2 us -> none  [the longest x2 5.64 us: padded_2(): after = lax.ppermute(leading, axis, down)]
    slice x6 -> x0, local copies, waits for them, and re-layouts: 7.23 us -> none  [the longest x1 3.94 us: shards(): summed[:base].reshape(9, lanes, width, 128).swapaxes(1, 2)]
    mul x1 -> x0, other arithmetic: 5.04 us -> none  [shards(): summed = lax.psum(parts.astype(jnp.float32), ('lat', 'lon')) * loss_scale]
  transfers between devices with their start and end apart: 4 -> 0, of which waited for: 1 -> 0; matrix products, arithmetic and copies ran while one was open for 12% -> 0% of each run, Pallas kernels for 0% -> 0%
where the time goes in v2:
time: 243 us; the launch traced here: 242 us
  Pallas kernels  225 us (93%)
  local copies, waits for them, and re-layouts  9.03 us (4%)
  other arithmetic  7.04 us (3%)
    pallas_call x1, Pallas kernels, exchange(): pl.pallas_call(exchange_kernel, name='exchange', out_shape=(whole, whole,...  95.6 us
    pallas_call x1, Pallas kernels, sum_all(): pl.pallas_call(sum_kernel, name='sum_all', out_shape=(jax.ShapeDtypeStruc...  66.9 us
    pallas_call x1, Pallas kernels, middle(): pl.pallas_call(middle_kernel, name='middle', out_shape=(jax.ShapeDtypeStr...  45.5 us
    pallas_call x1, Pallas kernels, finish(): pl.pallas_call(lambda *refs: finish_kernel(scale, *refs), name='finish',...  10.4 us
    unnamed x7, local copies, waits for them, and re-layouts  8.26 us
    pallas_call x1, Pallas kernels, pack(): pl.pallas_call(pack_kernel, name='pack', out_shape=(out, out), in_specs=[...  6.8 us

profile of v2, /device:TPU:1, one launch (start us, length us, event | category | flops | bytes accessed | tf_op | source)
XLA Modules:
  0.0 241.9 jit_solution(4428885310263981127)
XLA Ops:
  0.6 0.9 convert_reduce_fusion
  1.5 0.7 multiply_add_fusion
  2.2 0.7 broadcast_add_fusion.2
  2.9 0.7 broadcast_add_fusion.3
  3.5 0.1 select_reduce_fusion.1
  3.6 0.1 max.12
  3.7 0.1 sub.13
  3.8 0.1 pad_add_fusion
  3.9 0.6 pad.4
  4.5 0.5 broadcast_add_fusion.1.source_ref
  5.0 6.1 %copy.17 = bf16[3072,616]{1,0:T(8,128)(2,1)} copy(bf16[3072,616]{0,1:T(8,128)(2,1)} %param.9) | data formatting | bytes 7569408 | tf_op args[0]
  11.1 6.8 %pack.1 = (bf16[4,4,3,64,616]{4,3,2,1,0:T(8,128)(2,1)}, bf16[4,4,3,64,616]{4,3,2,1,0:T(8,128)(2,1)}) custom-call(s32[48]{0:T(128)} %broadcast_add_fusion.1.source_ref, bf16[24,128,616]{2,1,0:T(8,128)(2,1)} %bitcast.15), custom_call_target="tpu_custom_call" | custom-call | tf_op jit(solution)/shard_map/pack/pallas_call | solution.py:65
  17.9 1.7 slice_convert_fusion.2
  19.6 0.0 copy-start
  19.6 95.6 %exchange.1 = (bf16[4,4,3,64,616]{4,3,2,1,0:T(8,128)(2,1)}, bf16[4,4,3,64,616]{4,3,2,1,0:T(8,128)(2,1)}, s32[16,1,128]{2,1,0:T(1,128)}, bf16[26,64,1536]{2,1,0:T...) custom-call(bf16[4,4,3,64,616]{4,3,2,1,0:T(8,128)(2,1)} %get-tuple-e, ...), custom_call_target="tpu_custom_call" | custom-call | tf_op jit(solution)/shard_map/exchange/pallas_call | solution.py:305
  115.2 0.0 copy-done
  115.2 1.0 copy.18
  116.2 45.5 %middle.1 = (bf16[24,64,512]{2,1,0:T(8,128)(2,1)}, bf16[21504,128]{1,0:T(8,128)(2,1)}) custom-call(s32[16,128]{1,0:T(8,128)} %bitcast.19, bf16[4,4,3,64,616]{4,3,2,1,0:T(8,128)(2,1)} %get-tuple-element.18.send_a.own_a, bf16[4,4,3,64,616]{4,3,2,1,0:T(8,128)(2,1)} %get-tuple-element.19.send_b.own_b, bf16[4,4,3,64,616]{4,3,2,1,0:T(8,128)(2,1)} %get-tuple-element.21.got_a, ...), custom_call_target="tpu_custom_call" | custom-call | tf_op jit(solution)/shard_map/middle/pallas_call | solution.py:447
  161.7 1.7 slice_convert_fusion
  163.5 66.9 %sum_all.1 = (bf16[24,64,512]{2,1,0:T(8,128)(2,1)}, bf16[2,6,16,112,128]{4,3,2,1,0:T(8,128)(2,1)}) custom-call(bf16[2,6,16,112,128]{4,3,2,1,0:T(8,128)(2,1)} %bitcast.16, bf16[24,64,512]{2,1,0:T(8,128)(2,1)} %get-tuple-element.26.normed, f32[24,1,512]{2,1,0:T(1,128)} %get-tuple-element.36.first, f32[24,1,512]{2,1,0:T(1,128)} %get-tuple-element.35.last, ...), custom_call_target="tpu_custom_call" | custom-call | tf_op jit(solution)/shard_map/sum_all/pallas_call | solution.py:661
  230.4 0.0 copy-start.1
  230.4 10.4 %finish.1 = (f32[9,512,512]{2,1,0:T(8,128)}, f32[616,512]{1,0:T(8,128)}, f32[1,512]{1,0:T(1,128)}) custom-call(bf16[21504,128]{1,0:T(8,128)(2,1)} %bitcast.11, bf16[21504,128]{1,0:T(8,128)(2,1)} %bitcast.12), custom_call_target="tpu_custom_call" | custom-call | tf_op jit(solution)/shard_map/finish/pallas_call | solution.py:717
  240.8 0.0 copy-done.1
  240.8 1.1 copy.20
  (2 shorter events, 0.0 us)
Async XLA Ops:
  19.6 95.6 %copy-start = (bf16[16,128,128]{2,1,0:T(8,128)(2,1)S(1)}, bf16[16,128,128]{2,1,0:T(8,128)(2,1)}, u32[]{:S(2)}) copy-start(bf16[16,128,128]{2,1,0:T(8,128)(2,1)} %kernels.1) | copy-start | bytes 1572868
  230.4 10.4 %copy-start.1 = (bf16[24,64,512]{2,1,0:T(8,128)(2,1)S(1)}, bf16[24,64,512]{2,1,0:T(8,128)(2,1)}, u32[]{:S(2)}) copy-start(bf16[24,64,512]{2,1,0:T(8,128)(2,1)} %get-tuple-element.45) | copy-start | bytes 4718596

commit v3 on v2

--- a/solution.py
+++ b/solution.py
@@ -21,7 +21,8 @@
 
 def pack_kernel(source_ref, spectra, to_a, to_b, held, blank, in_sem, out_sems):
     slots = source_ref.shape[0]
-    rows = held.shape[1] // 2
+    high, block = to_a.shape[3:]
+    low = to_b.shape[3]
     fetch = pltpu.make_async_copy(spectra, held, in_sem)
     fetch.start()
     blank[...] = jnp.zeros_like(blank)
@@ -32,50 +33,51 @@
         rank = slot - tile * MOST
         y, z = tile // SIDE, tile % SIDE
         return (
-            pltpu.make_async_copy(source(0), to_a.at[z, y, rank], out_sems.at[slot, 0]),
-            pltpu.make_async_copy(source(1), to_b.at[y, z, rank], out_sems.at[slot, 1]),
+            pltpu.make_async_copy(source(0, high), to_a.at[z, y, rank], out_sems.at[slot, 0]),
+            pltpu.make_async_copy(source(high, low), to_b.at[y, z, rank], out_sems.at[slot, 1]),
         )
 
     @pl.loop(0, slots)
     def _(slot):
-        block = source_ref[slot]
-
-        @pl.when(block >= 0)
+        which = source_ref[slot]
+
+        @pl.when(which >= 0)
         def _():
-            for piece in pieces(slot, lambda half: held.at[block, pl.ds(half * rows, rows)]):
+            lanes = pl.ds(pl.multiple_of(which * block, block), block)
+            for piece in pieces(slot, lambda base, size: held.at[pl.ds(base, size), lanes]):
                 piece.start()
 
-        @pl.when(block < 0)
+        @pl.when(which < 0)
         def _():
-            for piece in pieces(slot, lambda half: blank):
+            for piece in pieces(slot, lambda base, size: blank.at[pl.ds(0, size)]):
                 piece.start()
 
     @pl.loop(0, slots)
     def _(slot):
-        for piece in pieces(slot, lambda half: blank):
+        for piece in pieces(slot, lambda base, size: blank.at[pl.ds(0, size)]):
             piece.wait()
 
 
-def pack(source_block, spectra, block_rows):
-    blocks = spectra.shape[0] // block_rows
-    channels = spectra.shape[1]
-    half = block_rows // 2
+def pack(source_block, flipped_spectra, block):
+    channels = flipped_spectra.shape[0]
+    high = channels // 32 * 16
+    low = channels - high
     slots = source_block.shape[0]
-    out = jax.ShapeDtypeStruct((SIDE, SIDE, MOST, half, channels), jnp.bfloat16)
+    outs = [jax.ShapeDtypeStruct((SIDE, SIDE, MOST, size, block), jnp.bfloat16) for size in (high, low)]
     return pl.pallas_call(
         pack_kernel,
         name="pack",
-        out_shape=(out, out),
+        out_shape=outs,
         in_specs=[pl.BlockSpec(memory_space=pltpu.SMEM), pl.BlockSpec(memory_space=pl.ANY)],
         out_specs=(pl.BlockSpec(memory_space=pl.ANY),) * 2,
         scratch_shapes=[
-            pltpu.VMEM((blocks, block_rows, channels), jnp.bfloat16),
-            pltpu.VMEM((half, channels), jnp.bfloat16),
+            pltpu.VMEM(flipped_spectra.shape, jnp.bfloat16),
+            pltpu.VMEM((max(high, low), block), jnp.bfloat16),
             pltpu.SemaphoreType.DMA,
             pltpu.SemaphoreType.DMA((slots, 2)),
         ],
         compiler_params=pltpu.CompilerParams(vmem_limit_bytes=VMEM_LIMIT),
-    )(source_block, spectra.reshape(blocks, block_rows, channels))
+    )(source_block, flipped_spectra)
 
 
 def position():
@@ -296,19 +298,18 @@
 
 def exchange(send_a, send_b, meta, cotangent, first, last, weight):
     rows, cols, width = cotangent.shape
-    slot = send_a.shape[2:]
     lon = SIDE * SIDE
     bf, f32 = jnp.bfloat16, jnp.float32
     anywhere = pl.BlockSpec(memory_space=pl.ANY)
-    whole = jax.ShapeDtypeStruct((SIDE, SIDE) + slot, bf)
-    relay = jax.ShapeDtypeStruct((2, 2, 2) + slot, bf)
+    whole = [jax.ShapeDtypeStruct(a.shape, bf) for a in (send_a, send_b)]
+    relay = [jax.ShapeDtypeStruct((2, 2, 2) + a.shape[2:], bf) for a in (send_a, send_b)]
     out = pl.pallas_call(
         exchange_kernel,
         name="exchange",
         out_shape=(
-            whole, whole, jax.ShapeDtypeStruct(meta.shape, meta.dtype),
+            *whole, jax.ShapeDtypeStruct(meta.shape, meta.dtype),
             jax.ShapeDtypeStruct((rows + 2, cols, 3 * width), bf), jax.ShapeDtypeStruct((rows, cols, width), f32),
-            whole, whole, relay, relay,
+            *whole, *relay,
         ),
         in_specs=[anywhere] * 7,
         out_specs=(anywhere,) * 9,
@@ -338,24 +339,31 @@
 
 def middle_kernel(
     meta, own_a, own_b, got_a, got_b, encoder, kernels, turned, gain, wide_in, back_in,
-    normed, parts,
+    normed, first, last, parts,
     x, slope, encoded, spread, d_spread, wide, back, flipped, d_rows, encoder_sum, gain_sum,
     x_sems, local,
 ):
     lat, lon, y, z = position()
     rows, cols, width = normed.shape
-    channels = encoder.shape[0]
+    channels = encoder.shape[1]
+    high = own_a.shape[3]
     sources = SIDE * SIDE
     block = kernels.shape[1]
-    copies = []
+
+    def fetch(n, rank, from_a, from_b):
+        lanes = pl.ds(rank * block, block)
+        return (
+            pltpu.make_async_copy(from_a.at[rank], x.at[n, pl.ds(0, high), lanes], x_sems.at[n, rank, 0]),
+            pltpu.make_async_copy(from_b.at[rank], x.at[n, pl.ds(high, channels - high), lanes], x_sems.at[n, rank, 1]),
+        )
+
     for n in range(sources):
         dy, dz = n // SIDE, n % SIDE
         from_a = own_a.at[z, y] if n == 0 else got_a.at[dy, dz]
         from_b = own_b.at[y, z] if n == 0 else got_b.at[dz, dy]
-        copies.append(pltpu.make_async_copy(from_a, x.at[n, :, 0], x_sems.at[n, 0]))
-        copies.append(pltpu.make_async_copy(from_b, x.at[n, :, 1], x_sems.at[n, 1]))
-    for copy in copies:
-        copy.start()
+        for rank in range(MOST):
+            for copy in fetch(n, rank, from_a, from_b):
+                copy.start()
     load_back = pltpu.make_async_copy(back_in, back, local.at[0])
     load_wide = pltpu.make_async_copy(wide_in, wide, local.at[1])
     load_back.start()
@@ -364,18 +372,19 @@
 
     @pl.loop(0, sources)
     def _(n):
-        for half in range(2):
-            pltpu.make_async_copy(got_a.at[0, 0], x.at[n, :, half], x_sems.at[n, half]).wait()
-        pre = dot(x[n].reshape(MOST * block, channels), encoder[...], 1, 0)
+        for rank in range(MOST):
+            for copy in fetch(n, rank, got_a.at[0, 0], got_b.at[0, 0]):
+                copy.wait()
+        pre = dot(encoder[...], x[n], 1, 0)
         logistic = 0.5 * jnp.tanh(0.5 * pre) + 0.5
         encoded[...] = (pre * logistic).astype(jnp.bfloat16)
-        slope[n] = (logistic * (1.0 + pre * (1.0 - logistic))).astype(jnp.bfloat16)
+        slope[n] = logistic * (1.0 + pre * (1.0 - logistic))
         for rank in range(MOST):
             which, patch = meta[n, rank], meta[n, MOST + rank]
 
             @pl.when(which >= 0)
             def _():
-                spread[patch] += dot(turned[which], encoded[rank * block : (rank + 1) * block], 1, 0)
+                spread[patch] += dot(turned[which], encoded[:, rank * block : (rank + 1) * block], 1, 1)
 
     load_back.wait()
     gain_sum[...] = jnp.zeros_like(gain_sum)
@@ -393,7 +402,7 @@
         product = given * unit
         gain_sum[...] += jnp.sum(product.reshape(PH * PW // 8, 8, width), axis=0)
         inner = jnp.mean(product * weight, axis=1, keepdims=True)
-        d_spread[q] = (scale * (given * weight - unit * inner)).astype(jnp.bfloat16)
+        d_spread[q] = (scale * (given * weight - unit * inner)).astype(jnp.bfloat16).T
 
     step_rows = 4
 
@@ -401,6 +410,12 @@
     def _(n):
         some = normed[pl.ds(n * step_rows, step_rows)].reshape(step_rows * cols, width)
         flipped[:, pl.ds(pl.multiple_of(n * step_rows * cols, 128), step_rows * cols)] = some.T
+
+    @pl.loop(0, rows)
+    def _(row):
+        some = normed[row].astype(jnp.float32)
+        first[row] = some[:1]
+        last[row] = some[cols - 1 :]
 
     load_wide.wait()
     for a in range(3):
@@ -419,10 +434,10 @@
     def _(n):
         for rank in range(MOST):
             which, patch = jnp.maximum(meta[n, rank], 0), meta[n, MOST + rank]
-            at = slice(rank * block, (rank + 1) * block)
-            here = dot(kernels[which], d_spread[patch], 1, 0).astype(jnp.bfloat16).astype(jnp.float32)
-            d_rows[at] = (here * slope[n, at].astype(jnp.float32)).astype(jnp.bfloat16)
-        encoder_sum[...] += dot(x[n].reshape(MOST * block, channels), d_rows[...], 0, 0)
+            lanes = slice(rank * block, (rank + 1) * block)
+            here = dot(d_spread[patch], turned[which], 1, 0).astype(jnp.bfloat16).astype(jnp.float32)
+            d_rows[:, lanes] = (here * slope[n, :, lanes]).astype(jnp.bfloat16)
+        encoder_sum[...] += dot(x[n], d_rows[...], 1, 1)
 
     base = 9 * width * width // 128
     for n in range(width // 128):
@@ -444,36 +459,39 @@
     bf, f32 = jnp.bfloat16, jnp.float32
     anywhere = pl.BlockSpec(memory_space=pl.ANY)
     local = pl.BlockSpec(memory_space=pltpu.VMEM)
+    column = jax.ShapeDtypeStruct((rows, 1, width), f32)
     return pl.pallas_call(
         middle_kernel,
         name="middle",
-        out_shape=(jax.ShapeDtypeStruct((rows, cols, width), bf), jax.ShapeDtypeStruct((part_rows, 128), bf)),
+        out_shape=(
+            jax.ShapeDtypeStruct((rows, cols, width), bf), column, column, jax.ShapeDtypeStruct((part_rows, 128), bf)
+        ),
         in_specs=[pl.BlockSpec(memory_space=pltpu.SMEM)] + [anywhere] * 4 + [local] * 4 + [anywhere] * 2,
-        out_specs=(local, local),
+        out_specs=(local,) * 4,
         scratch_shapes=[
-            pltpu.VMEM((sources, MOST, 2, block // 2, channels), bf),
-            pltpu.VMEM((sources, MOST * block, width), bf),
-            pltpu.VMEM((MOST * block, width), bf),
+            pltpu.VMEM((sources, channels, MOST * block), bf),
+            pltpu.VMEM((sources, width, MOST * block), f32),
+            pltpu.VMEM((width, MOST * block), bf),
             pltpu.VMEM((patches, cells, width), f32),
-            pltpu.VMEM((patches, cells, width), bf),
+            pltpu.VMEM((patches, width, cells), bf),
             pltpu.VMEM(wide.shape, bf),
             pltpu.VMEM(back.shape, f32),
             pltpu.VMEM((width, rows * cols), bf),
-            pltpu.VMEM((MOST * block, width), bf),
+            pltpu.VMEM((width, MOST * block), bf),
             pltpu.VMEM((channels, width), f32),
             pltpu.VMEM((8, width), f32),
-            pltpu.SemaphoreType.DMA((sources, 2)),
+            pltpu.SemaphoreType.DMA((sources, MOST, 2)),
             pltpu.SemaphoreType.DMA((2,)),
         ],
         compiler_params=pltpu.CompilerParams(vmem_limit_bytes=VMEM_LIMIT),
-    )(meta, own_a, own_b, got_a, got_b, encoder, kernels, kernels.swapaxes(1, 2), gain, wide, back)
+    )(meta, own_a, own_b, got_a, got_b, encoder.T, kernels, kernels.swapaxes(1, 2), gain, wide, back)
 
 
 PIECES = 16
 PIECE_ROWS = 112
 FLOWS = 6
-STEP_AT = (0, 0, 8, 12, 14, 15, 16)
-STEP_PIECES = 17
+STEP_AT = (0, 0, 8, 0, 2, 3, 4)
+EARLY_PIECES, LATE_PIECES = 12, 5
 
 
 def pairing(place, parity):
@@ -485,7 +503,7 @@
 def sum_kernel(
     parts, normed, first, last, weight,
     conv_out, summed,
-    own, other, total, outgoing, incoming, result,
+    own, other, total, early_out, early_in, late_out, late_in, result,
     tile, wide, held_weight, made, above, below, lefts, rights,
     halo_send, halo_recv, sends, recvs, local,
 ):
@@ -566,21 +584,28 @@
             value += dot(window.reshape(step_rows * cols, 3 * width), held_weight[a], 1, 0)
         made[chunk * step_rows : (chunk + 1) * step_rows] = value.astype(jnp.bfloat16).reshape(step_rows, cols, width)
 
+    def leaving(k):
+        return early_out if k < 3 else late_out
+
+    def arriving(k):
+        return early_in if k < 3 else late_in
+
     def send_step(f, k):
         to, size, _, _ = plans[f][k - 1]
         at = pl.ds(STEP_AT[k], size)
-        return remote(outgoing.at[f, at], incoming.at[f, at], f, k, to)
+        return remote(leaving(k).at[f, at], arriving(k).at[f, at], f, k, to)
 
     def absorb(f, k):
         _, size, kept, _ = plans[f][k - 1]
         _, _, kept_next, sent_next = plans[f][k]
         half = size // 2
+        incoming, outgoing = arriving(k), leaving(k + 1)
 
         @pl.loop(0, half)
         def _(i):
             total[f, kept_next + i] += incoming[f, STEP_AT[k] + kept_next - kept + i].astype(jnp.float32)
             value = total[f, sent_next + i] + incoming[f, STEP_AT[k] + sent_next - kept + i].astype(jnp.float32)
-            outgoing[f, STEP_AT[k + 1] + i] = value.astype(jnp.bfloat16)
+            outgoing[f, STEP_AT[k + 1] + i] = value.astype(outgoing.dtype)
 
     convolve(0)
     flying = []
@@ -593,7 +618,7 @@
         def _(i):
             total[f, kept + i] = own[f, kept + i].astype(jnp.float32) + other[f, kept + i].astype(jnp.float32)
             value = own[f, sent + i].astype(jnp.float32) + other[f, sent + i].astype(jnp.float32)
-            outgoing[f, i] = value.astype(jnp.bfloat16)
+            early_out[f, i] = value.astype(jnp.bfloat16)
 
         flying.append(send_step(f, 1))
     for k in range(1, 4):
@@ -607,13 +632,11 @@
             flying[f] = send_step(f, k + 1)
     for f in range(FLOWS):
         flying[f].wait_recv()
-        value = total[f, plans[f][3][2]] + incoming[f, STEP_AT[4]].astype(jnp.float32)
-        outgoing[f, STEP_AT[5]] = value.astype(jnp.bfloat16)
+        late_out[f, STEP_AT[5]] = total[f, plans[f][3][2]] + late_in[f, STEP_AT[4]]
         flying[f] = send_step(f, 5)
     for f in range(FLOWS):
         flying[f].wait_recv()
-        value = outgoing[f, STEP_AT[5]].astype(jnp.float32) + incoming[f, STEP_AT[5]].astype(jnp.float32)
-        outgoing[f, STEP_AT[6]] = value.astype(jnp.bfloat16)
+        late_out[f, STEP_AT[6]] = late_out[f, STEP_AT[5]] + late_in[f, STEP_AT[5]]
         flying[f] = send_step(f, 6)
 
     n = 7
@@ -625,7 +648,7 @@
 
     for f in range(FLOWS):
         flying[f].wait_recv()
-        value = outgoing[f, STEP_AT[6]].astype(jnp.float32) + incoming[f, STEP_AT[6]].astype(jnp.float32)
+        value = late_out[f, STEP_AT[6]] + late_in[f, STEP_AT[6]]
         base = plans[f][3][2]
         result[core, f, base] = value.astype(jnp.bfloat16)
         at = result.at[core, f, pl.ds(base, 1)]
@@ -668,8 +691,10 @@
             pltpu.VMEM((FLOWS, PIECES) + piece, bf),
             pltpu.VMEM((FLOWS, PIECES) + piece, bf),
             pltpu.VMEM((FLOWS, PIECES) + piece, f32),
-            pltpu.VMEM((FLOWS, STEP_PIECES) + piece, bf),
-            pltpu.VMEM((FLOWS, STEP_PIECES) + piece, bf),
+            pltpu.VMEM((FLOWS, EARLY_PIECES) + piece, bf),
+            pltpu.VMEM((FLOWS, EARLY_PIECES) + piece, bf),
+            pltpu.VMEM((FLOWS, LATE_PIECES) + piece, f32),
+            pltpu.VMEM((FLOWS, LATE_PIECES) + piece, f32),
             pltpu.VMEM((2, FLOWS, PIECES) + piece, bf),
             pltpu.VMEM((rows, cols, width), bf),
             pltpu.VMEM((rows + 2, cols, 3 * width), bf),
@@ -755,18 +780,16 @@
     channels = spectra.shape[1]
     loss_scale = 1.0 / math.sqrt(rows * bands * cols * tiles)
     source, meta = slot_tables(target, patch, kernel, tiles)
-    send_a, send_b = pack(source, spectra, kernels.shape[1])
+    send_a, send_b = pack(source, spectra.T, kernels.shape[1])
     first = cotangent[:, :1].astype(jnp.float32)
     last = cotangent[:, -1:].astype(jnp.float32)
     weight = conv_weight.reshape(9, width, width)
     got_a, got_b, got_meta, wide, back = exchange(send_a, send_b, meta, cotangent, first, last, weight)
     part_rows = 192 * 112
-    normed, parts = middle(
+    normed, first, last, parts = middle(
         got_meta.reshape(tiles, 128), send_a, send_b, got_a, got_b, encoder_weight, kernels,
         gain.reshape(1, width), wide, back, part_rows,
     )
-    first = normed[:, :1].astype(jnp.float32)
-    last = normed[:, -1:].astype(jnp.float32)
     conv_out, summed = sum_all(parts, normed, first, last, conv_weight.reshape(3, 3 * width, width))
     conv_grad, encoder_grad, gain_grad = finish(summed.reshape(part_rows, 128), loss_scale, channels, width)
     return conv_out, conv_grad.reshape(3, 3, width, width), encoder_grad, gain_grad.reshape(width)

time: 243 us -> 239 us (0.984)
  local copies, waits for them, and re-layouts: 9.03 us -> 4.03 us
  Pallas kernels: 225 us -> 228 us
    unnamed x7 -> x9, local copies, waits for them, and re-layouts: 8.26 us -> 3.25 us
    pallas_call x1, Pallas kernels: 45.5 us -> 49.1 us  [middle(): pl.pallas_call(middle_kernel, name='middle', out_shape=(jax.ShapeDtypeStr...]
    pallas_call x2, Pallas kernels: 102 us -> 99.1 us  [the longest x1 92.4 us: exchange(): pl.pallas_call(exchange_kernel, name='exchange', out_shape=(*whole, jax.S...]
    pallas_call x1, Pallas kernels: 66.9 us -> 69.7 us  [sum_all(): pl.pallas_call(sum_kernel, name='sum_all', out_shape=(jax.ShapeDtypeStruc...]
where the time goes in v3:
time: 239 us; the launch traced here: 238 us
  Pallas kernels  228 us (95%)
  other arithmetic  5.31 us (2%)
  local copies, waits for them, and re-layouts  4.03 us (2%)
    pallas_call x1, Pallas kernels, exchange(): pl.pallas_call(exchange_kernel, name='exchange', out_shape=(*whole, jax.S...  92.4 us
    pallas_call x1, Pallas kernels, sum_all(): pl.pallas_call(sum_kernel, name='sum_all', out_shape=(jax.ShapeDtypeStruc...  69.7 us
    pallas_call x1, Pallas kernels, middle(): pl.pallas_call(middle_kernel, name='middle', out_shape=(jax.ShapeDtypeStr...  49.1 us
    pallas_call x1, Pallas kernels, finish(): pl.pallas_call(lambda *refs: finish_kernel(scale, *refs), name='finish',...  10.4 us
    pallas_call x1, Pallas kernels, pack(): pl.pallas_call(pack_kernel, name='pack', out_shape=outs, in_specs=[pl.Blo...  6.61 us

profile of v3, /device:TPU:1, one launch (start us, length us, event | category | flops | bytes accessed | tf_op | source)
XLA Modules:
  0.0 238.3 jit_solution(15163912799372443682)
XLA Ops:
  0.6 0.9 convert_reduce_fusion
  1.5 0.7 multiply_add_fusion
  2.2 0.7 broadcast_add_fusion.2
  2.9 0.7 broadcast_add_fusion.3
  3.5 0.1 select_reduce_fusion.1
  3.6 0.1 max.12
  3.7 0.1 sub.13
  3.8 0.1 pad_add_fusion
  3.9 0.6 pad.4
  4.5 0.5 broadcast_add_fusion.1.source_ref
  5.0 6.6 %pack.1 = (bf16[4,4,3,304,128]{4,3,2,1,0:T(8,128)(2,1)}, bf16[4,4,3,312,128]{4,3,2,1,0:T(8,128)(2,1)}) custom-call(s32[48]{0:T(128)} %broadcast_add_fusion.1.source_ref, bf16[616,3072]{1,0:T(8,128)(2,1)} %bitcast.17), custom_call_target="tpu_custom_call" | custom-call | tf_op jit(solution)/shard_map/pack/pallas_call | solution.py:67
  11.6 1.7 slice_convert_fusion
  13.4 0.0 copy-start.2
  13.4 0.0 copy-start
  13.4 92.4 %exchange.1 = (bf16[4,4,3,304,128]{4,3,2,1,0:T(8,128)(2,1)}, bf16[4,4,3,312,128]{4,3,2,1,0:T(8,128)(2,1)}, s32[16,1,128]{2,1,0:T(1,128)}, bf16[26,64,1536]{2,1,0...) custom-call(bf16[4,4,3,304,128]{4,3,2,1,0:T(8,128)(2,1)} %get-tuple-, ...), custom_call_target="tpu_custom_call" | custom-call | tf_op jit(solution)/shard_map/exchange/pallas_call | solution.py:306
  105.8 0.0 copy-done.2
  105.8 1.1 copy.17
  106.9 0.0 copy-done
  106.9 1.0 copy.18
  107.9 49.1 %middle.1 = (bf16[24,64,512]{2,1,0:T(8,128)(2,1)}, f32[24,1,512]{2,1,0:T(1,128)}, f32[24,1,512]{2,1,0:T(1,128)}, bf16[21504,128]{1,0:T(8,128)(2,1)}) custom-call(s32[16,128]{1,0:T(8,128)} %bitcast.21, bf16[4,4,3,304,128]{4,3,2,1,0:T(8,128)(2,1)} %get-tuple-element.20.send_a.own_a, bf16[4,4,3,312,128]{4,3,2,1,0:T(8,128)(2,1)} %get-tuple-element.21.send_b.own_b, ...), custom_call_target="tpu_custom_call" | custom-call | tf_op jit(solution)/shard_map/middle/pallas_call | solution.py:463
  157.0 69.7 %sum_all.1 = (bf16[24,64,512]{2,1,0:T(8,128)(2,1)}, bf16[2,6,16,112,128]{4,3,2,1,0:T(8,128)(2,1)}) custom-call(bf16[2,6,16,112,128]{4,3,2,1,0:T(8,128)(2,1)} %bitcast.16, bf16[24,64,512]{2,1,0:T(8,128)(2,1)} %get-tuple-element.28.normed, f32[24,1,512]{2,1,0:T(1,128)} %get-tuple-element.29.first, f32[24,1,512]{2,1,0:T(1,128)} %get-tuple-element.30.last, ...), custom_call_target="tpu_custom_call" | custom-call | tf_op jit(solution)/shard_map/sum_all/pallas_call | solution.py:684
  226.8 0.0 copy-start.1
  226.8 10.4 %finish.1 = (f32[9,512,512]{2,1,0:T(8,128)}, f32[616,512]{1,0:T(8,128)}, f32[1,512]{1,0:T(1,128)}) custom-call(bf16[21504,128]{1,0:T(8,128)(2,1)} %bitcast.12, bf16[21504,128]{1,0:T(8,128)(2,1)} %bitcast.13), custom_call_target="tpu_custom_call" | custom-call | tf_op jit(solution)/shard_map/finish/pallas_call | solution.py:742
  237.2 0.0 copy-done.1
  237.2 1.1 copy.20
  (2 shorter events, 0.0 us)
Async XLA Ops:
  13.4 92.5 %copy-start.2 = (bf16[616,512]{1,0:T(8,128)(2,1)S(1)}, bf16[616,512]{1,0:T(8,128)(2,1)}, u32[]{:S(2)}) copy-start(bf16[616,512]{1,0:T(8,128)(2,1)} %param.13) | copy-start | bytes 1892356
  13.4 93.5 %copy-start = (bf16[16,128,128]{2,1,0:T(8,128)(2,1)S(1)}, bf16[16,128,128]{2,1,0:T(8,128)(2,1)}, u32[]{:S(2)}) copy-start(bf16[16,128,128]{2,1,0:T(8,128)(2,1)} %kernels.1) | copy-start | bytes 1572868
  226.8 10.4 %copy-start.1 = (bf16[24,64,512]{2,1,0:T(8,128)(2,1)S(1)}, bf16[24,64,512]{2,1,0:T(8,128)(2,1)}, u32[]{:S(2)}) copy-start(bf16[24,64,512]{2,1,0:T(8,128)(2,1)} %get-tuple-element.47) | copy-start | bytes 4718596

commit v4 on v3

--- a/solution.py
+++ b/solution.py
@@ -19,13 +19,41 @@
     return lax.dot_general(a, b, (((ca,), (cb,)), ((), ())), preferred_element_type=jnp.float32)
 
 
-def pack_kernel(source_ref, spectra, to_a, to_b, held, blank, in_sem, out_sems):
-    slots = source_ref.shape[0]
+def pack_kernel(
+    target, patch, kernel, spectra, cot, to_a, to_b, meta, first, last,
+    held, blank, near, far, block_in, counts, in_sems, out_sems,
+):
+    slots = block_in.shape[0]
     high, block = to_a.shape[3:]
     low = to_b.shape[3]
-    fetch = pltpu.make_async_copy(spectra, held, in_sem)
+    rows, cols, _ = cot.shape
+    fetch = pltpu.make_async_copy(spectra, held, in_sems.at[0])
     fetch.start()
+    edges = [
+        pltpu.make_async_copy(cot.at[:, pl.ds(0, 8)], near, in_sems.at[1]),
+        pltpu.make_async_copy(cot.at[:, pl.ds(cols - 8, 8)], far, in_sems.at[2]),
+    ]
+    for edge in edges:
+        edge.start()
     blank[...] = jnp.zeros_like(blank)
+
+    @pl.loop(0, slots // MOST)
+    def _(tile):
+        counts[tile] = 0
+        for rank in range(MOST):
+            block_in[tile * MOST + rank] = -1
+            meta[tile, rank] = -1
+            meta[tile, MOST + rank] = 0
+
+    @pl.loop(0, target.shape[0])
+    def _(which):
+        tile = target[which]
+        rank = counts[tile]
+        counts[tile] = rank + 1
+        block_in[tile * MOST + rank] = which
+        meta[tile, rank] = kernel[which]
+        meta[tile, MOST + rank] = patch[which]
+
     fetch.wait()
 
     def pieces(slot, source):
@@ -39,7 +67,7 @@
 
     @pl.loop(0, slots)
     def _(slot):
-        which = source_ref[slot]
+        which = block_in[slot]
 
         @pl.when(which >= 0)
         def _():
@@ -52,32 +80,51 @@
             for piece in pieces(slot, lambda base, size: blank.at[pl.ds(0, size)]):
                 piece.start()
 
+    for edge in edges:
+        edge.wait()
+
+    @pl.loop(0, rows)
+    def _(row):
+        first[row] = near[row].astype(jnp.float32)[:1]
+        last[row] = far[row].astype(jnp.float32)[7:]
+
     @pl.loop(0, slots)
     def _(slot):
         for piece in pieces(slot, lambda base, size: blank.at[pl.ds(0, size)]):
             piece.wait()
 
 
-def pack(source_block, flipped_spectra, block):
+def pack(target, patch, kernel, flipped_spectra, cotangent, block, tiles):
     channels = flipped_spectra.shape[0]
+    rows, _, width = cotangent.shape
     high = channels // 32 * 16
     low = channels - high
-    slots = source_block.shape[0]
-    outs = [jax.ShapeDtypeStruct((SIDE, SIDE, MOST, size, block), jnp.bfloat16) for size in (high, low)]
+    slots = tiles * MOST
+    bf, f32 = jnp.bfloat16, jnp.float32
+    outs = [jax.ShapeDtypeStruct((SIDE, SIDE, MOST, size, block), bf) for size in (high, low)]
+    outs.append(jax.ShapeDtypeStruct((tiles, 128), jnp.int32))
+    outs += [jax.ShapeDtypeStruct((rows, 1, width), f32)] * 2
+    anywhere = pl.BlockSpec(memory_space=pl.ANY)
+    scalars = pl.BlockSpec(memory_space=pltpu.SMEM)
+    inside = pl.BlockSpec(memory_space=pltpu.VMEM)
     return pl.pallas_call(
         pack_kernel,
         name="pack",
         out_shape=outs,
-        in_specs=[pl.BlockSpec(memory_space=pltpu.SMEM), pl.BlockSpec(memory_space=pl.ANY)],
-        out_specs=(pl.BlockSpec(memory_space=pl.ANY),) * 2,
+        in_specs=[scalars] * 3 + [anywhere] * 2,
+        out_specs=(anywhere, anywhere, scalars, inside, inside),
         scratch_shapes=[
-            pltpu.VMEM(flipped_spectra.shape, jnp.bfloat16),
-            pltpu.VMEM((max(high, low), block), jnp.bfloat16),
-            pltpu.SemaphoreType.DMA,
+            pltpu.VMEM(flipped_spectra.shape, bf),
+            pltpu.VMEM((max(high, low), block), bf),
+            pltpu.VMEM((rows, 8, width), bf),
+            pltpu.VMEM((rows, 8, width), bf),
+            pltpu.SMEM((slots,), jnp.int32),
+            pltpu.SMEM((tiles,), jnp.int32),
+            pltpu.SemaphoreType.DMA((3,)),
             pltpu.SemaphoreType.DMA((slots, 2)),
         ],
         compiler_params=pltpu.CompilerParams(vmem_limit_bytes=VMEM_LIMIT),
-    )(source_block, flipped_spectra)
+    )(target, patch, kernel, flipped_spectra, cotangent)
 
 
 def position():
@@ -490,8 +537,7 @@
 PIECES = 16
 PIECE_ROWS = 112
 FLOWS = 6
-STEP_AT = (0, 0, 8, 0, 2, 3, 4)
-EARLY_PIECES, LATE_PIECES = 12, 5
+HALVED = 12
 
 
 def pairing(place, parity):
@@ -503,7 +549,7 @@
 def sum_kernel(
     parts, normed, first, last, weight,
     conv_out, summed,
-    own, other, total, early_out, early_in, late_out, late_in, result,
+    own, other, total, outgoing, incoming, quarter_out, quarter_in, shared, result,
     tile, wide, held_weight, made, above, below, lefts, rights,
     halo_send, halo_recv, sends, recvs, local,
 ):
@@ -521,7 +567,7 @@
     barrier = pltpu.get_barrier_semaphore()
     peers = [twin]
     for axis, place in enumerate((x, y, z)):
-        peers += [at_place(axis, (place + 1) % SIDE), at_place(axis, (place + 3) % SIDE)]
+        peers += [at_place(axis, (place + step) % SIDE) for step in range(1, SIDE)]
     peers += [(lat, left), (lat, right)]
     peers += [(a, b) for a in (up, down) for b in (left, lon, right)]
     for peer in peers:
@@ -550,22 +596,17 @@
         begun.append(copy)
         return copy
 
+    places = (x, y, z)
     plans = []
     for f in range(FLOWS):
         turn, parity = f // 2, f % 2
-        places = (x, y, z)
         steps, base = [], 0
-        for k in range(3):
-            axis = (turn + k) % 3
-            for partner, keep in pairing(places[axis], parity):
-                size = PIECES >> (len(steps) + 1)
-                if k < 2:
-                    kept, sent = base + keep * size, base + (1 - keep) * size
-                    base = kept
-                else:
-                    size, kept, sent = 1, base, base
-                steps.append((at_place(axis, partner), size, kept, sent))
-        plans.append(steps)
+        for k, (partner, keep) in enumerate(pairing(places[turn], parity)):
+            size = PIECES >> (k + 1)
+            kept, sent = base + keep * size, base + (1 - keep) * size
+            base = kept
+            steps.append((at_place(turn, partner), size, kept, sent))
+        plans.append((steps, (turn + 1) % 3, (turn + 2) % 3))
 
     crossing = [remote(parts.at[1 - core, f], other.at[f], f, 0, twin) for f in range(FLOWS)]
 
@@ -584,33 +625,15 @@
             value += dot(window.reshape(step_rows * cols, 3 * width), held_weight[a], 1, 0)
         made[chunk * step_rows : (chunk + 1) * step_rows] = value.astype(jnp.bfloat16).reshape(step_rows, cols, width)
 
-    def leaving(k):
-        return early_out if k < 3 else late_out
-
-    def arriving(k):
-        return early_in if k < 3 else late_in
-
-    def send_step(f, k):
-        to, size, _, _ = plans[f][k - 1]
-        at = pl.ds(STEP_AT[k], size)
-        return remote(leaving(k).at[f, at], arriving(k).at[f, at], f, k, to)
-
-    def absorb(f, k):
-        _, size, kept, _ = plans[f][k - 1]
-        _, _, kept_next, sent_next = plans[f][k]
-        half = size // 2
-        incoming, outgoing = arriving(k), leaving(k + 1)
-
-        @pl.loop(0, half)
-        def _(i):
-            total[f, kept_next + i] += incoming[f, STEP_AT[k] + kept_next - kept + i].astype(jnp.float32)
-            value = total[f, sent_next + i] + incoming[f, STEP_AT[k] + sent_next - kept + i].astype(jnp.float32)
-            outgoing[f, STEP_AT[k + 1] + i] = value.astype(outgoing.dtype)
+    def halve(f, k):
+        to, size, _, _ = plans[f][0][k]
+        at = pl.ds((0, PIECES // 2)[k], size)
+        return remote(outgoing.at[f, at], incoming.at[f, at], f, 1 + k, to)
 
     convolve(0)
     flying = []
     for f in range(FLOWS):
-        _, size, kept, sent = plans[f][0]
+        _, size, kept, sent = plans[f][0][0]
         load_own[f].wait()
         crossing[f].wait_recv()
 
@@ -618,28 +641,51 @@
         def _(i):
             total[f, kept + i] = own[f, kept + i].astype(jnp.float32) + other[f, kept + i].astype(jnp.float32)
             value = own[f, sent + i].astype(jnp.float32) + other[f, sent + i].astype(jnp.float32)
-            early_out[f, i] = value.astype(jnp.bfloat16)
-
-        flying.append(send_step(f, 1))
-    for k in range(1, 4):
-        for chunk in ((), (1, 2, 3), (4,), (5,))[k]:
-            convolve(chunk)
-        if k == 3:
-            save[0].start()
-        for f in range(FLOWS):
-            flying[f].wait_recv()
-            absorb(f, k)
-            flying[f] = send_step(f, k + 1)
+            outgoing[f, i] = value.astype(jnp.bfloat16)
+
+        flying.append(halve(f, 0))
+    for chunk in (1, 2, 3):
+        convolve(chunk)
     for f in range(FLOWS):
+        _, _, kept, _ = plans[f][0][0]
+        _, size, keep_next, send_next = plans[f][0][1]
         flying[f].wait_recv()
-        late_out[f, STEP_AT[5]] = total[f, plans[f][3][2]] + late_in[f, STEP_AT[4]]
-        flying[f] = send_step(f, 5)
+
+        @pl.loop(0, size)
+        def _(i):
+            total[f, keep_next + i] += incoming[f, keep_next - kept + i].astype(jnp.float32)
+            value = total[f, send_next + i] + incoming[f, send_next - kept + i].astype(jnp.float32)
+            outgoing[f, PIECES // 2 + i] = value.astype(jnp.bfloat16)
+
+        flying[f] = halve(f, 1)
+    convolve(4)
     for f in range(FLOWS):
+        steps, axis, _ = plans[f]
+        base = steps[1][2]
         flying[f].wait_recv()
-        late_out[f, STEP_AT[6]] = late_out[f, STEP_AT[5]] + late_in[f, STEP_AT[5]]
-        flying[f] = send_step(f, 6)
-
-    n = 7
+        flying[f] = []
+        for step in range(1, SIDE):
+            place = (places[axis] + step) % SIDE
+            value = total[f, base + place] + incoming[f, PIECES // 2 + place].astype(jnp.float32)
+            quarter_out[f, step - 1] = value.astype(jnp.bfloat16)
+            flying[f].append(
+                remote(quarter_out.at[f, step - 1], quarter_in.at[f, step - 1], f, 2 + step, at_place(axis, place))
+            )
+    convolve(5)
+    save[0].start()
+    for f in range(FLOWS):
+        steps, axis, other_axis = plans[f]
+        here, there = places[axis], places[other_axis]
+        value = total[f, steps[1][2] + here] + incoming[f, PIECES // 2 + here].astype(jnp.float32)
+        for step in range(1, SIDE):
+            flying[f][step - 1].wait_recv()
+            value += quarter_in[f, step - 1].astype(jnp.float32)
+        shared[f, there] = value.astype(jnp.bfloat16)
+        flying[f] = [
+            remote(shared.at[f, there], shared.at[f, there], f, 5 + step, at_place(other_axis, (there + step) % SIDE))
+            for step in range(1, SIDE)
+        ]
+
     passed = []
 
     def pass_on(f, start, size, n):
@@ -647,23 +693,33 @@
         passed.append(remote(at, at, f, n, twin))
 
     for f in range(FLOWS):
-        flying[f].wait_recv()
-        value = late_out[f, STEP_AT[6]] + late_in[f, STEP_AT[6]]
-        base = plans[f][3][2]
-        result[core, f, base] = value.astype(jnp.bfloat16)
-        at = result.at[core, f, pl.ds(base, 1)]
-        flying[f] = remote(at, at, f, n, plans[f][3][0])
-        pass_on(f, base, 1, n + 1)
-    for k in range(4, 0, -1):
-        n += 2
+        steps, axis, _ = plans[f]
+        mine = steps[1][2] + places[axis]
+        for copy in flying[f]:
+            copy.wait_recv()
+        value = shared[f, 0].astype(jnp.float32)
+        for place in range(1, SIDE):
+            value += shared[f, place].astype(jnp.float32)
+        result[core, f, mine] = value.astype(jnp.bfloat16)
+        at = result.at[core, f, mine]
+        flying[f] = [
+            remote(at, at, f, 8 + step, at_place(axis, (places[axis] + step) % SIDE)) for step in range(1, SIDE)
+        ]
+    for k in (1, 0):
         for f in range(FLOWS):
-            _, size, kept, sent = plans[f][k - 1]
-            flying[f].wait_recv()
-            if k > 1:
-                to, size_up, kept_up, _ = plans[f][k - 2]
-                at = result.at[core, f, pl.ds(kept_up, size_up)]
-                flying[f] = remote(at, at, f, n, to)
-            pass_on(f, sent, size, n + 1)
+            to, size, kept, _ = plans[f][0][k]
+            for copy in flying[f]:
+                copy.wait_recv()
+            at = result.at[core, f, pl.ds(kept, size)]
+            flying[f] = [remote(at, at, f, 13 - k, to)]
+            if k == 1:
+                pass_on(f, kept, size, 14)
+            else:
+                pass_on(f, plans[f][0][1][3], plans[f][0][1][1], 15)
+    for f in range(FLOWS):
+        _, size, _, sent = plans[f][0][0]
+        flying[f][0].wait_recv()
+        pass_on(f, sent, size, 16)
     for copy in passed:
         copy.wait_recv()
     stored = pltpu.make_async_copy(result, summed, local.at[FLOWS + 3])
@@ -691,10 +747,11 @@
             pltpu.VMEM((FLOWS, PIECES) + piece, bf),
             pltpu.VMEM((FLOWS, PIECES) + piece, bf),
             pltpu.VMEM((FLOWS, PIECES) + piece, f32),
-            pltpu.VMEM((FLOWS, EARLY_PIECES) + piece, bf),
-            pltpu.VMEM((FLOWS, EARLY_PIECES) + piece, bf),
-            pltpu.VMEM((FLOWS, LATE_PIECES) + piece, f32),
-            pltpu.VMEM((FLOWS, LATE_PIECES) + piece, f32),
+            pltpu.VMEM((FLOWS, HALVED) + piece, bf),
+            pltpu.VMEM((FLOWS, HALVED) + piece, bf),
+            pltpu.VMEM((FLOWS, SIDE - 1) + piece, bf),
+            pltpu.VMEM((FLOWS, SIDE - 1) + piece, bf),
+            pltpu.VMEM((FLOWS, SIDE) + piece, bf),
             pltpu.VMEM((2, FLOWS, PIECES) + piece, bf),
             pltpu.VMEM((rows, cols, width), bf),
             pltpu.VMEM((rows + 2, cols, 3 * width), bf),
@@ -716,62 +773,72 @@
     )(parts, normed, first, last, weight)
 
 
-def finish_kernel(scale, some, everything, conv_grad, encoder_grad, gain_grad, rest, sem):
-    width = conv_grad.shape[2]
+def finish_kernel(scale, summed, conv_grad, encoder_grad, gain_grad, held, taps, encoder, sems):
+    count, width = taps.shape[0], taps.shape[2]
     lanes = width // 128
-    channels = encoder_grad.shape[0]
+    channels = encoder.shape[0]
+    size = lanes * width
+    base = count * size
+    rest = channels * lanes + 8 * lanes
+
+    def load(tap):
+        at = pl.ds(pl.multiple_of(tap * size, size), size)
+        return pltpu.make_async_copy(summed.at[at], held.at[at], sems.at[0, tap])
+
+    def save(tap):
+        return pltpu.make_async_copy(taps.at[tap], conv_grad.at[tap], sems.at[1, tap])
+
+    last = pl.ds(base, rest)
+    load_rest = pltpu.make_async_copy(summed.at[last], held.at[last], sems.at[0, count])
+    for tap in range(count):
+        load(tap).start()
+    load_rest.start()
+
+    @pl.loop(0, count)
+    def _(tap):
+        load(tap).wait()
+        for n in range(lanes):
+            at = pl.ds(pl.multiple_of(tap * size + n * width, width), width)
+            taps[tap, :, n * 128 : (n + 1) * 128] = held[at].astype(jnp.float32) * scale
+        save(tap).start()
+
+    load_rest.wait()
     for n in range(lanes):
-        conv_grad[0, :, n * 128 : (n + 1) * 128] = some[n * width : (n + 1) * width].astype(jnp.float32) * scale
-
-    @pl.when(pl.program_id(0) == 0)
-    def _():
-        copy = pltpu.make_async_copy(everything.at[pl.ds(9 * lanes * width, rest.shape[0])], rest, sem)
-        copy.start()
-        copy.wait()
-        base = channels * lanes
-        for n in range(lanes):
-            at = slice(n * 128, (n + 1) * 128)
-            encoder_grad[:, at] = rest[n * channels : (n + 1) * channels].astype(jnp.float32) * scale
-            eight = rest[base + n * 8 : base + (n + 1) * 8].astype(jnp.float32)
-            gain_grad[:, at] = jnp.sum(eight, axis=0, keepdims=True) * scale
+        at = slice(n * 128, (n + 1) * 128)
+        encoder[:, at] = held[base + n * channels : base + (n + 1) * channels].astype(jnp.float32) * scale
+        start = base + channels * lanes + n * 8
+        gain_grad[:, at] = jnp.sum(held[start : start + 8].astype(jnp.float32), axis=0, keepdims=True) * scale
+    save_encoder = pltpu.make_async_copy(encoder, encoder_grad, sems.at[1, count])
+    save_encoder.start()
+
+    @pl.loop(0, count)
+    def _(tap):
+        save(tap).wait()
+
+    save_encoder.wait()
 
 
 def finish(summed, scale, channels, width):
     f32 = jnp.float32
-    lanes = width // 128
+    anywhere = pl.BlockSpec(memory_space=pl.ANY)
     return pl.pallas_call(
         lambda *refs: finish_kernel(scale, *refs),
         name="finish",
-        grid=(9,),
         out_shape=(
             jax.ShapeDtypeStruct((9, width, width), f32),
             jax.ShapeDtypeStruct((channels, width), f32),
             jax.ShapeDtypeStruct((1, width), f32),
         ),
-        in_specs=[pl.BlockSpec((lanes * width, 128), lambda t: (t, 0)), pl.BlockSpec(memory_space=pl.ANY)],
-        out_specs=(
-            pl.BlockSpec((1, width, width), lambda t: (t, 0, 0)),
-            pl.BlockSpec((channels, width), lambda t: (0, 0)),
-            pl.BlockSpec((1, width), lambda t: (0, 0)),
-        ),
-        scratch_shapes=[pltpu.VMEM((channels * lanes + 8 * lanes, 128), jnp.bfloat16), pltpu.SemaphoreType.DMA],
+        in_specs=[anywhere],
+        out_specs=(anywhere, anywhere, pl.BlockSpec(memory_space=pltpu.VMEM)),
+        scratch_shapes=[
+            pltpu.VMEM(summed.shape, jnp.bfloat16),
+            pltpu.VMEM((9, width, width), f32),
+            pltpu.VMEM((channels, width), f32),
+            pltpu.SemaphoreType.DMA((2, 10)),
+        ],
         compiler_params=pltpu.CompilerParams(vmem_limit_bytes=VMEM_LIMIT),
-    )(summed, summed)
-
-
-def slot_tables(target, patch, kernel, tiles):
-    blocks = target.shape[0]
-    index = jnp.arange(blocks, dtype=jnp.int32)
-    same = (target[:, None] == target[None, :]) & (index[None, :] < index[:, None])
-    slot = target * MOST + jnp.sum(same, axis=1, dtype=jnp.int32)
-    chosen = slot[None, :] == jnp.arange(tiles * MOST, dtype=jnp.int32)[:, None]
-
-    def pick(values):
-        return jnp.sum(jnp.where(chosen, values[None, :] + 1, 0), axis=1, dtype=jnp.int32) - 1
-
-    source, kernels, patches = pick(index), pick(kernel), jnp.maximum(pick(patch), 0)
-    meta = jnp.concatenate([kernels.reshape(tiles, MOST), patches.reshape(tiles, MOST)], axis=1)
-    return source, jnp.pad(meta, ((0, 0), (0, 128 - 2 * MOST))).reshape(tiles, 1, 128)
+    )(summed)
 
 
 def shards(spectra, target, patch, kernel, encoder_weight, kernels, gain, conv_weight, cotangent):
@@ -779,10 +846,8 @@
     rows, cols, width = cotangent.shape
     channels = spectra.shape[1]
     loss_scale = 1.0 / math.sqrt(rows * bands * cols * tiles)
-    source, meta = slot_tables(target, patch, kernel, tiles)
-    send_a, send_b = pack(source, spectra.T, kernels.shape[1])
-    first = cotangent[:, :1].astype(jnp.float32)
-    last = cotangent[:, -1:].astype(jnp.float32)
+    send_a, send_b, meta, first, last = pack(target, patch, kernel, spectra.T, cotangent, kernels.shape[1], tiles)
+    meta = meta.reshape(tiles, 1, 128)
     weight = conv_weight.reshape(9, width, width)
     got_a, got_b, got_meta, wide, back = exchange(send_a, send_b, meta, cotangent, first, last, weight)
     part_rows = 192 * 112

time: 239 us -> 223 us (0.933)
  Pallas kernels: 228 us -> 218 us
  other arithmetic: 5.31 us -> 0 us
    pallas_call x1, Pallas kernels: 69.7 us -> 63 us  [sum_all(): pl.pallas_call(sum_kernel, name='sum_all', out_shape=(jax.ShapeDtypeStruc...]
    pallas_call x1, Pallas kernels: 10.4 us -> 6.33 us  [finish(): pl.pallas_call(lambda *refs: finish_kernel(scale, *refs), name='finish',...]
where the time goes in v4:
time: 223 us; the launch traced here: 222 us
  Pallas kernels  218 us (98%)
  local copies, waits for them, and re-layouts  3.23 us (1%)
    pallas_call x1, Pallas kernels, exchange(): pl.pallas_call(exchange_kernel, name='exchange', out_shape=(*whole, jax.S...  92.6 us
    pallas_call x1, Pallas kernels, sum_all(): pl.pallas_call(sum_kernel, name='sum_all', out_shape=(jax.ShapeDtypeStruc...  63 us
    pallas_call x1, Pallas kernels, middle(): pl.pallas_call(middle_kernel, name='middle', out_shape=(jax.ShapeDtypeStr...  49.1 us
    pallas_call x1, Pallas kernels, pack(): pl.pallas_call(pack_kernel, name='pack', out_shape=outs, in_specs=[scalar...  7.39 us
    pallas_call x1, Pallas kernels, finish(): pl.pallas_call(lambda *refs: finish_kernel(scale, *refs), name='finish',...  6.33 us

profile of v4, /device:TPU:1, one launch (start us, length us, event | category | flops | bytes accessed | tf_op | source)
XLA Modules:
  0.0 222.3 jit_solution(1025669454695043952)
XLA Ops:
  0.6 7.4 %pack.1 = (bf16[4,4,3,304,128]{4,3,2,1,0:T(8,128)(2,1)}, bf16[4,4,3,312,128]{4,3,2,1,0:T(8,128)(2,1)}, s32[16,128]{1,0:T(8,128)}, f32[24,1,512]{2,1,0:T(1,128)}, f32[24,1,512]{2,1,0:T(1,128)}) custom-call(s32[24]{0:T(128)} %target.1, s32[24]{0:T(128)} %patch.1, s32[24]{0:T(128)} %kernel.1, bf16[616,3072]{1,0:T(8,128)(2,1)} %bitcast.16, bf16[24,64,512]{2,1,0:T(8,128)(2,1)} %cot.3), custom_call_target="tpu_custom_call" | custom-call | tf_op jit(solution)/shard_map/pack/pallas_call | solution.py:110
  8.0 0.0 copy-start.2
  8.0 0.0 copy-start
  8.1 92.6 %exchange.1 = (bf16[4,4,3,304,128]{4,3,2,1,0:T(8,128)(2,1)}, bf16[4,4,3,312,128]{4,3,2,1,0:T(8,128)(2,1)}, s32[16,1,128]{2,1,0:T(1,128)}, bf16[26,64,1536]{2,1,0...) custom-call(bf16[4,4,3,304,128]{4,3,2,1,0:T(8,128)(2,1)} %get-tuple-, ...), custom_call_target="tpu_custom_call" | custom-call | tf_op jit(solution)/shard_map/exchange/pallas_call | solution.py:353
  100.6 0.0 copy-done.2
  100.6 1.1 copy.13
  101.7 0.0 copy-done
  101.7 1.0 copy.14
  102.7 49.1 %middle.1 = (bf16[24,64,512]{2,1,0:T(8,128)(2,1)}, f32[24,1,512]{2,1,0:T(1,128)}, f32[24,1,512]{2,1,0:T(1,128)}, bf16[21504,128]{1,0:T(8,128)(2,1)}) custom-call(s32[16,128]{1,0:T(8,128)} %bitcast.19, bf16[4,4,3,304,128]{4,3,2,1,0:T(8,128)(2,1)} %get-tuple-element.23.send_a.own_a, bf16[4,4,3,312,128]{4,3,2,1,0:T(8,128)(2,1)} %get-tuple-element.24.send_b.own_b, ...), custom_call_target="tpu_custom_call" | custom-call | tf_op jit(solution)/shard_map/middle/pallas_call | solution.py:510
  151.8 63.0 %sum_all.1 = (bf16[24,64,512]{2,1,0:T(8,128)(2,1)}, bf16[2,6,16,112,128]{4,3,2,1,0:T(8,128)(2,1)}) custom-call(bf16[2,6,16,112,128]{4,3,2,1,0:T(8,128)(2,1)} %bitcast.14, bf16[24,64,512]{2,1,0:T(8,128)(2,1)} %get-tuple-element.34.normed, f32[24,1,512]{2,1,0:T(1,128)} %get-tuple-element.35.first, f32[24,1,512]{2,1,0:T(1,128)} %get-tuple-element.36.last, ...), custom_call_target="tpu_custom_call" | custom-call | tf_op jit(solution)/shard_map/sum_all/pallas_call | solution.py:740
  214.8 0.0 copy-start.1
  214.9 6.3 %finish.1 = (f32[9,512,512]{2,1,0:T(8,128)}, f32[616,512]{1,0:T(8,128)}, f32[1,512]{1,0:T(1,128)}) custom-call(bf16[21504,128]{1,0:T(8,128)(2,1)} %bitcast.15), custom_call_target="tpu_custom_call" | custom-call | tf_op jit(solution)/shard_map/finish/pallas_call | solution.py:824
  221.2 0.0 copy-done.1
  221.2 1.1 copy.16
Async XLA Ops:
  8.0 92.6 %copy-start.2 = (bf16[616,512]{1,0:T(8,128)(2,1)S(1)}, bf16[616,512]{1,0:T(8,128)(2,1)}, u32[]{:S(2)}) copy-start(bf16[616,512]{1,0:T(8,128)(2,1)} %param.13) | copy-start | bytes 1892356
  8.0 93.7 %copy-start = (bf16[16,128,128]{2,1,0:T(8,128)(2,1)S(1)}, bf16[16,128,128]{2,1,0:T(8,128)(2,1)}, u32[]{:S(2)}) copy-start(bf16[16,128,128]{2,1,0:T(8,128)(2,1)} %kernels.1) | copy-start | bytes 1572868
  214.8 6.3 %copy-start.1 = (bf16[24,64,512]{2,1,0:T(8,128)(2,1)S(1)}, bf16[24,64,512]{2,1,0:T(8,128)(2,1)}, u32[]{:S(2)}) copy-start(bf16[24,64,512]{2,1,0:T(8,128)(2,1)} %get-tuple-element.46) | copy-start | bytes 4718596

commit v5 on v4

--- a/solution.py
+++ b/solution.py
@@ -13,6 +13,8 @@
 SIDE = 4
 MESH = pl.DeviceIdType.MESH
 VMEM_LIMIT = 60 * 1024 * 1024
+SOURCES = sorted(((dy, dz) for dy in range(SIDE) for dz in range(SIDE)), key=lambda o: (o.count(2), o))
+GROUPS = (0, 9, 15, 16)
 
 
 def dot(a, b, ca, cb):
@@ -186,16 +188,18 @@
 
 
 def exchange_kernel(
-    send_a, send_b, meta, cot, first, last, weight,
-    got_a, got_b, got_meta, wide_out, back_out, mid_a, mid_b, relay_a, relay_b,
-    tile, wide, held_weight, back, above, below, lefts, rights,
-    halo_send, halo_recv, meta_send, meta_recv, sends, recvs, local,
+    send_a, send_b, meta, cot, first, last, weight, encoder_in, kernels_in,
+    got_a, got_b, got_meta, wide_out, back_out, encoded_out, slope_out, turned_out, mid_a, mid_b, relay_a, relay_b,
+    tile, wide, held_weight, back, above, below, lefts, rights, encoder, flat, table, turned, x, encoded, slope,
+    halo_send, halo_recv, meta_send, meta_recv, sends, recvs, local, x_sems, out_sems,
 ):
     lat, lon, y, z = position()
     lats = lax.axis_size("lat")
     count = lax.axis_size("lon")
     _, _, up, down, left, right = halo_peers()
     rows, cols, width = tile.shape
+    high, block = send_a.shape[3:]
+    channels = x.shape[1]
 
     barrier = pltpu.get_barrier_semaphore()
     for step in range(1, SIDE * SIDE):
@@ -210,6 +214,24 @@
     load_weight.start()
     own_meta = pltpu.make_async_copy(meta.at[lon], got_meta.at[0], local.at[2])
     own_meta.start()
+    load_encoder = pltpu.make_async_copy(encoder_in, flat, local.at[5])
+    load_kernels = pltpu.make_async_copy(kernels_in, table, local.at[6])
+    load_encoder.start()
+    load_kernels.start()
+
+    def fetch(at, rank, from_a, from_b):
+        lanes = pl.ds(rank * block, block)
+        return (
+            pltpu.make_async_copy(from_a.at[rank], x.at[at, pl.ds(0, high), lanes], x_sems.at[at, rank, 0]),
+            pltpu.make_async_copy(from_b.at[rank], x.at[at, pl.ds(high, channels - high), lanes], x_sems.at[at, rank, 1]),
+        )
+
+    def bring(at, from_a, from_b):
+        for rank in range(MOST):
+            for copy in fetch(at, rank, from_a, from_b):
+                copy.start()
+
+    bring(0, send_a.at[z, y], send_b.at[y, z])
     pl.semaphore_wait(barrier, SIDE * SIDE - 1 + 6)
 
     halo = halo_copies(
@@ -221,7 +243,7 @@
     for dy in range(SIDE):
         for dz in range(SIDE):
             if dy or dz:
-                n = dy * SIDE + dz
+                n = SOURCES.index((dy, dz))
                 to = (y + dy) % SIDE * SIDE + (z + dz) % SIDE
                 notes.append(
                     pltpu.make_async_remote_copy(
@@ -306,12 +328,52 @@
 
     save_back = pltpu.make_async_copy(back, back_out, local.at[4])
     save_back.start()
+    load_encoder.wait()
+    encoder[...] = flat[...].T
+    load_kernels.wait()
+    for n in range(table.shape[0]):
+        turned[n] = table[n].T
+    save_turned = pltpu.make_async_copy(turned, turned_out, local.at[7])
+    save_turned.start()
+
+    def landed(f, stage, e):
+        if stage == 0:
+            return f[{1: ("d1", 0, 0), 3: ("d1", 1, 0), 2: ("r1", 0, 0)}[e]]
+        if stage == 2:
+            return f[{0: ("r2", 0, 0), 1: ("r2", 0, 1), 3: ("r2", 1, 0), 2: ("r2", 1, 1)}[e]]
+        return f["d2", stage // 2, e]
+
+    def save(at):
+        return (
+            pltpu.make_async_copy(encoded.at[at], encoded_out.at[at], out_sems.at[at, 0]),
+            pltpu.make_async_copy(slope.at[at], slope_out.at[at], out_sems.at[at, 1]),
+        )
+
+    def encode(group):
+        for at in range(GROUPS[group], GROUPS[group + 1]):
+            dy, dz = SOURCES[at]
+            if at:
+                landed(flows[0], dy, dz).wait_recv()
+                landed(flows[1], dz, dy).wait_recv()
+                bring(at, got_a.at[dy, dz], got_b.at[dz, dy])
+
+        @pl.loop(GROUPS[group], GROUPS[group + 1])
+        def _(at):
+            for rank in range(MOST):
+                for copy in fetch(at, rank, got_a.at[0, 0], got_b.at[0, 0]):
+                    copy.wait()
+            pre = dot(encoder[...], x[at], 1, 0)
+            logistic = 0.5 * jnp.tanh(0.5 * pre) + 0.5
+            encoded[at] = (pre * logistic).astype(jnp.bfloat16)
+            slope[at] = logistic * (1.0 + pre * (1.0 - logistic))
+            for copy in save(at):
+                copy.start()
 
     for d, j in ((0, 1), (1, 0), (0, 0), (1, 1)):
         arrived(("q1", d, j))
         start(("r1", d, j))
     start(("q2", 0, 0), ("d2", 0, 0), ("d2", 1, 0))
-    for g in (2, 1, 3, 0):
+    for g in (2, 1, 3):
         arrived(("d1", 0, g), ("d1", 1, g))
         if g == 2:
             start(("q2", 0, 1), ("q2", 1, 0))
@@ -327,12 +389,11 @@
     arrived(("q2", 0, 1), ("q2", 1, 0))
     start(("r2", 0, 1), ("r2", 1, 0))
     start(("d2", 0, 2), ("d2", 1, 2))
+    encode(0)
     arrived(("q2", 1, 1))
     start(("r2", 1, 1))
-    arrived(("r1", 0, 0))
-    for d in range(2):
-        arrived(*(("d2", d, e) for e in range(SIDE)))
-        arrived(("r2", d, 0), ("r2", d, 1))
+    encode(1)
+    encode(2)
     for f in flows:
         for copy in f["made"]:
             copy.wait_send()
@@ -341,11 +402,19 @@
     own_meta.wait()
     save_wide.wait()
     save_back.wait()
-
-
-def exchange(send_a, send_b, meta, cotangent, first, last, weight):
+    save_turned.wait()
+
+    @pl.loop(0, len(SOURCES))
+    def _(at):
+        for copy in save(at):
+            copy.wait()
+
+
+def exchange(send_a, send_b, meta, cotangent, first, last, weight, encoder, kernels):
     rows, cols, width = cotangent.shape
     lon = SIDE * SIDE
+    channels = encoder.shape[0]
+    observed = MOST * send_a.shape[4]
     bf, f32 = jnp.bfloat16, jnp.float32
     anywhere = pl.BlockSpec(memory_space=pl.ANY)
     whole = [jax.ShapeDtypeStruct(a.shape, bf) for a in (send_a, send_b)]
@@ -356,10 +425,12 @@
         out_shape=(
             *whole, jax.ShapeDtypeStruct(meta.shape, meta.dtype),
             jax.ShapeDtypeStruct((rows + 2, cols, 3 * width), bf), jax.ShapeDtypeStruct((rows, cols, width), f32),
+            jax.ShapeDtypeStruct((lon, width, observed), bf), jax.ShapeDtypeStruct((lon, width, observed), f32),
+            jax.ShapeDtypeStruct(kernels.shape, bf),
             *whole, *relay,
         ),
-        in_specs=[anywhere] * 7,
-        out_specs=(anywhere,) * 9,
+        in_specs=[anywhere] * 9,
+        out_specs=(anywhere,) * 12,
         scratch_shapes=[
             pltpu.VMEM((rows, cols, width), bf),
             pltpu.VMEM((rows + 2, cols, 3 * width), bf),
@@ -369,33 +440,41 @@
             pltpu.VMEM((cols, width), bf),
             pltpu.VMEM((rows + 2, 1, width), f32),
             pltpu.VMEM((rows + 2, 1, width), f32),
+            pltpu.VMEM((width, channels), bf),
+            pltpu.VMEM((channels, width), bf),
+            pltpu.VMEM(kernels.shape, bf),
+            pltpu.VMEM(kernels.shape, bf),
+            pltpu.VMEM((lon, channels, observed), bf),
+            pltpu.VMEM((lon, width, observed), bf),
+            pltpu.VMEM((lon, width, observed), f32),
             pltpu.SemaphoreType.DMA((8,)),
             pltpu.SemaphoreType.DMA((8,)),
             pltpu.SemaphoreType.DMA((lon,)),
             pltpu.SemaphoreType.DMA((lon,)),
             pltpu.SemaphoreType.DMA((2, 32)),
             pltpu.SemaphoreType.DMA((2, 32)),
-            pltpu.SemaphoreType.DMA((5,)),
+            pltpu.SemaphoreType.DMA((8,)),
+            pltpu.SemaphoreType.DMA((lon, MOST, 2)),
+            pltpu.SemaphoreType.DMA((lon, 2)),
         ],
         compiler_params=pltpu.CompilerParams(
             collective_id=0, has_side_effects=True, vmem_limit_bytes=VMEM_LIMIT
         ),
-    )(send_a, send_b, meta, cotangent, first, last, weight)
-    return out[:5]
+    )(send_a, send_b, meta, cotangent, first, last, weight, encoder, kernels)
+    return out[:8]
 
 
 def middle_kernel(
-    meta, own_a, own_b, got_a, got_b, encoder, kernels, turned, gain, wide_in, back_in,
+    meta, own_a, own_b, got_a, got_b, turned, gain, wide_in, back_in, encoded_in, slope_in,
     normed, first, last, parts,
     x, slope, encoded, spread, d_spread, wide, back, flipped, d_rows, encoder_sum, gain_sum,
-    x_sems, local,
+    x_sems, pair_sems, local,
 ):
     lat, lon, y, z = position()
     rows, cols, width = normed.shape
-    channels = encoder.shape[1]
-    high = own_a.shape[3]
+    channels = x.shape[1]
+    high, block = own_a.shape[3:]
     sources = SIDE * SIDE
-    block = kernels.shape[1]
 
     def fetch(n, rank, from_a, from_b):
         lanes = pl.ds(rank * block, block)
@@ -404,34 +483,36 @@
             pltpu.make_async_copy(from_b.at[rank], x.at[n, pl.ds(high, channels - high), lanes], x_sems.at[n, rank, 1]),
         )
 
+    def load_encoded(n):
+        return pltpu.make_async_copy(encoded_in.at[n], encoded.at[n], pair_sems.at[n, 0])
+
+    def load_slope(n):
+        return pltpu.make_async_copy(slope_in.at[n], slope.at[n], pair_sems.at[n, 1])
+
+    load_back = pltpu.make_async_copy(back_in, back, local.at[0])
+    load_wide = pltpu.make_async_copy(wide_in, wide, local.at[1])
     for n in range(sources):
-        dy, dz = n // SIDE, n % SIDE
+        load_encoded(n).start()
+    load_back.start()
+    load_wide.start()
+    for n, (dy, dz) in enumerate(SOURCES):
         from_a = own_a.at[z, y] if n == 0 else got_a.at[dy, dz]
         from_b = own_b.at[y, z] if n == 0 else got_b.at[dz, dy]
         for rank in range(MOST):
             for copy in fetch(n, rank, from_a, from_b):
                 copy.start()
-    load_back = pltpu.make_async_copy(back_in, back, local.at[0])
-    load_wide = pltpu.make_async_copy(wide_in, wide, local.at[1])
-    load_back.start()
-    load_wide.start()
+        load_slope(n).start()
     spread[...] = jnp.zeros_like(spread)
 
     @pl.loop(0, sources)
     def _(n):
-        for rank in range(MOST):
-            for copy in fetch(n, rank, got_a.at[0, 0], got_b.at[0, 0]):
-                copy.wait()
-        pre = dot(encoder[...], x[n], 1, 0)
-        logistic = 0.5 * jnp.tanh(0.5 * pre) + 0.5
-        encoded[...] = (pre * logistic).astype(jnp.bfloat16)
-        slope[n] = logistic * (1.0 + pre * (1.0 - logistic))
+        load_encoded(n).wait()
         for rank in range(MOST):
             which, patch = meta[n, rank], meta[n, MOST + rank]
 
             @pl.when(which >= 0)
             def _():
-                spread[patch] += dot(turned[which], encoded[:, rank * block : (rank + 1) * block], 1, 1)
+                spread[patch] += dot(turned[which], encoded[n, :, rank * block : (rank + 1) * block], 1, 1)
 
     load_back.wait()
     gain_sum[...] = jnp.zeros_like(gain_sum)
@@ -480,6 +561,10 @@
     @pl.loop(0, sources)
     def _(n):
         for rank in range(MOST):
+            for copy in fetch(n, rank, got_a.at[0, 0], got_b.at[0, 0]):
+                copy.wait()
+        load_slope(n).wait()
+        for rank in range(MOST):
             which, patch = jnp.maximum(meta[n, rank], 0), meta[n, MOST + rank]
             lanes = slice(rank * block, (rank + 1) * block)
             here = dot(d_spread[patch], turned[which], 1, 0).astype(jnp.bfloat16).astype(jnp.float32)
@@ -497,10 +582,9 @@
     parts[base:] = jnp.zeros((parts.shape[0] - base, 128), jnp.bfloat16)
 
 
-def middle(meta, own_a, own_b, got_a, got_b, encoder, kernels, gain, wide, back, part_rows):
+def middle(meta, own_a, own_b, got_a, got_b, turned, gain, wide, back, encoded, slope, channels, part_rows):
     rows, cols, width = back.shape
-    channels = encoder.shape[0]
-    block, cells = kernels.shape[1:]
+    cells, block = turned.shape[1:]
     patches = rows * cols // cells
     sources = SIDE * SIDE
     bf, f32 = jnp.bfloat16, jnp.float32
@@ -513,12 +597,12 @@
         out_shape=(
             jax.ShapeDtypeStruct((rows, cols, width), bf), column, column, jax.ShapeDtypeStruct((part_rows, 128), bf)
         ),
-        in_specs=[pl.BlockSpec(memory_space=pltpu.SMEM)] + [anywhere] * 4 + [local] * 4 + [anywhere] * 2,
+        in_specs=[pl.BlockSpec(memory_space=pltpu.SMEM)] + [anywhere] * 4 + [local] * 2 + [anywhere] * 4,
         out_specs=(local,) * 4,
         scratch_shapes=[
             pltpu.VMEM((sources, channels, MOST * block), bf),
             pltpu.VMEM((sources, width, MOST * block), f32),
-            pltpu.VMEM((width, MOST * block), bf),
+            pltpu.VMEM((sources, width, MOST * block), bf),
             pltpu.VMEM((patches, cells, width), f32),
             pltpu.VMEM((patches, width, cells), bf),
             pltpu.VMEM(wide.shape, bf),
@@ -528,10 +612,11 @@
             pltpu.VMEM((channels, width), f32),
             pltpu.VMEM((8, width), f32),
             pltpu.SemaphoreType.DMA((sources, MOST, 2)),
+            pltpu.SemaphoreType.DMA((sources, 2)),
             pltpu.SemaphoreType.DMA((2,)),
         ],
         compiler_params=pltpu.CompilerParams(vmem_limit_bytes=VMEM_LIMIT),
-    )(meta, own_a, own_b, got_a, got_b, encoder.T, kernels, kernels.swapaxes(1, 2), gain, wide, back)
+    )(meta, own_a, own_b, got_a, got_b, turned, gain, wide, back, encoded, slope)
 
 
 PIECES = 16
@@ -849,11 +934,13 @@
     send_a, send_b, meta, first, last = pack(target, patch, kernel, spectra.T, cotangent, kernels.shape[1], tiles)
     meta = meta.reshape(tiles, 1, 128)
     weight = conv_weight.reshape(9, width, width)
-    got_a, got_b, got_meta, wide, back = exchange(send_a, send_b, meta, cotangent, first, last, weight)
+    got_a, got_b, got_meta, wide, back, encoded, slope, turned = exchange(
+        send_a, send_b, meta, cotangent, first, last, weight, encoder_weight, kernels
+    )
     part_rows = 192 * 112
     normed, first, last, parts = middle(
-        got_meta.reshape(tiles, 128), send_a, send_b, got_a, got_b, encoder_weight, kernels,
-        gain.reshape(1, width), wide, back, part_rows,
+        got_meta.reshape(tiles, 128), send_a, send_b, got_a, got_b, turned, gain.reshape(1, width), wide, back,
+        encoded, slope, channels, part_rows,
     )
     conv_out, summed = sum_all(parts, normed, first, last, conv_weight.reshape(3, 3 * width, width))
     conv_grad, encoder_grad, gain_grad = finish(summed.reshape(part_rows, 128), loss_scale, channels, width)

time: 223 us -> 218 us (0.978)
    pallas_call x1, Pallas kernels: 92.6 us -> 101 us  [exchange(): pl.pallas_call(exchange_kernel, name='exchange', out_shape=(*whole, jax.S...]
    pallas_call x1, Pallas kernels: 49.1 us -> 41.6 us  [middle(): pl.pallas_call(middle_kernel, name='middle', out_shape=(jax.ShapeDtypeStr...]
    pallas_call x1, Pallas kernels: 63 us -> 59.3 us  [sum_all(): pl.pallas_call(sum_kernel, name='sum_all', out_shape=(jax.ShapeDtypeStruc...]
where the time goes in v5:
time: 218 us
  Pallas kernels  216 us (99%)
    pallas_call x1, Pallas kernels, exchange(): pl.pallas_call(exchange_kernel, name='exchange', out_shape=(*whole, jax.S...  101 us
    pallas_call x1, Pallas kernels, sum_all(): pl.pallas_call(sum_kernel, name='sum_all', out_shape=(jax.ShapeDtypeStruc...  59.3 us
    pallas_call x1, Pallas kernels, middle(): pl.pallas_call(middle_kernel, name='middle', out_shape=(jax.ShapeDtypeStr...  41.6 us
    pallas_call x1, Pallas kernels, pack(): pl.pallas_call(pack_kernel, name='pack', out_shape=outs, in_specs=[scalar...  7.41 us
    pallas_call x1, Pallas kernels, finish(): pl.pallas_call(lambda *refs: finish_kernel(scale, *refs), name='finish',...  6.33 us

profile of v5, /device:TPU:1, one launch (start us, length us, event | category | flops | bytes accessed | tf_op | source)
XLA Modules:
  0.0 217.7 jit_solution(1923982291514519115)
XLA Ops:
  0.6 7.4 %pack.1 = (bf16[4,4,3,304,128]{4,3,2,1,0:T(8,128)(2,1)}, bf16[4,4,3,312,128]{4,3,2,1,0:T(8,128)(2,1)}, s32[16,128]{1,0:T(8,128)}, f32[24,1,512]{2,1,0:T(1,128)}, f32[24,1,512]{2,1,0:T(1,128)}) custom-call(s32[24]{0:T(128)} %target.1, s32[24]{0:T(128)} %patch.1, s32[24]{0:T(128)} %kernel.1, bf16[616,3072]{1,0:T(8,128)(2,1)} %bitcast.14, bf16[24,64,512]{2,1,0:T(8,128)(2,1)} %cot.3), custom_call_target="tpu_custom_call" | custom-call | tf_op jit(solution)/shard_map/pack/pallas_call | solution.py:112
  8.0 101.2 %exchange.1 = (bf16[4,4,3,304,128]{4,3,2,1,0:T(8,128)(2,1)}, bf16[4,4,3,312,128]{4,3,2,1,0:T(8,128)(2,1)}, s32[16,1,128]{2,1,0:T(1,128)}, bf16[26,64,1536]{2,1,0...) custom-call(bf16[4,4,3,304,128]{4,3,2,1,0:T(8,128)(2,1)} %get-tuple-, ...), custom_call_target="tpu_custom_call" | custom-call | tf_op jit(solution)/shard_map/exchange/pallas_call | solution.py:422
  109.3 41.6 %middle.1 = (bf16[24,64,512]{2,1,0:T(8,128)(2,1)}, f32[24,1,512]{2,1,0:T(1,128)}, f32[24,1,512]{2,1,0:T(1,128)}, bf16[21504,128]{1,0:T(8,128)(2,1)}) custom-call(s32[16,128]{1,0:T(8,128)} %bitcast.15, bf16[4,4,3,304,128]{4,3,2,1,0:T(8,128)(2,1)} %get-tuple-element.26.send_a.own_a, bf16[4,4,3,312,128]{4,3,2,1,0:T(8,128)(2,1)} %get-tuple-element.27.send_b.own_b, ...), custom_call_target="tpu_custom_call" | custom-call | tf_op jit(solution)/shard_map/middle/pallas_call | solution.py:594
  150.9 59.3 %sum_all.1 = (bf16[24,64,512]{2,1,0:T(8,128)(2,1)}, bf16[2,6,16,112,128]{4,3,2,1,0:T(8,128)(2,1)}) custom-call(bf16[2,6,16,112,128]{4,3,2,1,0:T(8,128)(2,1)} %bitcast.12, bf16[24,64,512]{2,1,0:T(8,128)(2,1)} %get-tuple-element.40.normed, f32[24,1,512]{2,1,0:T(1,128)} %get-tuple-element.41.first, f32[24,1,512]{2,1,0:T(1,128)} %get-tuple-element.42.last, ...), custom_call_target="tpu_custom_call" | custom-call | tf_op jit(solution)/shard_map/sum_all/pallas_call | solution.py:825
  210.2 0.0 copy-start
  210.3 6.3 %finish.1 = (f32[9,512,512]{2,1,0:T(8,128)}, f32[616,512]{1,0:T(8,128)}, f32[1,512]{1,0:T(1,128)}) custom-call(bf16[21504,128]{1,0:T(8,128)(2,1)} %bitcast.13), custom_call_target="tpu_custom_call" | custom-call | tf_op jit(solution)/shard_map/finish/pallas_call | solution.py:909
  216.6 0.0 copy-done
  216.6 1.1 copy.14
Async XLA Ops:
  210.2 6.3 %copy-start = (bf16[24,64,512]{2,1,0:T(8,128)(2,1)S(1)}, bf16[24,64,512]{2,1,0:T(8,128)(2,1)}, u32[]{:S(2)}) copy-start(bf16[24,64,512]{2,1,0:T(8,128)(2,1)} %get-tuple-element.52) | copy-start | bytes 4718596

commit v6 on v5

--- a/solution.py
+++ b/solution.py
@@ -13,8 +13,8 @@
 SIDE = 4
 MESH = pl.DeviceIdType.MESH
 VMEM_LIMIT = 60 * 1024 * 1024
-SOURCES = sorted(((dy, dz) for dy in range(SIDE) for dz in range(SIDE)), key=lambda o: (o.count(2), o))
-GROUPS = (0, 9, 15, 16)
+SOURCES = sorted(((dy, dz) for dy in range(SIDE) for dz in range(SIDE)), key=lambda o: (o.count(2), sum(o) if 2 in o else 0, o))
+GROUPS = (0, 9, 11, 13, 15, 16)
 
 
 def dot(a, b, ca, cb):
@@ -389,11 +389,10 @@
     arrived(("q2", 0, 1), ("q2", 1, 0))
     start(("r2", 0, 1), ("r2", 1, 0))
     start(("d2", 0, 2), ("d2", 1, 2))
-    encode(0)
     arrived(("q2", 1, 1))
     start(("r2", 1, 1))
-    encode(1)
-    encode(2)
+    for group in range(len(GROUPS) - 1):
+        encode(group)
     for f in flows:
         for copy in f["made"]:
             copy.wait_send()

time: 218 us -> 219 us (level)
  no operation moved by 1% of the time
where the time goes in v6:
time: 219 us; the launch traced here: 218 us
  Pallas kernels  216 us (99%)
    pallas_call x1, Pallas kernels, exchange(): pl.pallas_call(exchange_kernel, name='exchange', out_shape=(*whole, jax.S...  102 us
    pallas_call x1, Pallas kernels, sum_all(): pl.pallas_call(sum_kernel, name='sum_all', out_shape=(jax.ShapeDtypeStruc...  58.9 us
    pallas_call x1, Pallas kernels, middle(): pl.pallas_call(middle_kernel, name='middle', out_shape=(jax.ShapeDtypeStr...  41.6 us
    pallas_call x1, Pallas kernels, pack(): pl.pallas_call(pack_kernel, name='pack', out_shape=outs, in_specs=[scalar...  7.41 us
    pallas_call x1, Pallas kernels, finish(): pl.pallas_call(lambda *refs: finish_kernel(scale, *refs), name='finish',...  6.33 us

profile of v6, /device:TPU:1, one launch (start us, length us, event | category | flops | bytes accessed | tf_op | source)
XLA Modules:
  0.0 218.2 jit_solution(15229790542084784829)
XLA Ops:
  0.6 7.4 %pack.1 = (bf16[4,4,3,304,128]{4,3,2,1,0:T(8,128)(2,1)}, bf16[4,4,3,312,128]{4,3,2,1,0:T(8,128)(2,1)}, s32[16,128]{1,0:T(8,128)}, f32[24,1,512]{2,1,0:T(1,128)}, f32[24,1,512]{2,1,0:T(1,128)}) custom-call(s32[24]{0:T(128)} %target.1, s32[24]{0:T(128)} %patch.1, s32[24]{0:T(128)} %kernel.1, bf16[616,3072]{1,0:T(8,128)(2,1)} %bitcast.14, bf16[24,64,512]{2,1,0:T(8,128)(2,1)} %cot.3), custom_call_target="tpu_custom_call" | custom-call | tf_op jit(solution)/shard_map/pack/pallas_call | solution.py:112
  8.0 102.1 %exchange.1 = (bf16[4,4,3,304,128]{4,3,2,1,0:T(8,128)(2,1)}, bf16[4,4,3,312,128]{4,3,2,1,0:T(8,128)(2,1)}, s32[16,1,128]{2,1,0:T(1,128)}, bf16[26,64,1536]{2,1,0...) custom-call(bf16[4,4,3,304,128]{4,3,2,1,0:T(8,128)(2,1)} %get-tuple-, ...), custom_call_target="tpu_custom_call" | custom-call | tf_op jit(solution)/shard_map/exchange/pallas_call | solution.py:421
  110.1 41.6 %middle.1 = (bf16[24,64,512]{2,1,0:T(8,128)(2,1)}, f32[24,1,512]{2,1,0:T(1,128)}, f32[24,1,512]{2,1,0:T(1,128)}, bf16[21504,128]{1,0:T(8,128)(2,1)}) custom-call(s32[16,128]{1,0:T(8,128)} %bitcast.15, bf16[4,4,3,304,128]{4,3,2,1,0:T(8,128)(2,1)} %get-tuple-element.26.send_a.own_a, bf16[4,4,3,312,128]{4,3,2,1,0:T(8,128)(2,1)} %get-tuple-element.27.send_b.own_b, ...), custom_call_target="tpu_custom_call" | custom-call | tf_op jit(solution)/shard_map/middle/pallas_call | solution.py:593
  151.7 58.9 %sum_all.1 = (bf16[24,64,512]{2,1,0:T(8,128)(2,1)}, bf16[2,6,16,112,128]{4,3,2,1,0:T(8,128)(2,1)}) custom-call(bf16[2,6,16,112,128]{4,3,2,1,0:T(8,128)(2,1)} %bitcast.12, bf16[24,64,512]{2,1,0:T(8,128)(2,1)} %get-tuple-element.40.normed, f32[24,1,512]{2,1,0:T(1,128)} %get-tuple-element.41.first, f32[24,1,512]{2,1,0:T(1,128)} %get-tuple-element.42.last, ...), custom_call_target="tpu_custom_call" | custom-call | tf_op jit(solution)/shard_map/sum_all/pallas_call | solution.py:824
  210.7 0.0 copy-start
  210.7 6.3 %finish.1 = (f32[9,512,512]{2,1,0:T(8,128)}, f32[616,512]{1,0:T(8,128)}, f32[1,512]{1,0:T(1,128)}) custom-call(bf16[21504,128]{1,0:T(8,128)(2,1)} %bitcast.13), custom_call_target="tpu_custom_call" | custom-call | tf_op jit(solution)/shard_map/finish/pallas_call | solution.py:908
  217.0 0.0 copy-done
  217.0 1.1 copy.14
Async XLA Ops:
  210.7 6.3 %copy-start = (bf16[24,64,512]{2,1,0:T(8,128)(2,1)S(1)}, bf16[24,64,512]{2,1,0:T(8,128)(2,1)}, u32[]{:S(2)}) copy-start(bf16[24,64,512]{2,1,0:T(8,128)(2,1)} %get-tuple-element.52) | copy-start | bytes 4718596

commit v7 on v6

--- a/solution.py
+++ b/solution.py
@@ -464,29 +464,17 @@
 
 
 def middle_kernel(
-    meta, own_a, own_b, got_a, got_b, turned, gain, wide_in, back_in, encoded_in, slope_in,
-    normed, first, last, parts,
-    x, slope, encoded, spread, d_spread, wide, back, flipped, d_rows, encoder_sum, gain_sum,
-    x_sems, pair_sems, local,
+    channels, meta, turned, gain, wide_in, back_in, encoded_in,
+    normed, first, last, d_spread, parts,
+    encoded, spread, wide, back, flipped, gain_sum,
+    pair_sems, local,
 ):
-    lat, lon, y, z = position()
     rows, cols, width = normed.shape
-    channels = x.shape[1]
-    high, block = own_a.shape[3:]
     sources = SIDE * SIDE
-
-    def fetch(n, rank, from_a, from_b):
-        lanes = pl.ds(rank * block, block)
-        return (
-            pltpu.make_async_copy(from_a.at[rank], x.at[n, pl.ds(0, high), lanes], x_sems.at[n, rank, 0]),
-            pltpu.make_async_copy(from_b.at[rank], x.at[n, pl.ds(high, channels - high), lanes], x_sems.at[n, rank, 1]),
-        )
+    block = turned.shape[2]
 
     def load_encoded(n):
-        return pltpu.make_async_copy(encoded_in.at[n], encoded.at[n], pair_sems.at[n, 0])
-
-    def load_slope(n):
-        return pltpu.make_async_copy(slope_in.at[n], slope.at[n], pair_sems.at[n, 1])
+        return pltpu.make_async_copy(encoded_in.at[n], encoded.at[n], pair_sems.at[n])
 
     load_back = pltpu.make_async_copy(back_in, back, local.at[0])
     load_wide = pltpu.make_async_copy(wide_in, wide, local.at[1])
@@ -494,13 +482,6 @@
         load_encoded(n).start()
     load_back.start()
     load_wide.start()
-    for n, (dy, dz) in enumerate(SOURCES):
-        from_a = own_a.at[z, y] if n == 0 else got_a.at[dy, dz]
-        from_b = own_b.at[y, z] if n == 0 else got_b.at[dz, dy]
-        for rank in range(MOST):
-            for copy in fetch(n, rank, from_a, from_b):
-                copy.start()
-        load_slope(n).start()
     spread[...] = jnp.zeros_like(spread)
 
     @pl.loop(0, sources)
@@ -555,33 +536,14 @@
             parts[pl.ds(base, width)] = got[:, :128]
             parts[pl.ds(pl.multiple_of(base + width, width), width)] = got[:, 128:]
 
-    encoder_sum[...] = jnp.zeros_like(encoder_sum)
-
-    @pl.loop(0, sources)
-    def _(n):
-        for rank in range(MOST):
-            for copy in fetch(n, rank, got_a.at[0, 0], got_b.at[0, 0]):
-                copy.wait()
-        load_slope(n).wait()
-        for rank in range(MOST):
-            which, patch = jnp.maximum(meta[n, rank], 0), meta[n, MOST + rank]
-            lanes = slice(rank * block, (rank + 1) * block)
-            here = dot(d_spread[patch], turned[which], 1, 0).astype(jnp.bfloat16).astype(jnp.float32)
-            d_rows[:, lanes] = (here * slope[n, :, lanes]).astype(jnp.bfloat16)
-        encoder_sum[...] += dot(x[n], d_rows[...], 1, 1)
-
-    base = 9 * width * width // 128
-    for n in range(width // 128):
-        lanes = slice(n * 128, (n + 1) * 128)
-        parts[base + n * channels : base + (n + 1) * channels] = encoder_sum[:, lanes].astype(jnp.bfloat16)
-    base += channels * width // 128
+    base = 9 * width * width // 128 + channels * width // 128
     for n in range(width // 128):
         parts[base + n * 8 : base + (n + 1) * 8] = gain_sum[:, n * 128 : (n + 1) * 128].astype(jnp.bfloat16)
     base += 8 * width // 128
     parts[base:] = jnp.zeros((parts.shape[0] - base, 128), jnp.bfloat16)
 
 
-def middle(meta, own_a, own_b, got_a, got_b, turned, gain, wide, back, encoded, slope, channels, part_rows):
+def middle(meta, turned, gain, wide, back, encoded, channels, part_rows):
     rows, cols, width = back.shape
     cells, block = turned.shape[1:]
     patches = rows * cols // cells
@@ -591,36 +553,32 @@
     local = pl.BlockSpec(memory_space=pltpu.VMEM)
     column = jax.ShapeDtypeStruct((rows, 1, width), f32)
     return pl.pallas_call(
-        middle_kernel,
+        lambda *refs: middle_kernel(channels, *refs),
         name="middle",
         out_shape=(
-            jax.ShapeDtypeStruct((rows, cols, width), bf), column, column, jax.ShapeDtypeStruct((part_rows, 128), bf)
+            jax.ShapeDtypeStruct((rows, cols, width), bf), column, column,
+            jax.ShapeDtypeStruct((patches, width, cells), bf), jax.ShapeDtypeStruct((part_rows, 128), bf),
         ),
-        in_specs=[pl.BlockSpec(memory_space=pltpu.SMEM)] + [anywhere] * 4 + [local] * 2 + [anywhere] * 4,
-        out_specs=(local,) * 4,
+        in_specs=[pl.BlockSpec(memory_space=pltpu.SMEM)] + [local] * 2 + [anywhere] * 3,
+        out_specs=(local,) * 5,
         scratch_shapes=[
-            pltpu.VMEM((sources, channels, MOST * block), bf),
-            pltpu.VMEM((sources, width, MOST * block), f32),
             pltpu.VMEM((sources, width, MOST * block), bf),
             pltpu.VMEM((patches, cells, width), f32),
-            pltpu.VMEM((patches, width, cells), bf),
             pltpu.VMEM(wide.shape, bf),
             pltpu.VMEM(back.shape, f32),
             pltpu.VMEM((width, rows * cols), bf),
-            pltpu.VMEM((width, MOST * block), bf),
-            pltpu.VMEM((channels, width), f32),
             pltpu.VMEM((8, width), f32),
-            pltpu.SemaphoreType.DMA((sources, MOST, 2)),
-            pltpu.SemaphoreType.DMA((sources, 2)),
+            pltpu.SemaphoreType.DMA((sources,)),
             pltpu.SemaphoreType.DMA((2,)),
         ],
         compiler_params=pltpu.CompilerParams(vmem_limit_bytes=VMEM_LIMIT),
-    )(meta, own_a, own_b, got_a, got_b, turned, gain, wide, back, encoded, slope)
+    )(meta, turned, gain, wide, back, encoded)
 
 
 PIECES = 16
 PIECE_ROWS = 112
 FLOWS = 6
+EARLY, LATE = (0, 1, 2, 3), (4, 5)
 HALVED = 12
 
 
@@ -631,11 +589,11 @@
 
 
 def sum_kernel(
-    parts, normed, first, last, weight,
+    meta, parts, normed, first, last, weight, own_a, own_b, got_a, got_b, slope_in, turned_in, d_spread_in,
     conv_out, summed,
-    own, other, total, outgoing, incoming, quarter_out, quarter_in, shared, result,
-    tile, wide, held_weight, made, above, below, lefts, rights,
-    halo_send, halo_recv, sends, recvs, local,
+    own, late, other, total, outgoing, incoming, quarter_out, quarter_in, shared, result,
+    tile, wide, held_weight, made, above, below, lefts, rights, observed, slope, turned, d_spread, d_rows, encoder_sum,
+    halo_send, halo_recv, sends, recvs, local, x_sems, slope_sems,
 ):
     lat, lon, y, z = position()
     x, core = lat // 2, lat % 2
@@ -656,10 +614,37 @@
     peers += [(a, b) for a in (up, down) for b in (left, lon, right)]
     for peer in peers:
         pl.semaphore_signal(barrier, inc=1, device_id=peer, device_id_type=MESH)
-    load_own = [pltpu.make_async_copy(parts.at[core, f], own.at[f], local.at[f]) for f in range(FLOWS)]
+    load_own = [pltpu.make_async_copy(parts.at[core, f], own.at[f], local.at[f]) for f in EARLY]
+    load_late = [
+        pltpu.make_async_copy(parts.at[:, f], late.at[:, f - LATE[0]], local.at[f]) for f in LATE
+    ]
+    load_turned = pltpu.make_async_copy(turned_in, turned, local.at[FLOWS + 4])
+    load_spread = pltpu.make_async_copy(d_spread_in, d_spread, local.at[FLOWS + 5])
+    channels, high, block = observed.shape[1], own_a.shape[3], own_a.shape[4]
+
+    def fetch(n, rank, from_a, from_b):
+        lanes = pl.ds(rank * block, block)
+        return (
+            pltpu.make_async_copy(from_a.at[rank], observed.at[n, pl.ds(0, high), lanes], x_sems.at[n, rank, 0]),
+            pltpu.make_async_copy(
+                from_b.at[rank], observed.at[n, pl.ds(high, channels - high), lanes], x_sems.at[n, rank, 1]
+            ),
+        )
+
+    def load_slope(n):
+        return pltpu.make_async_copy(slope_in.at[n], slope.at[n], slope_sems.at[n])
     load_tile = pltpu.make_async_copy(normed, tile, local.at[FLOWS])
     load_weight = pltpu.make_async_copy(weight, held_weight, local.at[FLOWS + 1])
-    for copy in (load_tile, *load_own, load_weight):
+    for copy in (load_turned, load_spread, *load_own):
+        copy.start()
+    for n, (dy, dz) in enumerate(SOURCES):
+        from_a = own_a.at[z, y] if n == 0 else got_a.at[dy, dz]
+        from_b = own_b.at[y, z] if n == 0 else got_b.at[dz, dy]
+        for rank in range(MOST):
+            for copy in fetch(n, rank, from_a, from_b):
+                copy.start()
+        load_slope(n).start()
+    for copy in (*load_late, load_tile, load_weight):
         copy.start()
     pl.semaphore_wait(barrier, len(peers))
 
@@ -692,13 +677,38 @@
             steps.append((at_place(turn, partner), size, kept, sent))
         plans.append((steps, (turn + 1) % 3, (turn + 2) % 3))
 
-    crossing = [remote(parts.at[1 - core, f], other.at[f], f, 0, twin) for f in range(FLOWS)]
-
-    load_tile.wait()
-    for copy in halo:
-        copy.wait()
-    lay_windows(tile, above, below, lefts, rights, wide, False)
-    load_weight.wait()
+    crossing = {f: remote(parts.at[1 - core, f], other.at[f], f, 0, twin) for f in EARLY}
+    encoder_sum[...] = jnp.zeros_like(encoder_sum)
+    load_turned.wait()
+    load_spread.wait()
+
+    def backward(low, high_end):
+        @pl.loop(low, high_end)
+        def _(n):
+            for rank in range(MOST):
+                for copy in fetch(n, rank, got_a.at[0, 0], got_b.at[0, 0]):
+                    copy.wait()
+            load_slope(n).wait()
+            for rank in range(MOST):
+                which, patch = jnp.maximum(meta[n, rank], 0), meta[n, MOST + rank]
+                lanes = slice(rank * block, (rank + 1) * block)
+                here = dot(d_spread[patch], turned[which], 1, 0).astype(jnp.bfloat16).astype(jnp.float32)
+                d_rows[:, lanes] = (here * slope[n, :, lanes]).astype(jnp.bfloat16)
+            encoder_sum[...] += dot(observed[n], d_rows[...], 1, 1)
+
+    def place_encoder():
+        flow_rows = PIECES * PIECE_ROWS
+        begin = 9 * width * width // 128 - (FLOWS + LATE[0]) * flow_rows
+        for n in range(width // 128):
+            done = 0
+            while done < channels:
+                at = begin + n * channels + done
+                flow, piece, row = at // flow_rows, at % flow_rows // PIECE_ROWS, at % PIECE_ROWS
+                size = min(PIECE_ROWS - row, channels - done)
+                some = encoder_sum[done : done + size, n * 128 : (n + 1) * 128]
+                late[1, flow, piece, row : row + size] = some.astype(jnp.bfloat16)
+                done += size
+
     step_rows = 4
     save = [pltpu.make_async_copy(made, conv_out, local.at[FLOWS + 2])]
 
@@ -714,23 +724,30 @@
         at = pl.ds((0, PIECES // 2)[k], size)
         return remote(outgoing.at[f, at], incoming.at[f, at], f, 1 + k, to)
 
-    convolve(0)
-    flying = []
-    for f in range(FLOWS):
+    flying, passed = {}, []
+
+    def pass_on(f, start, size, n):
+        at = result.at[core, f, pl.ds(start, size)]
+        passed.append(remote(at, at, f, n, twin))
+
+    def half(f):
         _, size, kept, sent = plans[f][0][0]
-        load_own[f].wait()
         crossing[f].wait_recv()
+        if f in EARLY:
+            load_own[f].wait()
+
+        def mine(i):
+            return (own[f, i] if f in EARLY else late[core, f - LATE[0], i]).astype(jnp.float32)
 
         @pl.loop(0, size)
         def _(i):
-            total[f, kept + i] = own[f, kept + i].astype(jnp.float32) + other[f, kept + i].astype(jnp.float32)
-            value = own[f, sent + i].astype(jnp.float32) + other[f, sent + i].astype(jnp.float32)
+            total[f, kept + i] = mine(kept + i) + other[f, kept + i].astype(jnp.float32)
+            value = mine(sent + i) + other[f, sent + i].astype(jnp.float32)
             outgoing[f, i] = value.astype(jnp.bfloat16)
 
-        flying.append(halve(f, 0))
-    for chunk in (1, 2, 3):
-        convolve(chunk)
-    for f in range(FLOWS):
+        flying[f] = halve(f, 0)
+
+    def quarter(f):
         _, _, kept, _ = plans[f][0][0]
         _, size, keep_next, send_next = plans[f][0][1]
         flying[f].wait_recv()
@@ -742,8 +759,8 @@
             outgoing[f, PIECES // 2 + i] = value.astype(jnp.bfloat16)
 
         flying[f] = halve(f, 1)
-    convolve(4)
-    for f in range(FLOWS):
+
+    def second(f):
         steps, axis, _ = plans[f]
         base = steps[1][2]
         flying[f].wait_recv()
@@ -755,9 +772,8 @@
             flying[f].append(
                 remote(quarter_out.at[f, step - 1], quarter_in.at[f, step - 1], f, 2 + step, at_place(axis, place))
             )
-    convolve(5)
-    save[0].start()
-    for f in range(FLOWS):
+
+    def third(f):
         steps, axis, other_axis = plans[f]
         here, there = places[axis], places[other_axis]
         value = total[f, steps[1][2] + here] + incoming[f, PIECES // 2 + here].astype(jnp.float32)
@@ -770,13 +786,7 @@
             for step in range(1, SIDE)
         ]
 
-    passed = []
-
-    def pass_on(f, start, size, n):
-        at = result.at[core, f, pl.ds(start, size)]
-        passed.append(remote(at, at, f, n, twin))
-
-    for f in range(FLOWS):
+    def settle(f):
         steps, axis, _ = plans[f]
         mine = steps[1][2] + places[axis]
         for copy in flying[f]:
@@ -789,21 +799,63 @@
         flying[f] = [
             remote(at, at, f, 8 + step, at_place(axis, (places[axis] + step) % SIDE)) for step in range(1, SIDE)
         ]
-    for k in (1, 0):
-        for f in range(FLOWS):
-            to, size, kept, _ = plans[f][0][k]
-            for copy in flying[f]:
-                copy.wait_recv()
-            at = result.at[core, f, pl.ds(kept, size)]
-            flying[f] = [remote(at, at, f, 13 - k, to)]
-            if k == 1:
-                pass_on(f, kept, size, 14)
-            else:
-                pass_on(f, plans[f][0][1][3], plans[f][0][1][1], 15)
-    for f in range(FLOWS):
+
+    def spread_out(f, k):
+        to, size, kept, _ = plans[f][0][k]
+        for copy in flying[f]:
+            copy.wait_recv()
+        at = result.at[core, f, pl.ds(kept, size)]
+        flying[f] = [remote(at, at, f, 13 - k, to)]
+        if k == 1:
+            pass_on(f, kept, size, 14)
+        else:
+            pass_on(f, plans[f][0][1][3], plans[f][0][1][1], 15)
+
+    def close(f):
         _, size, _, sent = plans[f][0][0]
         flying[f][0].wait_recv()
         pass_on(f, sent, size, 16)
+
+    def each(group, act, *rest):
+        for f in group:
+            act(f, *rest)
+
+    sources = len(SOURCES)
+    backward(0, sources * 3 // 8)
+    each(EARLY, half)
+    backward(sources * 3 // 8, sources)
+    for copy in load_late:
+        copy.wait()
+    place_encoder()
+    for f in LATE:
+        crossing[f] = remote(late.at[1 - core, f - LATE[0]], other.at[f], f, 0, twin)
+    each(EARLY, quarter)
+    load_tile.wait()
+    for copy in halo:
+        copy.wait()
+    lay_windows(tile, above, below, lefts, rights, wide, False)
+    load_weight.wait()
+    each(LATE, half)
+    each(EARLY, second)
+    convolve(0)
+    each(LATE, quarter)
+    convolve(1)
+    each(EARLY, third)
+    convolve(2)
+    each(LATE, second)
+    convolve(3)
+    each(EARLY, settle)
+    each(LATE, third)
+    convolve(4)
+    each(EARLY, spread_out, 1)
+    each(LATE, settle)
+    convolve(5)
+    save[0].start()
+    each(EARLY, spread_out, 0)
+    each(LATE, spread_out, 1)
+    each(LATE, spread_out, 0)
+    each(EARLY, close)
+    each(LATE, close)
     for copy in passed:
         copy.wait_recv()
     stored = pltpu.make_async_copy(result, summed, local.at[FLOWS + 3])
@@ -814,21 +866,23 @@
     stored.wait()
 
 
-def sum_all(parts, normed, first, last, weight):
+def sum_all(meta, parts, normed, first, last, weight, own_a, own_b, got_a, got_b, slope, turned, d_spread, channels):
     rows, cols, width = normed.shape
     bf, f32 = jnp.bfloat16, jnp.float32
     anywhere = pl.BlockSpec(memory_space=pl.ANY)
     inside = pl.BlockSpec(memory_space=pltpu.VMEM)
     piece = (PIECE_ROWS, 128)
     parts = parts.reshape((2, FLOWS, PIECES) + piece)
+    sources = len(SOURCES)
     return pl.pallas_call(
         sum_kernel,
         name="sum_all",
         out_shape=(jax.ShapeDtypeStruct(normed.shape, bf), jax.ShapeDtypeStruct(parts.shape, bf)),
-        in_specs=[anywhere, anywhere, inside, inside, anywhere],
+        in_specs=[pl.BlockSpec(memory_space=pltpu.SMEM), anywhere, anywhere, inside, inside] + [anywhere] * 8,
         out_specs=(anywhere, anywhere),
         scratch_shapes=[
-            pltpu.VMEM((FLOWS, PIECES) + piece, bf),
+            pltpu.VMEM((len(EARLY), PIECES) + piece, bf),
+            pltpu.VMEM((2, len(LATE), PIECES) + piece, bf),
             pltpu.VMEM((FLOWS, PIECES) + piece, bf),
             pltpu.VMEM((FLOWS, PIECES) + piece, f32),
             pltpu.VMEM((FLOWS, HALVED) + piece, bf),
@@ -845,16 +899,24 @@
             pltpu.VMEM((cols, width), bf),
             pltpu.VMEM((rows + 2, 1, width), f32),
             pltpu.VMEM((rows + 2, 1, width), f32),
+            pltpu.VMEM((sources, channels, slope.shape[2]), bf),
+            pltpu.VMEM(slope.shape, f32),
+            pltpu.VMEM(turned.shape, bf),
+            pltpu.VMEM(d_spread.shape, bf),
+            pltpu.VMEM(slope.shape[1:], bf),
+            pltpu.VMEM((channels, width), f32),
             pltpu.SemaphoreType.DMA((8,)),
             pltpu.SemaphoreType.DMA((8,)),
             pltpu.SemaphoreType.DMA((FLOWS, 17)),
             pltpu.SemaphoreType.DMA((FLOWS, 17)),
-            pltpu.SemaphoreType.DMA((FLOWS + 4,)),
+            pltpu.SemaphoreType.DMA((FLOWS + 6,)),
+            pltpu.SemaphoreType.DMA((sources, MOST, 2)),
+            pltpu.SemaphoreType.DMA((sources,)),
         ],
         compiler_params=pltpu.CompilerParams(
             collective_id=1, has_side_effects=True, vmem_limit_bytes=VMEM_LIMIT
         ),
-    )(parts, normed, first, last, weight)
+    )(meta, parts, normed, first, last, weight, own_a, own_b, got_a, got_b, slope, turned, d_spread)
 
 
 def finish_kernel(scale, summed, conv_grad, encoder_grad, gain_grad, held, taps, encoder, sems):
@@ -937,11 +999,14 @@
         send_a, send_b, meta, cotangent, first, last, weight, encoder_weight, kernels
     )
     part_rows = 192 * 112
-    normed, first, last, parts = middle(
-        got_meta.reshape(tiles, 128), send_a, send_b, got_a, got_b, turned, gain.reshape(1, width), wide, back,
-        encoded, slope, channels, part_rows,
+    got_meta = got_meta.reshape(tiles, 128)
+    normed, first, last, d_spread, parts = middle(
+        got_meta, turned, gain.reshape(1, width), wide, back, encoded, channels, part_rows
     )
-    conv_out, summed = sum_all(parts, normed, first, last, conv_weight.reshape(3, 3 * width, width))
+    conv_out, summed = sum_all(
+        got_meta, parts, normed, first, last, conv_weight.reshape(3, 3 * width, width), send_a, send_b, got_a, got_b,
+        slope, turned, d_spread, channels,
+    )
     conv_grad, encoder_grad, gain_grad = finish(summed.reshape(part_rows, 128), loss_scale, channels, width)
     return conv_out, conv_grad.reshape(3, 3, width, width), encoder_grad, gain_grad.reshape(width)
 

time: 219 us -> 217 us (level)
    pallas_call x1, Pallas kernels: 41.6 us -> 25.5 us  [middle(): pl.pallas_call(lambda *refs: middle_kernel(channels, *refs), name='middle...]
    pallas_call x1, Pallas kernels: 58.9 us -> 73.3 us  [sum_all(): pl.pallas_call(sum_kernel, name='sum_all', out_shape=(jax.ShapeDtypeStruc...]
where the time goes in v7:
time: 217 us; the launch traced here: 216 us
  Pallas kernels  215 us (99%)
    pallas_call x1, Pallas kernels, exchange(): pl.pallas_call(exchange_kernel, name='exchange', out_shape=(*whole, jax.S...  102 us
    pallas_call x1, Pallas kernels, sum_all(): pl.pallas_call(sum_kernel, name='sum_all', out_shape=(jax.ShapeDtypeStruc...  73.3 us
    pallas_call x1, Pallas kernels, middle(): pl.pallas_call(lambda *refs: middle_kernel(channels, *refs), name='middle...  25.5 us
    pallas_call x1, Pallas kernels, pack(): pl.pallas_call(pack_kernel, name='pack', out_shape=outs, in_specs=[scalar...  7.41 us
    pallas_call x1, Pallas kernels, finish(): pl.pallas_call(lambda *refs: finish_kernel(scale, *refs), name='finish',...  6.33 us

profile of v7, /device:TPU:1, one launch (start us, length us, event | category | flops | bytes accessed | tf_op | source)
XLA Modules:
  0.0 216.4 jit_solution(3340360875522382516)
XLA Ops:
  0.6 7.4 %pack.1 = (bf16[4,4,3,304,128]{4,3,2,1,0:T(8,128)(2,1)}, bf16[4,4,3,312,128]{4,3,2,1,0:T(8,128)(2,1)}, s32[16,128]{1,0:T(8,128)}, f32[24,1,512]{2,1,0:T(1,128)}, f32[24,1,512]{2,1,0:T(1,128)}) custom-call(s32[24]{0:T(128)} %target.1, s32[24]{0:T(128)} %patch.1, s32[24]{0:T(128)} %kernel.1, bf16[616,3072]{1,0:T(8,128)(2,1)} %bitcast.14, bf16[24,64,512]{2,1,0:T(8,128)(2,1)} %cot.3), custom_call_target="tpu_custom_call" | custom-call | tf_op jit(solution)/shard_map/pack/pallas_call | solution.py:112
  8.0 102.1 %exchange.1 = (bf16[4,4,3,304,128]{4,3,2,1,0:T(8,128)(2,1)}, bf16[4,4,3,312,128]{4,3,2,1,0:T(8,128)(2,1)}, s32[16,1,128]{2,1,0:T(1,128)}, bf16[26,64,1536]{2,1,0...) custom-call(bf16[4,4,3,304,128]{4,3,2,1,0:T(8,128)(2,1)} %get-tuple-, ...), custom_call_target="tpu_custom_call" | custom-call | tf_op jit(solution)/shard_map/exchange/pallas_call | solution.py:421
  110.1 25.5 %middle.1 = (bf16[24,64,512]{2,1,0:T(8,128)(2,1)}, f32[24,1,512]{2,1,0:T(1,128)}, f32[24,1,512]{2,1,0:T(1,128)}, bf16[12,512,128]{2,1,0:T(8,128)(2,1)}, bf16[21504,128]{1,0:T(8,128)(2,1)}) custom-call(s32[16,128]{1,0:T(8,128)} %bitcast.15, bf16[16,128,128]{2,1,0:T(8,128)(2,1)} %get-tuple-element.33.refs_1_.turned_in, f32[1,512]{1,0:T(1,128)} %bitcast.18, ...), custom_call_target="tpu_custom_call" | custom-call | tf_op jit(solution)/shard_map/middle/pallas_call | solution.py:555
  135.6 73.3 %sum_all.1 = (bf16[24,64,512]{2,1,0:T(8,128)(2,1)}, bf16[2,6,16,112,128]{4,3,2,1,0:T(8,128)(2,1)}) custom-call(s32[16,128]{1,0:T(8,128)} %bitcast.16, bf16[2,6,16,112,128]{4,3,2,1,0:T(8,128)(2,1)} %bitcast.12, bf16[24,64,512]{2,1,0:T(8,128)(2,1)} %get-tuple-element.38.normed, f32[24,1,512]{2,1,0:T(1,128)} %get-tuple-element.39.first, ...), custom_call_target="tpu_custom_call" | custom-call | tf_op jit(solution)/shard_map/sum_all/pallas_call | solution.py:877
  208.9 0.0 copy-start
  208.9 6.3 %finish.1 = (f32[9,512,512]{2,1,0:T(8,128)}, f32[616,512]{1,0:T(8,128)}, f32[1,512]{1,0:T(1,128)}) custom-call(bf16[21504,128]{1,0:T(8,128)(2,1)} %bitcast.13), custom_call_target="tpu_custom_call" | custom-call | tf_op jit(solution)/shard_map/finish/pallas_call | solution.py:970
  215.3 0.0 copy-done
  215.3 1.1 copy.14
Async XLA Ops:
  208.9 6.3 %copy-start = (bf16[24,64,512]{2,1,0:T(8,128)(2,1)S(1)}, bf16[24,64,512]{2,1,0:T(8,128)(2,1)}, u32[]{:S(2)}) copy-start(bf16[24,64,512]{2,1,0:T(8,128)(2,1)} %get-tuple-element.54) | copy-start | bytes 4718596
